TPU v7x, 32 devices: a whole 2x2x4 slice. The times are simulated.
32 devices in a mesh: grp: 2 (over x), blk: 8 (over z, y), vec: 2 (over core).
Axes of the slice: x: 2, y: 2, z: 4, core: 2. Of those that a mesh axis runs over, the one named last changes fastest.
Arguments:
- trial: bfloat16 [20480, 32], P(('grp', 'blk', 'vec')), may hold values from -6 to 6
- energy_gap: float32 [20480], P(('grp', 'blk', 'vec')), may hold values from 0.5 to 2.5
- coulomb_factors: bfloat16 [4096, 20480], P('blk'), may hold values from -0.0390625 to 0.0390625
- occ_values: bfloat16 [80, 40, 512], P('blk'), may hold values from -1 to 1
- vir_values: bfloat16 [80, 512, 512], P('blk'), may hold values from -1 to 1
- kernel: float32 [80, 512], P('blk'), may hold values from 0.2 to 2
- live_points: int32 [80], P('blk'), may hold values from 64 to 512
Outputs:
- sigma: bfloat16 [20480, 32], P(('grp', 'blk', 'vec'))
All inputs are finite; a program needn't handle non-finite values.
Results may differ from a plain program's by a relative error of at most 0.0029.
Values may be sent and summed in bfloat16 or wider, within the bound.
No kernel may reach another device: no remote copies, remote signals or barrier semaphores. Data moves between devices by JAX's collectives and lax.ppermute only.
A program may use at most 64 MiB of HBM per device.

v0:
```python
import jax
import jax.numpy as jnp
from jax import lax
from jax.sharding import PartitionSpec as P


def local(trial, energy_gap, coulomb_factors, occ_values, vir_values, kernel, live_points):
    pair_rows = lax.all_to_all(trial, "vec", split_axis=1, concat_axis=0, tiled=True)
    full = lax.all_gather(pair_rows, ("grp", "blk"), axis=0, tiled=True)
    occ_count = occ_values.shape[1]
    batch_size = occ_values.shape[2]
    vir_count = vir_values.shape[2]
    width = full.shape[1]
    batches = occ_values.shape[0]
    rearranged = (
        full.reshape(occ_count, vir_count, width)
        .transpose(1, 0, 2)
        .reshape(vir_count, occ_count * width)
    )
    slots = jnp.arange(batch_size, dtype=jnp.int32)

    def coulomb_term():
        factored = jnp.dot(coulomb_factors, full, preferred_element_type=jnp.float32).astype(
            jnp.bfloat16
        )
        return 2.0 * lax.dot_general(
            coulomb_factors, factored, (((0,), (0,)), ((), ())), preferred_element_type=jnp.float32
        )

    def grid_term(first, last):

        def step(carry, items):
            occ, vir, weight, live = items
            trans = jnp.dot(vir, rearranged, preferred_element_type=jnp.float32).reshape(
                batch_size, occ_count, width
            )
            occ_float = occ.astype(jnp.float32)
            density = jnp.einsum("gik,ig->gk", trans, occ_float)
            mask = (slots < live).astype(jnp.float32)
            weighted = density * (weight * mask)[:, None]
            scaled = (
                (occ_float.T[:, :, None] * weighted[:, None, :])
                .reshape(batch_size, occ_count * width)
                .astype(jnp.bfloat16)
            )
            return (
                carry
                + lax.dot_general(
                    vir, scaled, (((0,), (0,)), ((), ())), preferred_element_type=jnp.float32
                ),
                None,
            )

        start = jnp.zeros((vir_count, occ_count * width), jnp.float32)
        items = (
            occ_values[first:last],
            vir_values[first:last],
            kernel[first:last],
            live_points[first:last],
        )
        total, _ = lax.scan(step, start, items)
        return (
            total.reshape(vir_count, occ_count, width)
            .transpose(1, 0, 2)
            .reshape(occ_count * vir_count, width)
        )

    cut = batches // 2

    def first_group():
        return coulomb_term() + grid_term(0, cut)

    def second_group():
        return grid_term(cut, batches)

    partial_sum = lax.cond(lax.axis_index("grp") == 0, first_group, second_group)
    summed = lax.psum_scatter(partial_sum, ("grp", "blk"), scatter_dimension=0, tiled=True)
    joined = lax.all_to_all(summed, "vec", split_axis=0, concat_axis=1, tiled=True)
    result = energy_gap[:, None] * trial.astype(jnp.float32) + joined
    return result.astype(jnp.bfloat16)


def solution(mesh):
    in_specs = (
        P(("grp", "blk", "vec"), None),
        P(("grp", "blk", "vec")),
        P("blk", None),
        P("blk", None, None),
        P("blk", None, None),
        P("blk", None),
        P("blk"),
    )
    out_specs = P(("grp", "blk", "vec"), None)
    return jax.shard_map(local, mesh=mesh, in_specs=in_specs, out_specs=out_specs, check_vma=False)
```

profile of v0, /device:TPU:0, one launch (start us, length us, event | category | flops | bytes accessed | tf_op | source)
XLA Modules:
  0.0 206.8 jit_solution(335047641834568448)
XLA Ops:
  6.5 3.3 %all-to-all-start = ((bf16[640,2,16]{0,2,1:T(8,128)(2,1)}), bf16[640,2,16]{0,2,1:T(8,128)(2,1)S(1)}, u32[]{:S(2)}, u32[]{:S(2)}) async-start(bf16[640,2,16]{0,2,1:T(8,128)(2,1)} %bitcast.130), calls=%async_computation | async-start | bytes 81920 | tf_op jit(solution)/shard_map/all_to_all | solution.py:8
  9.8 0.0 reduce-scatter.2.cloned.1.call-start
  9.9 1.3 all-to-all-done
  11.2 46.4 %all_gather.3 = bf16[20480,16]{0,1:T(8,128)(2,1)S(1)} all-gather(bf16[1280,16]{0,1:T(8,128)(2,1)S(1)} %bitcast.131), channel_id=1, replica_groups=mesh['grp'=2,'blk'=8,'vec'=2] {'grp','blk'}, dimensions={0}, use_global_device_ids=true | all-gather | bytes 696320 | tf_op jit(solution)/shard_map/all_gather | solution.py:9
  57.6 0.0 copy-start.1
  57.6 0.0 copy-start.3
  57.6 0.0 copy-start.5
  57.6 0.2 copy.65
  57.8 0.2 copy.45
  58.0 0.6 copy-done.1
  58.6 0.0 copy-done.3
  58.6 0.0 copy-done.5
  58.6 60.6 %conditional.1 = (f32[20480,16]{0,1:T(8,128)}) conditional(s32[]{:T(128)} %convert_element_type.41, (bf16[10,40,512]{2,1,0:T(8,128)(2,1)S(1)}, bf16[10,512,512]{2,1,0:T(8,128)(2,1)}, f32[10,512]{1,0:T(8,128)S(1)}, s32[10]{0:T(128)S(1)}, bf16[512,640]{0,1:T(8,128)(2,1)S(1)}, /*index=5*/s32[512]{0:T(512)S(1)}) %tuple.68, (bf16[512,20480]{1,0:T(8,128)(2,1)}, ...), branch_computations={%region_0.3_spmd, %region_3.6_spmd} | conditional | flops 1344848896 | bytes 43934980 | solution.py:76
  58.6 0.0 copy-start
  58.6 3.8 %slice.20 = bf16[5,512,512]{2,1,0:T(8,128)(2,1)} slice(bf16[10,512,512]{2,1,0:T(8,128)(2,1)} %get-tuple-element.127), slice={[0:5], [0:512], [0:512]} | slice | bytes 5242880 | tf_op jit(solution)/shard_map/cond/branch_1_fun/slice | solution.py:57
  62.3 0.0 copy-done
  62.4 28.0 %while.21 = (s32[]{:T(128)}, f32[512,640]{1,0:T(8,128)S(1)}, bf16[5,512,512]{2,1,0:T(8,128)(2,1)}, bf16[5,40,512]{2,1,0:T(8,128)(2,1)S(1)}, bf16[512,640]{0,1:T(...) while((s32[]{:T(128)}, f32[512,640]{1,0:T(8,128)S(1)}, ...), condition=%wide.region_5.5_spmd.clone, body=%wide.region_4.4_spmd.clone.sunk | while | flops 673096704 | bytes 6149255 | solution.py:61
  62.4 2.0 fusion.38
  64.4 0.7 dynamic_slice.72
  65.1 0.7 compare_select_fusion.4
  65.8 0.1 multiply_convert_fusion.4
  65.9 2.1 convolution_add_fusion.4
  68.0 2.0 fusion.38
  70.0 0.7 dynamic_slice.72
  70.7 0.7 compare_select_fusion.4
  71.4 0.1 multiply_convert_fusion.4
  71.5 2.1 convolution_add_fusion.4
  73.6 2.0 fusion.38
  75.6 0.7 dynamic_slice.72
  76.3 0.7 compare_select_fusion.4
  77.0 0.1 multiply_convert_fusion.4
  77.1 2.1 convolution_add_fusion.4
  79.2 2.0 fusion.38
  81.2 0.7 dynamic_slice.72
  81.9 0.7 compare_select_fusion.4
  82.6 0.1 multiply_convert_fusion.4
  82.7 2.1 convolution_add_fusion.4
  84.8 2.0 fusion.38
  86.8 0.7 dynamic_slice.72
  87.5 0.7 compare_select_fusion.4
  88.2 0.1 multiply_convert_fusion.4
  88.3 2.1 convolution_add_fusion.4
  90.4 0.4 copy.42
  90.8 0.1 copy.62
  90.9 28.3 %fusion.17 = f32[20480,16]{0,1:T(8,128)} fusion(f32[20480,16]{0,1:T(8,128)S(1)} %bitcast.118, bf16[512,20480]{1,0:T(8,128)(2,1)} %get-tuple-element.135, bf16[20480,16]{0,1:T(8,128)(2,1)S(1)} %get-tuple-element.126), kind=kOutput, calls=%fused_computation.34 | convolution fusion | flops 671752192 | bytes 24248320 | tf_op jit(solution)/shard_map/cond/branch_1_fun/dot_general | solution.py:26
  119.2 0.0 copy-start.2
  119.2 0.0 copy-start.4
  119.2 0.0 reduce-scatter.2.cloned.1.call-update
  119.2 75.5 %reduce-scatter.2.cloned.1.call-done = f32[1280,16]{0,1:T(8,128)} async-done(((f32[20480,16]{0,1:T(8,128)}), f32[1280,16]{0,1:T(8,128)}) %reduce-scatter.2.cloned.1.call-update) | async-done | bytes 81936 | tf_op jit(solution)/shard_map/reduce_scatter | solution.py:77
  194.7 0.9 copy.71
  195.6 3.8 %all_to_all.38 = f32[2,640,16]{1,2,0:T(8,128)S(1)} all-to-all(f32[2,640,16]{1,2,0:T(8,128)S(1)} %bitcast.126), channel_id=1, replica_groups=mesh['grp'=2,'blk'=8,'vec'=2] {'vec'}, dimensions={0} | all-to-all | bytes 163840 | tf_op jit(solution)/shard_map/all_to_all | solution.py:78
  199.3 0.0 copy-done.2
  199.3 0.0 copy-done.4
  199.3 0.6 fusion.18
  (21 shorter events, 0.2 us)
Async XLA Ops:
  6.5 4.7 %all-to-all-start = ((bf16[640,2,16]{0,2,1:T(8,128)(2,1)}), bf16[640,2,16]{0,2,1:T(8,128)(2,1)S(1)}, u32[]{:S(2)}, u32[]{:S(2)}) async-start(bf16[640,2,16]{0,2,1:T(8,128)(2,1)} %bitcast.130), calls=%async_computation | async-start | bytes 81920 | tf_op jit(solution)/shard_map/all_to_all | solution.py:8
  9.8 184.9 %reduce-scatter.2.cloned.1.call-start = ((), (), s32[]{:S(2)}) async-start(), calls=%async_computation.3 | async-start | bytes 1392640 | tf_op jit(solution)/shard_map/reduce_scatter | solution.py:77
  57.6 1.0 copy-start.1
  57.6 1.0 copy-start.3
  57.6 1.0 copy-start.5
  58.6 3.8 %copy-start = (bf16[512,640]{0,1:T(8,128)(2,1)}, bf16[512,640]{0,1:T(8,128)(2,1)S(1)}, u32[]{:S(2)}) copy-start(bf16[512,640]{0,1:T(8,128)(2,1)S(1)} %get-tuple-element.336) | copy-start | bytes 1966084 | tf_op jit(solution)/shard_map/cond
  119.2 80.1 %copy-start.2 = (bf16[640,32]{0,1:T(8,128)(2,1)S(1)}, bf16[640,32]{0,1:T(8,128)(2,1)}, u32[]{:S(2)}) copy-start(bf16[640,32]{0,1:T(8,128)(2,1)} %param.13) | copy-start | bytes 122884
  119.2 80.1 %copy-start.4 = (f32[640]{0:T(1024)S(1)}, f32[640]{0:T(1024)}, u32[]{:S(2)}) copy-start(f32[640]{0:T(1024)} %param.14) | copy-start | bytes 7684
Sparse Core Ops, SparseCore 0:
  119.3 75.2 reduce-scatter.1
where the time goes:
time: 208 us; the launch traced here: 207 us
  waiting for transfers between devices  76.8 us (37%)
  blocking collectives  50.1 us (24%)
  matrix products  48.4 us (23%)
  between operations  13.4 us (6%)
  local copies, waits for them, and re-layouts  9.57 us (5%)
  other arithmetic  4.78 us (2%)
  starting transfers between devices  3.31 us (2%)
    reduce_scatter x1, waiting for transfers between devices, local(): lax.psum_scatter(partial_sum, ('grp', 'blk'), scatter_dimension=0, tiled=...  75.5 us
    all_gather x1, blocking collectives, local(): full = lax.all_gather(pair_rows, ('grp', 'blk'), axis=0, tiled=True)  46.4 us
    dot_general x1, matrix products, coulomb_term(): lax.dot_general(coulomb_factors, factored, (((0,), (0,)), ((), ())), pref...  28.3 us
    dot_general x5, matrix products, step(): lax.dot_general(vir, scaled, (((0,), (0,)), ((), ())), preferred_element_...  10.3 us
    dot_general x5, matrix products, step(): jnp.dot(vir, rearranged, preferred_element_type=jnp.float32)  9.84 us
  transfers between devices with their start and end apart: 2, of which 2 were waited for; matrix products, arithmetic and copies ran while one was open for 0% of the time, Pallas kernels for 0%

commit v1 on v0

v1 whole, which is shorter than its diff:
```python
import jax
import jax.numpy as jnp
from jax import lax
from jax.experimental import pallas as pl
from jax.experimental.pallas import tpu as pltpu
from jax.sharding import PartitionSpec as P

LANES = 128
NT = (((1,), (1,)), ((), ()))
NN = (((1,), (0,)), ((), ()))


def digits_of(count):
    digits, stride = [], 1
    bits = count.bit_length() - 1
    if bits % 2:
        digits.append((1, 2))
        stride = 2
    while stride < count:
        digits.append((stride, 4))
        stride *= 4
    return digits


def swap(x, axis, count, mask):
    return lax.ppermute(x, axis, [(i, i ^ mask) for i in range(count)])


def first_kernel(half, masks, *refs):
    pieces = refs[: len(masks)]
    occ_ref, vir_hbm, fac_hbm, dens_ref, part_ref, rows, flat, occ32, vir, fac, vsem, fsem = refs[
        len(masks) :
    ]
    me, grp = lax.axis_index("blk"), lax.axis_index("grp")
    batches, points, virs = vir_hbm.shape
    occs = rows.shape[0] // half
    chunks = fac.shape[0]
    wide = fac.shape[2]
    start = pl.multiple_of(grp * (occs * virs), LANES)

    def vir_copy(b):
        return pltpu.make_async_copy(vir_hbm.at[b], vir.at[b], vsem.at[b])

    def fac_copy(c):
        at = pl.multiple_of(start + c * wide, LANES)
        return pltpu.make_async_copy(fac_hbm.at[:, pl.ds(at, wide)], fac.at[c], fsem.at[c])

    for n in range(max(batches, chunks)):
        if n < batches:
            vir_copy(n).start()
        if n < chunks:
            fac_copy(n).start()

    tiles = virs // LANES
    for piece, mask in zip(pieces, masks):
        parts, _, length = piece.shape
        per = length // LANES
        for p in range(parts):
            for j in range(per):
                at = (me ^ mask) * (parts * per) + p * per + j if len(masks) > 1 else p * per + j
                block = piece[p, :, j * LANES : (j + 1) * LANES]
                i, t = at // tiles, at % tiles
                rows[
                    pl.ds(pl.multiple_of(i * half, half), half),
                    pl.ds(pl.multiple_of(t * LANES, LANES), LANES),
                ] = block
                flat[:, pl.ds(pl.multiple_of(at * LANES, LANES), LANES)] = block

    def dens_step(b, _):
        vir_copy(b).wait()
        occ32[...] = occ_ref[b].astype(jnp.float32)
        trans = lax.dot_general(rows[...], vir[b], NT, preferred_element_type=jnp.float32)
        total = jnp.zeros((half, points), jnp.float32)
        for i in range(occs):
            row = occ32[pl.ds(grp * occs + i, 1), :]
            total = total + row * trans[i * half : (i + 1) * half, :]
        dens_ref[b] = total.astype(dens_ref.dtype)
        return 0

    lax.fori_loop(0, batches, dens_step, 0)

    part_ref[...] = jnp.zeros(part_ref.shape, jnp.float32)

    def fac_step(c, _):
        fac_copy(c).wait()
        x = flat[:, pl.ds(pl.multiple_of(c * wide, LANES), wide)]
        part_ref[...] += lax.dot_general(x, fac[c], NT, preferred_element_type=jnp.float32)
        return 0

    lax.fori_loop(0, chunks, fac_step, 0)


def second_kernel(half, blocks, *refs):
    (
        live_ref, dens_a, dens_b, part_a, part_b, occ_ref, weight_ref, vir_hbm, fac_hbm,
    ) = refs[:9]
    outs = refs[9:-9]
    occ32, vir, fac, vsem, fsem, scaled, acc, both, held = refs[-9:]
    me, grp = lax.axis_index("blk"), lax.axis_index("grp")
    batches, points, virs = vir_hbm.shape
    occs = scaled.shape[0] // half
    chunks = fac.shape[0]
    wide = fac.shape[2]
    start = pl.multiple_of(grp * (occs * virs), LANES)

    def vir_copy(b):
        return pltpu.make_async_copy(vir_hbm.at[b], vir.at[b], vsem.at[b])

    def fac_copy(c):
        at = pl.multiple_of(start + c * wide, LANES)
        return pltpu.make_async_copy(fac_hbm.at[:, pl.ds(at, wide)], fac.at[c], fsem.at[c])

    for n in range(max(batches, chunks)):
        if n < batches:
            vir_copy(n).start()
        if n < chunks:
            fac_copy(n).start()

    slots = lax.broadcasted_iota(jnp.int32, (1, points), 1)
    acc[...] = jnp.zeros(acc.shape, jnp.float32)

    def grid_step(b, _):
        vir_copy(b).wait()
        occ32[...] = occ_ref[b].astype(jnp.float32)
        density = dens_a[b].astype(jnp.float32) + dens_b[b].astype(jnp.float32)
        weight = jnp.where(slots < live_ref[b], weight_ref[pl.ds(b, 1), :], 0.0)
        weighted = density * weight
        for i in range(occs):
            row = occ32[pl.ds(grp * occs + i, 1), :]
            scaled[i * half : (i + 1) * half, :] = (row * weighted).astype(jnp.bfloat16)
        acc[...] += lax.dot_general(scaled[...], vir[b], NN, preferred_element_type=jnp.float32)
        return 0

    lax.fori_loop(0, batches, grid_step, 0)

    both[...] = (part_a[...] + part_b[...]).astype(jnp.bfloat16)
    count, parts, length = blocks
    per = length // LANES
    tiles = virs // LANES
    each = wide // LANES

    def fac_step(c, _):
        fac_copy(c).wait()
        coulomb = 2.0 * lax.dot_general(both[...], fac[c], NN, preferred_element_type=jnp.float32)
        for t in range(each):
            at = c * each + t
            i, lane = at // tiles, at % tiles
            value = coulomb[:, t * LANES : (t + 1) * LANES] + acc[
                pl.ds(pl.multiple_of(i * half, half), half),
                pl.ds(pl.multiple_of(lane * LANES, LANES), LANES),
            ]
            owner, rest = at // (parts * per), at % (parts * per)
            slot = owner ^ me if count > 1 else owner
            held[
                slot, rest // per, :, pl.ds(pl.multiple_of((rest % per) * LANES, LANES), LANES)
            ] = value
        return 0

    lax.fori_loop(0, chunks, fac_step, 0)

    radix = len(outs)
    for d, out in enumerate(outs):
        for n in range(out.shape[0]):
            out[n] = held[n * radix + d].astype(out.dtype)


def local(trial, energy_gap, coulomb_factors, occ_values, vir_values, kernel, live_points, sizes):
    groups, blks, vecs = sizes
    rows, k = trial.shape
    half = k // vecs
    aux, pairs = coulomb_factors.shape
    batches, occ_count, points = occ_values.shape
    virs = vir_values.shape[2]
    mine = pairs // groups
    occs = occ_count // groups
    digits = digits_of(blks)
    vec = lax.axis_index("vec")
    me = lax.axis_index("blk")
    vmem = pl.BlockSpec(memory_space=pltpu.VMEM)
    anywhere = pl.BlockSpec(memory_space=pl.ANY)

    wide_rows = trial.T.reshape(vecs, half, rows)
    keep = lax.dynamic_index_in_dim(wide_rows, vec, 0, keepdims=False)
    give = lax.dynamic_index_in_dim(wide_rows, 1 - vec, 0, keepdims=False)
    take = swap(give, "vec", vecs, 1)
    first = vec == 0
    own = jnp.stack([jnp.where(first, keep, take), jnp.where(first, take, keep)])

    pieces, masks = [own], [0]
    for stride, radix in reversed(digits):
        base_pieces, base_masks = list(pieces), list(masks)
        for d in range(1, radix):
            for piece, mask in zip(base_pieces, base_masks):
                pieces.append(swap(piece, "blk", blks, d * stride))
                masks.append(mask ^ (d * stride))

    aligned = rows % LANES == 0
    if not aligned:
        ordered = jnp.stack([p for _, p in sorted(zip(masks, pieces), key=lambda x: x[0])])
        ordered = jnp.take(ordered, me ^ jnp.arange(blks), axis=0)
        pieces = [ordered.transpose(2, 0, 1, 3).reshape(1, half, mine)]
        masks = [0]

    chunks = 5 if (mine // LANES) % 5 == 0 else 1
    wide = mine // chunks
    scratch = [
        pltpu.VMEM((occ_count, points), jnp.float32),
        pltpu.VMEM((batches, points, virs), jnp.bfloat16),
        pltpu.VMEM((chunks, aux, wide), jnp.bfloat16),
        pltpu.SemaphoreType.DMA((batches,)),
        pltpu.SemaphoreType.DMA((chunks,)),
    ]
    limit = pltpu.CompilerParams(vmem_limit_bytes=40 * 2**20)
    dens, part = pl.pallas_call(
        lambda *refs: first_kernel(half, tuple(masks), *refs),
        out_shape=(
            jax.ShapeDtypeStruct((batches, half, points), jnp.float32),
            jax.ShapeDtypeStruct((half, aux), jnp.float32),
        ),
        in_specs=[vmem] * len(pieces) + [vmem, anywhere, anywhere],
        out_specs=(vmem, vmem),
        scratch_shapes=[
            pltpu.VMEM((occs * half, virs), jnp.bfloat16),
            pltpu.VMEM((half, mine), jnp.bfloat16),
        ]
        + scratch,
        compiler_params=limit,
        name="first",
        cost_estimate=pl.CostEstimate(
            flops=2 * half * mine * (aux + batches * points),
            bytes_accessed=2 * (aux * mine + vir_values.size),
            transcendentals=0,
        ),
    )(*pieces, occ_values, vir_values, coulomb_factors)

    other_part = swap(part, "grp", groups, 1)
    other_dens = swap(dens.astype(jnp.bfloat16), "grp", groups, 1)

    if aligned:
        blocks = (blks, vecs, rows)
        radix = digits[0][1]
    else:
        blocks = (1, 1, mine)
        radix = 1
    held = (blocks[0], blocks[1], half, blocks[2])
    out_shape = tuple(
        jax.ShapeDtypeStruct(
            (blocks[0] // radix,) + held[1:], jnp.float32 if d == 0 else jnp.bfloat16
        )
        for d in range(radix)
    )
    sums = pl.pallas_call(
        lambda *refs: second_kernel(half, blocks, *refs),
        out_shape=out_shape,
        in_specs=[pl.BlockSpec(memory_space=pltpu.SMEM)] + [vmem] * 6 + [anywhere, anywhere],
        out_specs=tuple(vmem for _ in out_shape),
        scratch_shapes=scratch
        + [
            pltpu.VMEM((occs * half, points), jnp.bfloat16),
            pltpu.VMEM((occs * half, virs), jnp.float32),
            pltpu.VMEM((half, aux), jnp.bfloat16),
            pltpu.VMEM(held, jnp.float32),
        ],
        compiler_params=limit,
        name="second",
        cost_estimate=pl.CostEstimate(
            flops=2 * half * mine * (aux + batches * points),
            bytes_accessed=2 * (aux * mine + vir_values.size),
            transcendentals=0,
        ),
    )(live_points, dens, other_dens, part, other_part, occ_values, kernel, vir_values, coulomb_factors)

    if aligned:
        stay, sends = sums[0], list(sums[1:])
    else:
        full = sums[0].reshape(half, blks, vecs, rows).transpose(1, 2, 0, 3)
        full = jnp.take(full, me ^ jnp.arange(blks), axis=0)
        radix = digits[0][1]
        full = full.reshape((blks // radix, radix) + full.shape[1:])
        stay = full[:, 0]
        sends = [full[:, d].astype(jnp.bfloat16) for d in range(1, radix)]

    for level, (stride, radix) in enumerate(digits):
        total = stay
        for d in range(1, radix):
            total = total + swap(sends[d - 1], "blk", blks, d * stride).astype(jnp.float32)
        if level + 1 < len(digits):
            radix = digits[level + 1][1]
            total = total.reshape((-1, radix) + total.shape[1:])
            stay = total[:, 0]
            sends = [total[:, d].astype(jnp.bfloat16) for d in range(1, radix)]
    total = total.reshape(vecs, half, rows)

    keep = lax.dynamic_index_in_dim(total, vec, 0, keepdims=False)
    give = lax.dynamic_index_in_dim(total, 1 - vec, 0, keepdims=False)
    take = swap(give, "vec", vecs, 1)
    joined = jnp.concatenate([jnp.where(first, keep, take), jnp.where(first, take, keep)])
    result = energy_gap[None, :] * trial.T.astype(jnp.float32) + joined
    return result.astype(jnp.bfloat16).T


def solution(mesh):
    sizes = tuple(mesh.shape[a] for a in ("grp", "blk", "vec"))
    in_specs = (
        P(("grp", "blk", "vec"), None),
        P(("grp", "blk", "vec")),
        P("blk", None),
        P("blk", None, None),
        P("blk", None, None),
        P("blk", None),
        P("blk"),
    )
    out_specs = P(("grp", "blk", "vec"), None)

    def program(*args):
        return local(*args, sizes=sizes)

    return jax.shard_map(program, mesh=mesh, in_specs=in_specs, out_specs=out_specs, check_vma=False)
```

time: 208 us -> 57.9 us (0.28)
  waiting for transfers between devices: 76.8 us -> 19.4 us
  blocking collectives: 50.1 us -> 0 us
  matrix products: 48.4 us -> 0 us
  Pallas kernels: 0 us -> 14.8 us
  starting transfers between devices: 3.31 us -> 17.5 us
  between operations: 13.4 us -> 0.13 us
  local copies, waits for them, and re-layouts: 9.57 us -> 4.28 us
  other arithmetic: 4.78 us -> 1.48 us
    reduce_scatter x1 -> x0, waiting for transfers between devices: 75.5 us -> none  [local(): lax.psum_scatter(partial_sum, ('grp', 'blk'), scatter_dimension=0, tiled=...]
    dot_general x11 -> x0, matrix products: 48.4 us -> none  [the longest x1 28.3 us: coulomb_term(): lax.dot_general(coulomb_factors, factored, (((0,), (0,)), ((), ())), pref...]
    all_gather x1 -> x0, blocking collectives: 46.4 us -> none  [local(): full = lax.all_gather(pair_rows, ('grp', 'blk'), axis=0, tiled=True)]
    ppermute x0 -> x15, waiting for transfers between devices: none -> 19.4 us  [swap(): return lax.ppermute(x, axis, [(i, i ^ mask) for i in range(count)])]
    ppermute x0 -> x15, starting transfers between devices: none -> 17.5 us  [swap(): return lax.ppermute(x, axis, [(i, i ^ mask) for i in range(count)])]
    pallas_call x0 -> x2, Pallas kernels: none -> 14.8 us  [the longest x1 8.27 us: local(): pl.pallas_call(lambda *refs: first_kernel(half, tuple(masks), *refs), out...]
    slice x3 -> x0, local copies, waits for them, and re-layouts: 3.78 us -> none  [the longest x1 3.76 us: grid_term(): vir_values[first:last]]
    all_to_all x1 -> x0, blocking collectives: 3.76 us -> none  [local(): lax.all_to_all(summed, 'vec', split_axis=0, concat_axis=1, tiled=True)]
  transfers between devices with their start and end apart: 2 -> 15, of which waited for: 2 -> 10; matrix products, arithmetic and copies ran while one was open for 0% -> 0% of each run, Pallas kernels for 0% -> 0%
where the time goes in v1:
time: 57.9 us; the launch traced here: 57.6 us
  waiting for transfers between devices  19.4 us (34%)
  starting transfers between devices  17.5 us (30%)
  Pallas kernels  14.8 us (26%)
  local copies, waits for them, and re-layouts  4.28 us (7%)
  other arithmetic  1.48 us (3%)
    ppermute x15, waiting for transfers between devices, swap(): return lax.ppermute(x, axis, [(i, i ^ mask) for i in range(count)])  19.4 us
    ppermute x15, starting transfers between devices, swap(): return lax.ppermute(x, axis, [(i, i ^ mask) for i in range(count)])  17.5 us
    pallas_call x1, Pallas kernels, local(): pl.pallas_call(lambda *refs: first_kernel(half, tuple(masks), *refs), out...  8.27 us
    pallas_call x1, Pallas kernels, local(): pl.pallas_call(lambda *refs: second_kernel(half, blocks, *refs), out_shap...  6.51 us
    unnamed x14, local copies, waits for them, and re-layouts  3.51 us
  transfers between devices with their start and end apart: 15, of which 10 were waited for; matrix products, arithmetic and copies ran while one was open for 0% of the time, Pallas kernels for 0%

profile of v1, /device:TPU:0, one launch (start us, length us, event | category | flops | bytes accessed | tf_op | source)
XLA Modules:
  0.0 57.6 jit_solution(13689877511280351658)
XLA Ops:
  0.0 0.0 copy-start.4
  0.0 0.0 copy-start.3
  0.0 0.7 %dynamic-slice_bitcast_fusion.1 = bf16[16,640]{1,0:T(8,128)(2,1)S(1)} fusion(bf16[2,16,640]{2,1,0:T(8,128)(2,1)} %bitcast.41, s32[]{:T(128)S(6)} %select_n.34), kind=kLoop, calls=%fused_computation.19 | loop fusion | bytes 40964 | tf_op jit(solution)/shard_map/jit(dynamic_index_in_dim)/squeeze | solution.py:184
  0.8 0.5 collective-permute-start
  1.2 0.8 %collective-permute-done = bf16[16,640]{1,0:T(8,128)(2,1)S(1)} collective-permute-done((bf16[16,640]{1,0:T(8,128)(2,1)S(1)}, bf16[16,640]{1,0:T(8,128)(2,1)S(1)}, u32[]{:S(2)}, u32[]{:S(2)}) %collective-permute-start) | collective-permute-done | bytes 20512 | tf_op jit(solution)/shard_map/ppermute | solution.py:26
  2.1 0.7 %fusion.5 = (bf16[1,16,640]{2,1,0:T(8,128)(2,1)S(1)}, bf16[1,16,640]{2,1,0:T(8,128)(2,1)S(1)}) fusion(bf16[16,640]{1,0:T(8,128)(2,1)S(1)} %collective-permute-done, pred[]{:T(512)S(6)} %eq.3, bf16[2,16,640]{2,1,0:T(8,128)(2,1)} %bitcast.42, s32[]{:T(128)S(6)} %select_n.33), kind=kLoop, calls=%fused_computation.17 | loop fusion | flops 20480 | bytes 81925 | tf_op jit(solution)/shard_map/stack | solution.py:187
  2.8 5.0 %collective-permute-start.3 = (bf16[2,16,640]{2,1,0:T(8,128)(2,1)S(1)}, bf16[2,16,640]{2,1,0:T(8,128)(2,1)S(1)}, u32[]{:S(2)}, u32[]{:S(2)}) collective-permute-start(bf16[2,16,640]{2,1,0:T(8,128)(2,1)S(1)} %pad_maximum_fusion.refs_0_), channel_id=1, source_target_pairs={{0,12},{2,14},{4,8},{6,10},{8,4},{10,6},{12,0},{14,2},{1,13},{3,15... | collective-permute-start | bytes 122888 | tf_op jit(solution)/shard_map/ppermute | solution.py:26
  7.8 0.0 collective-permute-start.2
  7.8 0.6 %collective-permute-start.1 = (bf16[2,16,640]{2,1,0:T(8,128)(2,1)S(1)}, bf16[2,16,640]{2,1,0:T(8,128)(2,1)S(1)}, u32[]{:S(2)}, u32[]{:S(2)}) collective-permute-start(bf16[2,16,640]{2,1,0:T(8,128)(2,1)S(1)} %pad_maximum_fusion.refs_0_), channel_id=1, source_target_pairs={{0,4},{2,6},{4,0},{6,2},{8,12},{10,14},{12,8},{14,10},{1,5},{3,7},... | collective-permute-start | bytes 122888 | tf_op jit(solution)/shard_map/ppermute | solution.py:26
  8.5 1.7 %collective-permute-start.4 = (bf16[2,16,640]{2,1,0:T(8,128)(2,1)S(1)}, bf16[2,16,640]{2,1,0:T(8,128)(2,1)S(1)}, u32[]{:S(2)}, u32[]{:S(2)}) collective-permute-start(bf16[2,16,640]{2,1,0:T(8,128)(2,1)S(1)} %pad_maximum_fusion.refs_0_), channel_id=1, source_target_pairs={{0,2},{2,0},{4,6},{6,4},{8,10},{10,8},{12,14},{14,12},{1,3},{3,1},... | collective-permute-start | bytes 122888 | tf_op jit(solution)/shard_map/ppermute | solution.py:26
  10.1 0.0 collective-permute-done.3.refs_3_
  10.1 1.4 %collective-permute-start.7 = (bf16[2,16,640]{2,1,0:T(8,128)(2,1)S(1)}, bf16[2,16,640]{2,1,0:T(8,128)(2,1)S(1)}, u32[]{:S(2)}, u32[]{:S(2)}) collective-permute-start(bf16[2,16,640]{2,1,0:T(8,128)(2,1)S(1)} %collective-permute-done.3.refs_3_), channel_id=1, source_target_pairs={{0,2},{2,0},{4,6},{6,4},{8,10},{10,8},{12,14},{14,12},{1,3},{3,1},... | collective-permute-start | bytes 122888 | tf_op jit(solution)/shard_map/ppermute | solution.py:26
  11.6 1.2 %collective-permute-done.2.refs_2_ = bf16[2,16,640]{2,1,0:T(8,128)(2,1)S(1)} collective-permute-done((bf16[2,16,640]{2,1,0:T(8,128)(2,1)S(1)}, bf16[2,16,640]{2,1,0:T(8,128)(2,1)S(1)}, u32[]{:S(2)}, u32[]{:S(2)}) %collective-permute-start.2) | collective-permute-done | bytes 40992 | tf_op jit(solution)/shard_map/ppermute | solution.py:26
  12.7 1.5 %collective-permute-start.6 = (bf16[2,16,640]{2,1,0:T(8,128)(2,1)S(1)}, bf16[2,16,640]{2,1,0:T(8,128)(2,1)S(1)}, u32[]{:S(2)}, u32[]{:S(2)}) collective-permute-start(bf16[2,16,640]{2,1,0:T(8,128)(2,1)S(1)} %collective-permute-done.2.refs_2_), channel_id=1, source_target_pairs={{0,2},{2,0},{4,6},{6,4},{8,10},{10,8},{12,14},{14,12},{1,3},{3,1},... | collective-permute-start | bytes 122888 | tf_op jit(solution)/shard_map/ppermute | solution.py:26
  14.3 0.0 collective-permute-done.1.refs_1_
  14.3 0.5 collective-permute-start.5
  14.8 0.0 collective-permute-done.4.refs_4_
  14.8 0.0 collective-permute-done.7.refs_7_
  14.8 2.0 %collective-permute-done.6.refs_6_ = bf16[2,16,640]{2,1,0:T(8,128)(2,1)S(1)} collective-permute-done((bf16[2,16,640]{2,1,0:T(8,128)(2,1)S(1)}, bf16[2,16,640]{2,1,0:T(8,128)(2,1)S(1)}, u32[]{:S(2)}, u32[]{:S(2)}) %collective-permute-start.6) | collective-permute-done | bytes 40992 | tf_op jit(solution)/shard_map/ppermute | solution.py:26
  16.7 1.5 %collective-permute-done.5.refs_5_ = bf16[2,16,640]{2,1,0:T(8,128)(2,1)S(1)} collective-permute-done((bf16[2,16,640]{2,1,0:T(8,128)(2,1)S(1)}, bf16[2,16,640]{2,1,0:T(8,128)(2,1)S(1)}, u32[]{:S(2)}, u32[]{:S(2)}) %collective-permute-start.5) | collective-permute-done | bytes 40992 | tf_op jit(solution)/shard_map/ppermute | solution.py:26
  18.3 0.0 copy-start
  18.3 2.5 %copy-done = bf16[10,512,512]{2,1,0:T(8,128)(2,1)S(1)} copy-done((bf16[10,512,512]{2,1,0:T(8,128)(2,1)S(1)}, bf16[10,512,512]{2,1,0:T(8,128)(2,1)}, u32[]{:S(2)}) %copy-start) | copy-done | bytes 5242904
  20.7 0.0 copy-start.2
  20.8 1.0 %copy-done.2 = bf16[10,40,512]{2,1,0:T(8,128)(2,1)S(1)} copy-done((bf16[10,40,512]{2,1,0:T(8,128)(2,1)S(1)}, bf16[10,40,512]{2,1,0:T(8,128)(2,1)}, u32[]{:S(2)}) %copy-start.2) | copy-done | bytes 409624
  21.8 0.0 copy-start.1
  21.8 8.3 %first.1 = (f32[10,16,512]{2,1,0:T(8,128)S(1)}, f32[16,512]{1,0:T(8,128)S(1)}) custom-call(bf16[2,16,640]{2,1,0:T(8,128)(2,1)S(1)} %pad_maximum_fusion.refs_0_, bf16[2,16,640]{2,1,0:T(8,128)(2,1)S(1)} %collective-permute-done.1.refs_1_, bf16[2,16,640]{2,1,0:T(8,128)(2,1)S(1)} %collective-permute-done.2.refs_2_, ...), custom_call_target="tpu_custom_call" | custom-call | flops 1845493760 | bytes 15728640 | tf_op jit(solution)/shard_map/first/pallas_call | solution.py:214
  30.0 0.0 copy-start.5
  30.0 0.0 copy-start.6
  30.1 1.5 %collective-permute-start.8 = (bf16[10,16,512]{2,1,0:T(8,128)(2,1)S(1)}, bf16[10,16,512]{2,1,0:T(8,128)(2,1)S(1)}, u32[]{:S(2)}, u32[]{:S(2)}) collective-permute-start(bf16[10,16,512]{2,1,0:T(8,128)(2,1)S(1)} %convert_element_type.58), channel_id=1, source_target_pairs={{0,16},{16,0},{1,17},{17,1},{2,18},{18,2},{3,19},{19,3},{4,20},{20... | collective-permute-start | bytes 491528 | tf_op jit(solution)/shard_map/ppermute | solution.py:26
  31.6 0.6 %collective-permute-start.9 = (f32[16,512]{1,0:T(8,128)S(1)}, f32[16,512]{1,0:T(8,128)S(1)}, u32[]{:S(2)}, u32[]{:S(2)}) collective-permute-start(f32[16,512]{1,0:T(8,128)S(1)} %get-tuple-element.10.refs_3_), channel_id=1, source_target_pairs={{0,16},{16,0},{1,17},{17,1},{2,18},{18,2},{3,19},{19,3},{4,20},{20... | collective-permute-start | bytes 98312 | tf_op jit(solution)/shard_map/ppermute | solution.py:26
  32.2 3.6 %collective-permute-done.9.refs_4_ = f32[16,512]{1,0:T(8,128)S(1)} collective-permute-done((f32[16,512]{1,0:T(8,128)S(1)}, f32[16,512]{1,0:T(8,128)S(1)}, u32[]{:S(2)}, u32[]{:S(2)}) %collective-permute-start.9) | collective-permute-done | bytes 32800 | tf_op jit(solution)/shard_map/ppermute | solution.py:26
  35.8 0.0 collective-permute-done.8.refs_2_
  35.8 0.0 copy-done.4
  35.8 0.0 copy-done.3
  35.8 0.0 copy-done.1
  35.8 6.5 %second.1 = (f32[4,2,16,640]{3,2,1,0:T(8,128)S(1)}, bf16[4,2,16,640]{3,2,1,0:T(8,128)(2,1)S(1)}) custom-call(s32[10]{0:T(128)S(1)} %copy-done.4, f32[10,16,512]{2,1,0:T(8,128)S(1)} %get-tuple-element.9.refs_1_, bf16[10,16,512]{2,1,0:T(8,128)(2,1)S(1)} %collective-permute-done.8.refs_2_, f32[16,512]{1,0:T(8,128)S(1)} %get-tuple-element.10.refs_3_, ...), custom_call_target="tpu_custom_call" | custom-call | flops 1845493760 | bytes 15728640 | tf_op jit(solution)/shard_map/second/pallas_call | solution.py:252
  42.4 0.6 collective-permute-start.10
  42.9 4.8 %collective-permute-done.10 = bf16[4,2,16,640]{3,2,1,0:T(8,128)(2,1)S(1)} collective-permute-done((bf16[4,2,16,640]{3,2,1,0:T(8,128)(2,1)S(1)}, bf16[4,2,16,640]{3,2,1,0:T(8,128)(2,1)S(1)}, u32[]{:S(2)}, u32[]{:S(2)}) %collective-permute-start.10) | collective-permute-done | bytes 163872 | tf_op jit(solution)/shard_map/ppermute | solution.py:26
  47.8 0.1 collective-permute-start.11
  47.9 2.3 %collective-permute-start.13 = (bf16[1,2,16,640]{3,2,1,0:T(8,128)(2,1)S(1)}, bf16[1,2,16,640]{3,2,1,0:T(8,128)(2,1)S(1)}, u32[]{:S(2)}, u32[]{:S(2)}) collective-permute-start(bf16[1,2,16,640]{3,2,1,0:T(8,128)(2,1)S(1)} %get-tuple-element.16), channel_id=1, source_target_pairs={{0,12},{2,14},{4,8},{6,10},{8,4},{10,6},{12,0},{14,2},{1,13},{3,15... | collective-permute-start | bytes 122888 | tf_op jit(solution)/shard_map/ppermute | solution.py:26
  50.2 1.2 %collective-permute-start.12 = (bf16[1,2,16,640]{3,2,1,0:T(8,128)(2,1)S(1)}, bf16[1,2,16,640]{3,2,1,0:T(8,128)(2,1)S(1)}, u32[]{:S(2)}, u32[]{:S(2)}) collective-permute-start(bf16[1,2,16,640]{3,2,1,0:T(8,128)(2,1)S(1)} %get-tuple-element.17), channel_id=1, source_target_pairs={{0,8},{2,10},{4,12},{6,14},{8,0},{10,2},{12,4},{14,6},{1,9},{3,11}... | collective-permute-start | bytes 122888 | tf_op jit(solution)/shard_map/ppermute | solution.py:26
  51.4 0.5 collective-permute-done.11
  51.9 1.9 %collective-permute-done.13 = bf16[1,2,16,640]{3,2,1,0:T(8,128)(2,1)S(1)} collective-permute-done((bf16[1,2,16,640]{3,2,1,0:T(8,128)(2,1)S(1)}, bf16[1,2,16,640]{3,2,1,0:T(8,128)(2,1)S(1)}, u32[]{:S(2)}, u32[]{:S(2)}) %collective-permute-start.13) | collective-permute-done | bytes 40992 | tf_op jit(solution)/shard_map/ppermute | solution.py:26
  53.8 1.8 %collective-permute-done.12 = bf16[1,2,16,640]{3,2,1,0:T(8,128)(2,1)S(1)} collective-permute-done((bf16[1,2,16,640]{3,2,1,0:T(8,128)(2,1)S(1)}, bf16[1,2,16,640]{3,2,1,0:T(8,128)(2,1)S(1)}, u32[]{:S(2)}, u32[]{:S(2)}) %collective-permute-start.12) | collective-permute-done | bytes 40992 | tf_op jit(solution)/shard_map/ppermute | solution.py:26
  55.6 0.1 collective-permute-start.14
  55.7 1.2 %collective-permute-done.14 = f32[16,640]{1,0:T(8,128)S(1)} collective-permute-done((f32[16,640]{1,0:T(8,128)S(1)}, f32[16,640]{1,0:T(8,128)S(1)}, u32[]{:S(2)}, u32[]{:S(2)}) %collective-permute-start.14) | collective-permute-done | bytes 40992 | tf_op jit(solution)/shard_map/ppermute | solution.py:26
  56.9 0.0 copy-done.5
  56.9 0.0 copy-done.6
  56.9 0.6 %fusion.4 = bf16[640,32]{0,1:T(8,128)(2,1)} fusion(f32[16,640]{1,0:T(8,128)S(1)} %get-tuple-element.19, f32[16,640]{1,0:T(8,128)S(1)} %get-tuple-element.18, bf16[640,32]{0,1:T(8,128)(2,1)S(1)} %copy-done.5, f32[640]{0:T(1024)S(1)} %copy-done.6), kind=kLoop, calls=%fused_computation.7 | loop fusion | flops 102400 | bytes 166400 | tf_op jit(solution)/shard_map/transpose | solution.py:299
  (7 shorter events, 0.1 us)
Async XLA Ops:
  0.0 35.8 %copy-start.4 = (s32[10]{0:T(128)S(1)}, s32[10]{0:T(128)}, u32[]{:S(2)}) copy-start(s32[10]{0:T(128)} %refs_0_.1) | copy-start | bytes 124
  0.0 35.8 %copy-start.3 = (f32[10,512]{1,0:T(8,128)S(1)}, f32[10,512]{1,0:T(8,128)}, u32[]{:S(2)}) copy-start(f32[10,512]{1,0:T(8,128)} %refs_6_.1) | copy-start | bytes 61444
  0.8 1.3 %collective-permute-start = (bf16[16,640]{1,0:T(8,128)(2,1)S(1)}, bf16[16,640]{1,0:T(8,128)(2,1)S(1)}, u32[]{:S(2)}, u32[]{:S(2)}) collective-permute-start(bf16[16,640]{1,0:T(8,128)(2,1)S(1)} %dynamic-slice_bitcast_fusion.1), channel_id=1, source_target_pairs={{0,1},{1,0},{2,3},{3,2},{4,5},{5,4},{6,7},{7,6},{8,9},{9,8},{10,11... | collective-permute-start | bytes 61448 | tf_op jit(solution)/shard_map/ppermute | solution.py:26
  2.8 7.3 %collective-permute-start.3 = (bf16[2,16,640]{2,1,0:T(8,128)(2,1)S(1)}, bf16[2,16,640]{2,1,0:T(8,128)(2,1)S(1)}, u32[]{:S(2)}, u32[]{:S(2)}) collective-permute-start(bf16[2,16,640]{2,1,0:T(8,128)(2,1)S(1)} %pad_maximum_fusion.refs_0_), channel_id=1, source_target_pairs={{0,12},{2,14},{4,8},{6,10},{8,4},{10,6},{12,0},{14,2},{1,13},{3,15... | collective-permute-start | bytes 122888 | tf_op jit(solution)/shard_map/ppermute | solution.py:26
  7.8 4.9 %collective-permute-start.2 = (bf16[2,16,640]{2,1,0:T(8,128)(2,1)S(1)}, bf16[2,16,640]{2,1,0:T(8,128)(2,1)S(1)}, u32[]{:S(2)}, u32[]{:S(2)}) collective-permute-start(bf16[2,16,640]{2,1,0:T(8,128)(2,1)S(1)} %pad_maximum_fusion.refs_0_), channel_id=1, source_target_pairs={{0,8},{2,10},{4,12},{6,14},{8,0},{10,2},{12,4},{14,6},{1,9},{3,11}... | collective-permute-start | bytes 122888 | tf_op jit(solution)/shard_map/ppermute | solution.py:26
  7.8 6.4 %collective-permute-start.1 = (bf16[2,16,640]{2,1,0:T(8,128)(2,1)S(1)}, bf16[2,16,640]{2,1,0:T(8,128)(2,1)S(1)}, u32[]{:S(2)}, u32[]{:S(2)}) collective-permute-start(bf16[2,16,640]{2,1,0:T(8,128)(2,1)S(1)} %pad_maximum_fusion.refs_0_), channel_id=1, source_target_pairs={{0,4},{2,6},{4,0},{6,2},{8,12},{10,14},{12,8},{14,10},{1,5},{3,7},... | collective-permute-start | bytes 122888 | tf_op jit(solution)/shard_map/ppermute | solution.py:26
  8.5 6.3 %collective-permute-start.4 = (bf16[2,16,640]{2,1,0:T(8,128)(2,1)S(1)}, bf16[2,16,640]{2,1,0:T(8,128)(2,1)S(1)}, u32[]{:S(2)}, u32[]{:S(2)}) collective-permute-start(bf16[2,16,640]{2,1,0:T(8,128)(2,1)S(1)} %pad_maximum_fusion.refs_0_), channel_id=1, source_target_pairs={{0,2},{2,0},{4,6},{6,4},{8,10},{10,8},{12,14},{14,12},{1,3},{3,1},... | collective-permute-start | bytes 122888 | tf_op jit(solution)/shard_map/ppermute | solution.py:26
  10.1 4.6 %collective-permute-start.7 = (bf16[2,16,640]{2,1,0:T(8,128)(2,1)S(1)}, bf16[2,16,640]{2,1,0:T(8,128)(2,1)S(1)}, u32[]{:S(2)}, u32[]{:S(2)}) collective-permute-start(bf16[2,16,640]{2,1,0:T(8,128)(2,1)S(1)} %collective-permute-done.3.refs_3_), channel_id=1, source_target_pairs={{0,2},{2,0},{4,6},{6,4},{8,10},{10,8},{12,14},{14,12},{1,3},{3,1},... | collective-permute-start | bytes 122888 | tf_op jit(solution)/shard_map/ppermute | solution.py:26
  12.7 4.0 %collective-permute-start.6 = (bf16[2,16,640]{2,1,0:T(8,128)(2,1)S(1)}, bf16[2,16,640]{2,1,0:T(8,128)(2,1)S(1)}, u32[]{:S(2)}, u32[]{:S(2)}) collective-permute-start(bf16[2,16,640]{2,1,0:T(8,128)(2,1)S(1)} %collective-permute-done.2.refs_2_), channel_id=1, source_target_pairs={{0,2},{2,0},{4,6},{6,4},{8,10},{10,8},{12,14},{14,12},{1,3},{3,1},... | collective-permute-start | bytes 122888 | tf_op jit(solution)/shard_map/ppermute | solution.py:26
  14.3 4.0 %collective-permute-start.5 = (bf16[2,16,640]{2,1,0:T(8,128)(2,1)S(1)}, bf16[2,16,640]{2,1,0:T(8,128)(2,1)S(1)}, u32[]{:S(2)}, u32[]{:S(2)}) collective-permute-start(bf16[2,16,640]{2,1,0:T(8,128)(2,1)S(1)} %collective-permute-done.1.refs_1_), channel_id=1, source_target_pairs={{0,2},{2,0},{4,6},{6,4},{8,10},{10,8},{12,14},{14,12},{1,3},{3,1},... | collective-permute-start | bytes 122888 | tf_op jit(solution)/shard_map/ppermute | solution.py:26
  18.3 2.5 %copy-start = (bf16[10,512,512]{2,1,0:T(8,128)(2,1)S(1)}, bf16[10,512,512]{2,1,0:T(8,128)(2,1)}, u32[]{:S(2)}) copy-start(bf16[10,512,512]{2,1,0:T(8,128)(2,1)} %refs_7_.1) | copy-start | bytes 15728644
  20.7 1.0 %copy-start.2 = (bf16[10,40,512]{2,1,0:T(8,128)(2,1)S(1)}, bf16[10,40,512]{2,1,0:T(8,128)(2,1)}, u32[]{:S(2)}) copy-start(bf16[10,40,512]{2,1,0:T(8,128)(2,1)} %refs_5_.1) | copy-start | bytes 1228804
  21.8 14.1 %copy-start.1 = (bf16[10,512,512]{2,1,0:T(8,128)(2,1)S(1)}, bf16[10,512,512]{2,1,0:T(8,128)(2,1)}, u32[]{:S(2)}) copy-start(bf16[10,512,512]{2,1,0:T(8,128)(2,1)} %refs_7_.1) | copy-start | bytes 15728644
  30.0 26.9 %copy-start.5 = (bf16[640,32]{0,1:T(8,128)(2,1)S(1)}, bf16[640,32]{0,1:T(8,128)(2,1)}, u32[]{:S(2)}) copy-start(bf16[640,32]{0,1:T(8,128)(2,1)} %param.7) | copy-start | bytes 122884
  30.0 26.9 %copy-start.6 = (f32[640]{0:T(1024)S(1)}, f32[640]{0:T(1024)}, u32[]{:S(2)}) copy-start(f32[640]{0:T(1024)} %param.8) | copy-start | bytes 7684
  30.1 5.7 %collective-permute-start.8 = (bf16[10,16,512]{2,1,0:T(8,128)(2,1)S(1)}, bf16[10,16,512]{2,1,0:T(8,128)(2,1)S(1)}, u32[]{:S(2)}, u32[]{:S(2)}) collective-permute-start(bf16[10,16,512]{2,1,0:T(8,128)(2,1)S(1)} %convert_element_type.58), channel_id=1, source_target_pairs={{0,16},{16,0},{1,17},{17,1},{2,18},{18,2},{3,19},{19,3},{4,20},{20... | collective-permute-start | bytes 491528 | tf_op jit(solution)/shard_map/ppermute | solution.py:26
  31.6 4.3 %collective-permute-start.9 = (f32[16,512]{1,0:T(8,128)S(1)}, f32[16,512]{1,0:T(8,128)S(1)}, u32[]{:S(2)}, u32[]{:S(2)}) collective-permute-start(f32[16,512]{1,0:T(8,128)S(1)} %get-tuple-element.10.refs_3_), channel_id=1, source_target_pairs={{0,16},{16,0},{1,17},{17,1},{2,18},{18,2},{3,19},{19,3},{4,20},{20... | collective-permute-start | bytes 98312 | tf_op jit(solution)/shard_map/ppermute | solution.py:26
  42.4 5.4 %collective-permute-start.10 = (bf16[4,2,16,640]{3,2,1,0:T(8,128)(2,1)S(1)}, bf16[4,2,16,640]{3,2,1,0:T(8,128)(2,1)S(1)}, u32[]{:S(2)}, u32[]{:S(2)}) collective-permute-start(bf16[4,2,16,640]{3,2,1,0:T(8,128)(2,1)S(1)} %get-tuple-element.12), channel_id=1, source_target_pairs={{0,2},{2,0},{4,6},{6,4},{8,10},{10,8},{12,14},{14,12},{1,3},{3,1},... | collective-permute-start | bytes 491528 | tf_op jit(solution)/shard_map/ppermute | solution.py:26
  47.8 4.1 %collective-permute-start.11 = (bf16[1,2,16,640]{3,2,1,0:T(8,128)(2,1)S(1)}, bf16[1,2,16,640]{3,2,1,0:T(8,128)(2,1)S(1)}, u32[]{:S(2)}, u32[]{:S(2)}) collective-permute-start(bf16[1,2,16,640]{3,2,1,0:T(8,128)(2,1)S(1)} %get-tuple-element.15), channel_id=1, source_target_pairs={{0,4},{2,6},{4,0},{6,2},{8,12},{10,14},{12,8},{14,10},{1,5},{3,7},... | collective-permute-start | bytes 122888 | tf_op jit(solution)/shard_map/ppermute | solution.py:26
  47.9 5.9 %collective-permute-start.13 = (bf16[1,2,16,640]{3,2,1,0:T(8,128)(2,1)S(1)}, bf16[1,2,16,640]{3,2,1,0:T(8,128)(2,1)S(1)}, u32[]{:S(2)}, u32[]{:S(2)}) collective-permute-start(bf16[1,2,16,640]{3,2,1,0:T(8,128)(2,1)S(1)} %get-tuple-element.16), channel_id=1, source_target_pairs={{0,12},{2,14},{4,8},{6,10},{8,4},{10,6},{12,0},{14,2},{1,13},{3,15... | collective-permute-start | bytes 122888 | tf_op jit(solution)/shard_map/ppermute | solution.py:26
  50.2 5.3 %collective-permute-start.12 = (bf16[1,2,16,640]{3,2,1,0:T(8,128)(2,1)S(1)}, bf16[1,2,16,640]{3,2,1,0:T(8,128)(2,1)S(1)}, u32[]{:S(2)}, u32[]{:S(2)}) collective-permute-start(bf16[1,2,16,640]{3,2,1,0:T(8,128)(2,1)S(1)} %get-tuple-element.17), channel_id=1, source_target_pairs={{0,8},{2,10},{4,12},{6,14},{8,0},{10,2},{12,4},{14,6},{1,9},{3,11}... | collective-permute-start | bytes 122888 | tf_op jit(solution)/shard_map/ppermute | solution.py:26
  55.6 1.3 %collective-permute-start.14 = (f32[16,640]{1,0:T(8,128)S(1)}, f32[16,640]{1,0:T(8,128)S(1)}, u32[]{:S(2)}, u32[]{:S(2)}) collective-permute-start(f32[16,640]{1,0:T(8,128)S(1)} %dynamic-slice_bitcast_fusion), channel_id=1, source_target_pairs={{0,1},{1,0},{2,3},{3,2},{4,5},{5,4},{6,7},{7,6},{8,9},{9,8},{10,11... | collective-permute-start | bytes 122888 | tf_op jit(solution)/shard_map/ppermute | solution.py:26

commit v2 on v0

v2 whole, which is shorter than its diff:
```python
import jax
import jax.numpy as jnp
from jax import lax
from jax.experimental import pallas as pl
from jax.experimental.pallas import tpu as pltpu
from jax.sharding import PartitionSpec as P

LANES = 128
NT = (((1,), (1,)), ((), ()))
NN = (((1,), (0,)), ((), ()))
VMEM = pl.BlockSpec(memory_space=pltpu.VMEM)
SMEM = pl.BlockSpec(memory_space=pltpu.SMEM)
HBM = pl.BlockSpec(memory_space=pltpu.HBM)


def digits_of(count):
    digits, stride = [], 1
    bits = count.bit_length() - 1
    if bits % 2:
        digits.append((1, 2))
        stride = 2
    while stride < count:
        digits.append((stride, 4))
        stride *= 4
    return digits


def swap(x, axis, count, mask):
    return lax.ppermute(x, axis, [(i, i ^ mask) for i in range(count)])


def call(body, out_shape, in_specs, flops=0, scratch=(), limit=24, name=None):
    return pl.pallas_call(
        body,
        out_shape=out_shape,
        in_specs=in_specs,
        out_specs=jax.tree.map(lambda _: VMEM, out_shape),
        scratch_shapes=list(scratch),
        compiler_params=pltpu.CompilerParams(vmem_limit_bytes=limit * 2**20),
        name=name,
        cost_estimate=pl.CostEstimate(flops=flops, bytes_accessed=0, transcendentals=0),
    )


def shape(dims, dtype):
    return jax.ShapeDtypeStruct(dims, dtype)


class Plan:
    def __init__(self, sizes, trial, coulomb_factors, occ_values, vir_values):
        self.groups, self.blks, self.vecs = sizes
        self.rows, self.k = trial.shape
        self.aux = coulomb_factors.shape[0] // self.vecs
        self.pairs = coulomb_factors.shape[1] // self.groups
        self.batches = occ_values.shape[0] // self.vecs
        self.occ_all, self.points = occ_values.shape[1:]
        self.occs = self.occ_all // self.groups
        self.virs = vir_values.shape[2]
        self.aligned = self.rows % LANES == 0
        self.count = self.blks if self.aligned else 1
        self.length = self.rows if self.aligned else self.pairs // self.vecs
        self.per = self.length // LANES

    def owner(self, m):
        return lax.axis_index("blk") ^ m if self.aligned else 0

    def part(self, h):
        return lax.axis_index("vec") ^ h if self.aligned else h

    def block(self, h, m, j):
        return (self.owner(m) * self.vecs + self.part(h)) * self.per + j

    def place(self, h, m, j):
        at = self.block(h, m, j)
        tiles = self.virs // LANES
        return (
            pl.ds(pl.multiple_of((at // tiles) * self.k, self.k), self.k),
            pl.ds(pl.multiple_of((at % tiles) * LANES, LANES), LANES),
        )


def load_kernel(plan, fac_hbm, vir_hbm, occ_hbm, fac, vir, occ, occ_in, fsem, vsem, osem):
    grp, vec = lax.axis_index("grp"), lax.axis_index("vec")
    top = pl.multiple_of(vec * plan.aux, 8)
    base = vec * plan.batches
    copies = [
        pltpu.make_async_copy(occ_hbm.at[pl.ds(base, plan.batches)], occ_in, osem),
        pltpu.make_async_copy(vir_hbm.at[pl.ds(base, plan.batches)], vir, vsem),
    ]
    for h in range(plan.vecs):
        for m in range(plan.count):
            at = pl.multiple_of(grp * plan.pairs + plan.block(h, m, 0) * LANES, LANES)
            copies.append(
                pltpu.make_async_copy(
                    fac_hbm.at[pl.ds(top, plan.aux), pl.ds(at, plan.length)],
                    fac.at[h, :, pl.ds(m * plan.length, plan.length)],
                    fsem.at[h, m],
                )
            )
    for copy in copies:
        copy.start()
    copies[0].wait()
    for b in range(plan.batches):
        value = occ_in[b].astype(jnp.float32)
        chosen = value[: plan.occs]
        for q in range(1, plan.groups):
            chosen = jnp.where(grp == q, value[q * plan.occs : (q + 1) * plan.occs], chosen)
        occ[b] = chosen
    for copy in copies[1:]:
        copy.wait()


def flat_of(ref, count):
    return jnp.concatenate([ref[m] for m in range(count)], axis=1)


def stack_kernel(plan, *refs):
    for m, piece in enumerate(refs[1:-1]):
        refs[-1][m] = piece[...]


def fac_kernel(plan, h, half, fac, *refs):
    value = lax.dot_general(
        flat_of(half, plan.count), fac[h], NT, preferred_element_type=jnp.float32
    )
    if len(refs) > 1:
        value = value + refs[0][...]
    refs[-1][...] = value


def dens_kernel(plan, mine, other, vir, occ, dens, sent, rows):
    k = plan.k
    for h, half in enumerate((mine, other)):
        for m in range(plan.count):
            for j in range(plan.per):
                rows[plan.place(h, m, j)] = half[m, :, j * LANES : (j + 1) * LANES]
    for b in range(plan.batches):
        trans = lax.dot_general(rows[...], vir[b], NT, preferred_element_type=jnp.float32)
        total = occ[b, 0:1, :] * trans[:k, :]
        for i in range(1, plan.occs):
            total = total + occ[b, i : i + 1, :] * trans[i * k : (i + 1) * k, :]
        dens[b] = total
        sent[b] = total.astype(sent.dtype)


def back_kernel(plan, part_a, part_b, fac, out):
    both = (part_a[...] + part_b[...]).astype(jnp.bfloat16)
    for h in range(plan.vecs):
        value = 2.0 * lax.dot_general(both, fac[h], NN, preferred_element_type=jnp.float32)
        for m in range(plan.count):
            out[h, m] = value[:, m * plan.length : (m + 1) * plan.length]


def grid_kernel(plan, live, dens_a, dens_b, occ, weight, vir, coulomb, stay, sent, scaled, acc):
    k = plan.k
    base = lax.axis_index("vec") * plan.batches
    slots = lax.broadcasted_iota(jnp.int32, (1, plan.points), 1)
    for b in range(plan.batches):
        density = dens_a[b] + dens_b[b].astype(jnp.float32)
        used = jnp.where(slots < live[base + b], weight[pl.ds(base + b, 1), :], 0.0)
        weighted = density * used
        for i in range(plan.occs):
            scaled[i * k : (i + 1) * k, :] = (occ[b, i : i + 1, :] * weighted).astype(jnp.bfloat16)
        value = lax.dot_general(scaled[...], vir[b], NN, preferred_element_type=jnp.float32)
        if b == 0:
            acc[...] = value
        else:
            acc[...] += value
    for h, out in enumerate((stay, sent)):
        for m in range(plan.count):
            for j in range(plan.per):
                lanes = slice(j * LANES, (j + 1) * LANES)
                value = coulomb[h, m, :, lanes] + acc[plan.place(h, m, j)]
                out[m, :, lanes] = value.astype(out.dtype)


def local(trial, energy_gap, coulomb_factors, occ_values, vir_values, kernel, live_points, sizes):
    plan = Plan(sizes, trial, coulomb_factors, occ_values, vir_values)
    groups, blks, vecs, k = plan.groups, plan.blks, plan.vecs, plan.k
    batches, points, virs, occs = plan.batches, plan.points, plan.virs, plan.occs
    digits = digits_of(blks)
    half = (plan.count, k, plan.length)
    bf16, f32 = jnp.bfloat16, jnp.float32

    def bind(body, *first):
        return lambda *refs: body(plan, *first, *refs)

    fac, vir, occ = call(
        bind(load_kernel),
        (
            shape((vecs, plan.aux, plan.count * plan.length), bf16),
            shape((batches, points, virs), bf16),
            shape((batches, occs, points), f32),
        ),
        [HBM] * 3,
        flops=10**9,
        scratch=[
            pltpu.VMEM((batches, plan.occ_all, points), bf16),
            pltpu.SemaphoreType.DMA((vecs, plan.count)),
            pltpu.SemaphoreType.DMA,
            pltpu.SemaphoreType.DMA,
        ],
        limit=44,
        name="load",
    )(coulomb_factors, vir_values, occ_values)

    pieces, masks = [trial.T], [0]
    for stride, radix in reversed(digits):
        known = len(masks)
        for d in range(1, radix):
            for n in range(known):
                pieces.append(swap(pieces[n], "blk", blks, d * stride))
                masks.append(masks[n] ^ (d * stride))
    pieces = [p for _, p in sorted(zip(masks, pieces), key=lambda pair: pair[0])]

    if plan.aligned:
        mine = call(
            bind(stack_kernel), shape(half, bf16), [VMEM] * (len(pieces) + 1), name="stack"
        )(occ, *pieces)
        other = swap(mine, "vec", vecs, 1)
    else:
        me, vec = lax.axis_index("blk"), lax.axis_index("vec")
        mine = jnp.take(jnp.stack(pieces), me ^ jnp.arange(blks), axis=0)
        both = jnp.stack([mine, swap(mine, "vec", vecs, 1)])
        both = jnp.take(both, vec ^ jnp.arange(vecs), axis=0)
        both = both.transpose(2, 1, 0, 3).reshape(k, vecs, plan.length)
        mine, other = both[None, :, 0], both[None, :, 1]

    flops = 2 * k * plan.aux * plan.pairs // 2
    part = call(bind(fac_kernel, 0), shape((k, plan.aux), f32), [VMEM] * 2, flops, name="fac0")(
        mine, fac
    )
    part = call(bind(fac_kernel, 1), shape((k, plan.aux), f32), [VMEM] * 3, flops, name="fac1")(
        other, fac, part
    )
    other_part = swap(part, "grp", groups, 1)

    grid_flops = 2 * batches * points * virs * occs * k
    dens, sent = call(
        bind(dens_kernel),
        (shape((batches, k, points), f32), shape((batches, k, points), bf16)),
        [VMEM] * 4,
        grid_flops,
        [pltpu.VMEM((occs * k, virs), bf16)],
        name="dens",
    )(mine, other, vir, occ)
    other_dens = swap(sent, "grp", groups, 1)

    coulomb = call(
        bind(back_kernel), shape((vecs,) + half, f32), [VMEM] * 3, 2 * flops, name="back"
    )(part, other_part, fac)
    stay, sent = call(
        bind(grid_kernel),
        (shape(half, f32), shape(half, bf16)),
        [SMEM] + [VMEM] * 6,
        grid_flops,
        [pltpu.VMEM((occs * k, points), bf16), pltpu.VMEM((occs * k, virs), f32)],
        name="grid",
    )(live_points, dens, other_dens, occ, kernel, vir, coulomb)

    if plan.aligned:
        total = stay + swap(sent, "vec", vecs, 1).astype(f32)
    else:
        full = jnp.concatenate([stay[0], sent[0].astype(f32)], axis=1)
        full = full.reshape(k, blks, vecs, plan.rows).transpose(2, 1, 0, 3)
        full = jnp.take(full, me ^ jnp.arange(blks), axis=1)
        full = jnp.take(full, vec ^ jnp.arange(vecs), axis=0)
        total = full[0] + swap(full[1].astype(bf16), "vec", vecs, 1).astype(f32)

    for stride, radix in digits:
        total = total.reshape((-1, radix) + total.shape[1:])
        came = [
            swap(total[:, d].astype(bf16), "blk", blks, d * stride).astype(f32)
            for d in range(1, radix)
        ]
        total = sum(came, total[:, 0])
    result = energy_gap[None, :] * trial.T.astype(f32) + total[0]
    return result.astype(bf16).T


def solution(mesh):
    sizes = tuple(mesh.shape[a] for a in ("grp", "blk", "vec"))
    in_specs = (
        P(("grp", "blk", "vec"), None),
        P(("grp", "blk", "vec")),
        P("blk", None),
        P("blk", None, None),
        P("blk", None, None),
        P("blk", None),
        P("blk"),
    )
    out_specs = P(("grp", "blk", "vec"), None)

    def program(*args):
        return local(*args, sizes=sizes)

    return jax.shard_map(program, mesh=mesh, in_specs=in_specs, out_specs=out_specs, check_vma=False)
```

time: 208 us -> 49.5 us (0.24)
  waiting for transfers between devices: 76.8 us -> 17.2 us
  blocking collectives: 50.1 us -> 0 us
  matrix products: 48.4 us -> 0 us
  starting transfers between devices: 3.31 us -> 18.6 us
  between operations: 13.4 us -> 0.2 us
  Pallas kernels: 0 us -> 11.5 us
  local copies, waits for them, and re-layouts: 9.57 us -> 1.05 us
  other arithmetic: 4.78 us -> 0.78 us
    reduce_scatter x1 -> x0, waiting for transfers between devices: 75.5 us -> none  [local(): lax.psum_scatter(partial_sum, ('grp', 'blk'), scatter_dimension=0, tiled=...]
    dot_general x11 -> x0, matrix products: 48.4 us -> none  [the longest x1 28.3 us: coulomb_term(): lax.dot_general(coulomb_factors, factored, (((0,), (0,)), ((), ())), pref...]
    all_gather x1 -> x0, blocking collectives: 46.4 us -> none  [local(): full = lax.all_gather(pair_rows, ('grp', 'blk'), axis=0, tiled=True)]
    ppermute x0 -> x15, starting transfers between devices: none -> 18.6 us  [swap(): return lax.ppermute(x, axis, [(i, i ^ mask) for i in range(count)])]
    ppermute x0 -> x15, waiting for transfers between devices: none -> 17.2 us  [swap(): return lax.ppermute(x, axis, [(i, i ^ mask) for i in range(count)])]
    pallas_call x0 -> x7, Pallas kernels: none -> 11.5 us  [the longest x1 3.73 us: local(): call(bind(load_kernel), (shape((vecs, plan.aux, plan.count * plan.length)...]
    slice x3 -> x0, local copies, waits for them, and re-layouts: 3.78 us -> none  [the longest x1 3.76 us: grid_term(): vir_values[first:last]]
    all_to_all x1 -> x0, blocking collectives: 3.76 us -> none  [local(): lax.all_to_all(summed, 'vec', split_axis=0, concat_axis=1, tiled=True)]
  transfers between devices with their start and end apart: 2 -> 15, of which waited for: 2 -> 8; matrix products, arithmetic and copies ran while one was open for 0% -> 0% of each run, Pallas kernels for 0% -> 13%
where the time goes in v2:
time: 49.5 us; the launch traced here: 49.3 us
  starting transfers between devices  18.6 us (38%)
  waiting for transfers between devices  17.2 us (35%)
  Pallas kernels  11.5 us (23%)
  local copies, waits for them, and re-layouts  1.05 us (2%)
  other arithmetic  0.78 us (2%)
    ppermute x15, starting transfers between devices, swap(): return lax.ppermute(x, axis, [(i, i ^ mask) for i in range(count)])  18.6 us
    ppermute x15, waiting for transfers between devices, swap(): return lax.ppermute(x, axis, [(i, i ^ mask) for i in range(count)])  17.2 us
    pallas_call x1, Pallas kernels, local(): call(bind(load_kernel), (shape((vecs, plan.aux, plan.count * plan.length)...  3.73 us
    pallas_call x1, Pallas kernels, local(): call(bind(grid_kernel), (shape(half, f32), shape(half, bf16)), [SMEM] + [...  2.62 us
    pallas_call x1, Pallas kernels, local(): call(bind(dens_kernel), (shape((batches, k, points), f32), shape((batches...  2.44 us
    unnamed x10, local copies, waits for them, and re-layouts  1.02 us
    pallas_call x1, Pallas kernels, local(): call(bind(back_kernel), shape((vecs,) + half, f32), [VMEM] * 3, 2 * flops...  1.01 us
  transfers between devices with their start and end apart: 15, of which 8 were waited for; matrix products, arithmetic and copies ran while one was open for 0% of the time, Pallas kernels for 13%

profile of v2, /device:TPU:0, one launch (start us, length us, event | category | flops | bytes accessed | tf_op | source)
XLA Modules:
  0.0 49.3 jit_solution(10300656962881975422)
XLA Ops:
  0.0 5.1 %collective-permute-start.5 = (bf16[32,640]{1,0:T(8,128)(2,1)}, bf16[32,640]{1,0:T(8,128)(2,1)S(1)}, u32[]{:S(2)}, u32[]{:S(2)}) collective-permute-start(bf16[32,640]{1,0:T(8,128)(2,1)} %bitcast.47), channel_id=1, source_target_pairs={{0,12},{2,14},{4,8},{6,10},{8,4},{10,6},{12,0},{14,2},{1,13},{3,15... | collective-permute-start | bytes 122888 | tf_op jit(solution)/shard_map/ppermute | solution.py:29
  5.1 0.0 collective-permute-start.3
  5.1 0.6 %collective-permute-start.1 = (bf16[32,640]{1,0:T(8,128)(2,1)}, bf16[32,640]{1,0:T(8,128)(2,1)S(1)}, u32[]{:S(2)}, u32[]{:S(2)}) collective-permute-start(bf16[32,640]{1,0:T(8,128)(2,1)} %bitcast.49), channel_id=1, source_target_pairs={{0,4},{2,6},{4,0},{6,2},{8,12},{10,14},{12,8},{14,10},{1,5},{3,7},... | collective-permute-start | bytes 122888 | tf_op jit(solution)/shard_map/ppermute | solution.py:29
  5.6 1.7 %collective-permute-start = (bf16[32,640]{1,0:T(8,128)(2,1)}, bf16[32,640]{1,0:T(8,128)(2,1)S(1)}, u32[]{:S(2)}, u32[]{:S(2)}) collective-permute-start(bf16[32,640]{1,0:T(8,128)(2,1)} %bitcast.50), channel_id=1, source_target_pairs={{0,2},{2,0},{4,6},{6,4},{8,10},{10,8},{12,14},{14,12},{1,3},{3,1},... | collective-permute-start | bytes 122888 | tf_op jit(solution)/shard_map/ppermute | solution.py:29
  7.4 0.0 collective-permute-done.5.refs_7_
  7.4 1.8 %collective-permute-start.6 = (bf16[32,640]{1,0:T(8,128)(2,1)S(1)}, bf16[32,640]{1,0:T(8,128)(2,1)S(1)}, u32[]{:S(2)}, u32[]{:S(2)}) collective-permute-start(bf16[32,640]{1,0:T(8,128)(2,1)S(1)} %collective-permute-done.5.refs_7_), channel_id=1, source_target_pairs={{0,2},{2,0},{4,6},{6,4},{8,10},{10,8},{12,14},{14,12},{1,3},{3,1},... | collective-permute-start | bytes 122888 | tf_op jit(solution)/shard_map/ppermute | solution.py:29
  9.2 1.0 %collective-permute-done.3.refs_5_ = bf16[32,640]{1,0:T(8,128)(2,1)S(1)} collective-permute-done((bf16[32,640]{1,0:T(8,128)(2,1)}, bf16[32,640]{1,0:T(8,128)(2,1)S(1)}, u32[]{:S(2)}, u32[]{:S(2)}) %collective-permute-start.3) | collective-permute-done | bytes 40992 | tf_op jit(solution)/shard_map/ppermute | solution.py:29
  10.2 1.5 %collective-permute-start.4 = (bf16[32,640]{1,0:T(8,128)(2,1)S(1)}, bf16[32,640]{1,0:T(8,128)(2,1)S(1)}, u32[]{:S(2)}, u32[]{:S(2)}) collective-permute-start(bf16[32,640]{1,0:T(8,128)(2,1)S(1)} %collective-permute-done.3.refs_5_), channel_id=1, source_target_pairs={{0,2},{2,0},{4,6},{6,4},{8,10},{10,8},{12,14},{14,12},{1,3},{3,1},... | collective-permute-start | bytes 122888 | tf_op jit(solution)/shard_map/ppermute | solution.py:29
  11.7 0.0 collective-permute-done.1.refs_3_
  11.7 0.5 %collective-permute-start.2 = (bf16[32,640]{1,0:T(8,128)(2,1)S(1)}, bf16[32,640]{1,0:T(8,128)(2,1)S(1)}, u32[]{:S(2)}, u32[]{:S(2)}) collective-permute-start(bf16[32,640]{1,0:T(8,128)(2,1)S(1)} %collective-permute-done.1.refs_3_), channel_id=1, source_target_pairs={{0,2},{2,0},{4,6},{6,4},{8,10},{10,8},{12,14},{14,12},{1,3},{3,1},... | collective-permute-start | bytes 122888 | tf_op jit(solution)/shard_map/ppermute | solution.py:29
  12.2 0.0 copy-start
  12.2 1.0 %copy-done = bf16[10,40,512]{2,1,0:T(8,128)(2,1)S(1)} copy-done((bf16[10,40,512]{2,1,0:T(8,128)(2,1)S(1)}, bf16[10,40,512]{2,1,0:T(8,128)(2,1)}, u32[]{:S(2)}) %copy-start) | copy-done | bytes 409624
  13.2 0.0 copy-start.1
  13.2 3.7 %load.1 = (bf16[2,256,5120]{2,1,0:T(8,128)(2,1)S(1)}, bf16[5,512,512]{2,1,0:T(8,128)(2,1)S(1)}, f32[5,20,512]{2,1,0:T(8,128)S(1)}) custom-call(bf16[512,20480]{1,0:T(8,128)(2,1)} %refs_0_.2, bf16[10,512,512]{2,1,0:T(8,128)(2,1)} %refs_1_.1, bf16[10,40,512]{2,1,0:T(8,128)(2,1)S(1)} %copy-done), custom_call_target="tpu_custom_call" | custom-call | flops 1000000000 | tf_op jit(solution)/shard_map/load/pallas_call | solution.py:188
  17.0 0.0 collective-permute-done.refs_2_
  17.0 0.0 collective-permute-done.6.refs_8_
  17.0 0.0 collective-permute-done.4.refs_6_
  17.0 0.0 collective-permute-done.2.refs_4_
  17.0 0.0 copy-done.1
  17.1 0.1 collective-permute-start.7
  17.1 1.6 %collective-permute-done.7.refs_1_.refs_0_ = bf16[8,32,640]{2,1,0:T(8,128)(2,1)S(1)} collective-permute-done((bf16[8,32,640]{2,1,0:T(8,128)(2,1)S(1)}, bf16[8,32,640]{2,1,0:T(8,128)(2,1)S(1)}, u32[]{:S(2)}, u32[]{:S(2)}) %collective-permute-start.7) | collective-permute-done | bytes 327712 | tf_op jit(solution)/shard_map/ppermute | solution.py:29
  18.8 2.4 %dens.1 = (f32[5,32,512]{2,1,0:T(8,128)S(1)}, bf16[5,32,512]{2,1,0:T(8,128)(2,1)S(1)}) custom-call(bf16[8,32,640]{2,1,0:T(8,128)(2,1)S(1)} %stack.1.refs_0_, bf16[8,32,640]{2,1,0:T(8,128)(2,1)S(1)} %collective-permute-done.7.refs_1_.refs_0_, bf16[5,512,512]{2,1,0:T(8,128)(2,1)S(1)} %get-tuple-element.13.refs_2_.refs_5_, ...), custom_call_target="tpu_custom_call" | custom-call | flops 1677721600 | tf_op jit(solution)/shard_map/dens/pallas_call | solution.py:239
  21.2 1.6 %collective-permute-start.8 = (bf16[5,32,512]{2,1,0:T(8,128)(2,1)S(1)}, bf16[5,32,512]{2,1,0:T(8,128)(2,1)S(1)}, u32[]{:S(2)}, u32[]{:S(2)}) collective-permute-start(bf16[5,32,512]{2,1,0:T(8,128)(2,1)S(1)} %get-tuple-element.15), channel_id=1, source_target_pairs={{0,16},{16,0},{1,17},{17,1},{2,18},{18,2},{3,19},{19,3},{4,20},{20... | collective-permute-start | bytes 491528 | tf_op jit(solution)/shard_map/ppermute | solution.py:29
  22.8 0.8 %fac0.1.refs_2_ = f32[32,256]{1,0:T(8,128)S(1)} custom-call(bf16[8,32,640]{2,1,0:T(8,128)(2,1)S(1)} %stack.1.refs_0_, bf16[2,256,5120]{2,1,0:T(8,128)(2,1)S(1)} %get-tuple-element.16.refs_1_.refs_2_), custom_call_target="tpu_custom_call" | custom-call | flops 83886080 | tf_op jit(solution)/shard_map/fac0/pallas_call | solution.py:230
  23.6 0.0 copy-start.2
  23.6 0.0 copy-start.3
  23.6 0.8 %fac1.1.refs_0_ = f32[32,256]{1,0:T(8,128)S(1)} custom-call(bf16[8,32,640]{2,1,0:T(8,128)(2,1)S(1)} %collective-permute-done.7.refs_1_.refs_0_, bf16[2,256,5120]{2,1,0:T(8,128)(2,1)S(1)} %get-tuple-element.16.refs_1_.refs_2_, f32[32,256]{1,0:T(8,128)S(1)} %fac0.1.refs_2_), custom_call_target="tpu_custom_call" | custom-call | flops 83886080 | tf_op jit(solution)/shard_map/fac1/pallas_call | solution.py:233
  24.5 0.6 %collective-permute-start.9 = (f32[32,256]{1,0:T(8,128)S(1)}, f32[32,256]{1,0:T(8,128)S(1)}, u32[]{:S(2)}, u32[]{:S(2)}) collective-permute-start(f32[32,256]{1,0:T(8,128)S(1)} %fac1.1.refs_0_), channel_id=1, source_target_pairs={{0,16},{16,0},{1,17},{17,1},{2,18},{18,2},{3,19},{19,3},{4,20},{20... | collective-permute-start | bytes 98312 | tf_op jit(solution)/shard_map/ppermute | solution.py:29
  25.1 3.4 %collective-permute-done.9.refs_1_ = f32[32,256]{1,0:T(8,128)S(1)} collective-permute-done((f32[32,256]{1,0:T(8,128)S(1)}, f32[32,256]{1,0:T(8,128)S(1)}, u32[]{:S(2)}, u32[]{:S(2)}) %collective-permute-start.9) | collective-permute-done | bytes 32800 | tf_op jit(solution)/shard_map/ppermute | solution.py:29
  28.4 1.0 %back.1.refs_6_ = f32[2,8,32,640]{3,2,1,0:T(8,128)S(1)} custom-call(f32[32,256]{1,0:T(8,128)S(1)} %fac1.1.refs_0_, f32[32,256]{1,0:T(8,128)S(1)} %collective-permute-done.9.refs_1_, bf16[2,256,5120]{2,1,0:T(8,128)(2,1)S(1)} %get-tuple-element.16.refs_1_.refs_2_), custom_call_target="tpu_custom_call" | custom-call | flops 167772160 | tf_op jit(solution)/shard_map/back/pallas_call | solution.py:249
  29.4 0.0 copy-start.4
  29.5 0.0 collective-permute-done.8.refs_2_
  29.5 0.0 copy-done.2
  29.5 0.0 copy-done.3
  29.5 2.6 %grid.1 = (f32[8,32,640]{2,1,0:T(8,128)S(1)}, bf16[8,32,640]{2,1,0:T(8,128)(2,1)S(1)}) custom-call(s32[10]{0:T(128)S(1)} %copy-done.3, f32[5,32,512]{2,1,0:T(8,128)S(1)} %get-tuple-element.14.refs_1_, bf16[5,32,512]{2,1,0:T(8,128)(2,1)S(1)} %collective-permute-done.8.refs_2_, f32[5,20,512]{2,1,0:T(8,128)S(1)} %get-tuple-element.12.refs_0_.refs_3_, ...), custom_call_target="tpu_custom_call" | custom-call | flops 1677721600 | tf_op jit(solution)/shard_map/grid/pallas_call | solution.py:252
  32.1 0.1 collective-permute-start.10
  32.2 1.6 %collective-permute-done.10 = bf16[8,32,640]{2,1,0:T(8,128)(2,1)S(1)} collective-permute-done((bf16[8,32,640]{2,1,0:T(8,128)(2,1)S(1)}, bf16[8,32,640]{2,1,0:T(8,128)(2,1)S(1)}, u32[]{:S(2)}, u32[]{:S(2)}) %collective-permute-start.10) | collective-permute-done | bytes 327712 | tf_op jit(solution)/shard_map/ppermute | solution.py:29
  33.8 0.1 convert_add_fusion
  33.9 1.6 %collective-permute-start.11 = (bf16[4,32,640]{2,1,0:T(8,128)(2,1)S(1)}, bf16[4,32,640]{2,1,0:T(8,128)(2,1)S(1)}, u32[]{:S(2)}, u32[]{:S(2)}) collective-permute-start(bf16[4,32,640]{2,1,0:T(8,128)(2,1)S(1)} %fusion.2), channel_id=1, source_target_pairs={{0,2},{2,0},{4,6},{6,4},{8,10},{10,8},{12,14},{14,12},{1,3},{3,1},... | collective-permute-start | bytes 491528 | tf_op jit(solution)/shard_map/ppermute | solution.py:29
  35.5 4.7 %collective-permute-done.11 = bf16[4,32,640]{2,1,0:T(8,128)(2,1)S(1)} collective-permute-done((bf16[4,32,640]{2,1,0:T(8,128)(2,1)S(1)}, bf16[4,32,640]{2,1,0:T(8,128)(2,1)S(1)}, u32[]{:S(2)}, u32[]{:S(2)}) %collective-permute-start.11) | collective-permute-done | bytes 163872 | tf_op jit(solution)/shard_map/ppermute | solution.py:29
  40.3 0.1 collective-permute-start.12
  40.4 3.0 %collective-permute-start.14 = (bf16[1,32,640]{2,1,0:T(8,128)(2,1)S(1)}, bf16[1,32,640]{2,1,0:T(8,128)(2,1)S(1)}, u32[]{:S(2)}, u32[]{:S(2)}) collective-permute-start(bf16[1,32,640]{2,1,0:T(8,128)(2,1)S(1)} %get-tuple-element.22), channel_id=1, source_target_pairs={{0,12},{2,14},{4,8},{6,10},{8,4},{10,6},{12,0},{14,2},{1,13},{3,15... | collective-permute-start | bytes 122888 | tf_op jit(solution)/shard_map/ppermute | solution.py:29
  43.3 0.5 %collective-permute-start.13 = (bf16[1,32,640]{2,1,0:T(8,128)(2,1)S(1)}, bf16[1,32,640]{2,1,0:T(8,128)(2,1)S(1)}, u32[]{:S(2)}, u32[]{:S(2)}) collective-permute-start(bf16[1,32,640]{2,1,0:T(8,128)(2,1)S(1)} %get-tuple-element.23), channel_id=1, source_target_pairs={{0,8},{2,10},{4,12},{6,14},{8,0},{10,2},{12,4},{14,6},{1,9},{3,11}... | collective-permute-start | bytes 122888 | tf_op jit(solution)/shard_map/ppermute | solution.py:29
  43.8 1.0 %collective-permute-done.12 = bf16[1,32,640]{2,1,0:T(8,128)(2,1)S(1)} collective-permute-done((bf16[1,32,640]{2,1,0:T(8,128)(2,1)S(1)}, bf16[1,32,640]{2,1,0:T(8,128)(2,1)S(1)}, u32[]{:S(2)}, u32[]{:S(2)}) %collective-permute-start.12) | collective-permute-done | bytes 40992 | tf_op jit(solution)/shard_map/ppermute | solution.py:29
  44.8 1.9 %collective-permute-done.14 = bf16[1,32,640]{2,1,0:T(8,128)(2,1)S(1)} collective-permute-done((bf16[1,32,640]{2,1,0:T(8,128)(2,1)S(1)}, bf16[1,32,640]{2,1,0:T(8,128)(2,1)S(1)}, u32[]{:S(2)}, u32[]{:S(2)}) %collective-permute-start.14) | collective-permute-done | bytes 40992 | tf_op jit(solution)/shard_map/ppermute | solution.py:29
  46.7 2.0 %collective-permute-done.13 = bf16[1,32,640]{2,1,0:T(8,128)(2,1)S(1)} collective-permute-done((bf16[1,32,640]{2,1,0:T(8,128)(2,1)S(1)}, bf16[1,32,640]{2,1,0:T(8,128)(2,1)S(1)}, u32[]{:S(2)}, u32[]{:S(2)}) %collective-permute-start.13) | collective-permute-done | bytes 40992 | tf_op jit(solution)/shard_map/ppermute | solution.py:29
  48.7 0.0 copy-done.4
  48.7 0.7 %fusion.9 = bf16[640,32]{0,1:T(8,128)(2,1)} fusion(bf16[1,32,640]{2,1,0:T(8,128)(2,1)S(1)} %collective-permute-done.14, bf16[1,32,640]{2,1,0:T(8,128)(2,1)S(1)} %collective-permute-done.13, bf16[1,32,640]{2,1,0:T(8,128)(2,1)S(1)} %collective-permute-done.12, f32[1,4,32,640]{3,2,1,0:T(8,128)S(1)} %get-tuple-element.20, f32[640]{0:T(1024)S(1)} %copy-done.4, ...), kind=kLoop, calls=%fused_computation.13 | loop fusion | flops 204800 | bytes 289280 | tf_op jit(solution)/shard_map/transpose | solution.py:278
  (4 shorter events, 0.1 us)
Async XLA Ops:
  0.0 7.4 %collective-permute-start.5 = (bf16[32,640]{1,0:T(8,128)(2,1)}, bf16[32,640]{1,0:T(8,128)(2,1)S(1)}, u32[]{:S(2)}, u32[]{:S(2)}) collective-permute-start(bf16[32,640]{1,0:T(8,128)(2,1)} %bitcast.47), channel_id=1, source_target_pairs={{0,12},{2,14},{4,8},{6,10},{8,4},{10,6},{12,0},{14,2},{1,13},{3,15... | collective-permute-start | bytes 122888 | tf_op jit(solution)/shard_map/ppermute | solution.py:29
  5.1 5.1 %collective-permute-start.3 = (bf16[32,640]{1,0:T(8,128)(2,1)}, bf16[32,640]{1,0:T(8,128)(2,1)S(1)}, u32[]{:S(2)}, u32[]{:S(2)}) collective-permute-start(bf16[32,640]{1,0:T(8,128)(2,1)} %bitcast.48), channel_id=1, source_target_pairs={{0,8},{2,10},{4,12},{6,14},{8,0},{10,2},{12,4},{14,6},{1,9},{3,11}... | collective-permute-start | bytes 122888 | tf_op jit(solution)/shard_map/ppermute | solution.py:29
  5.1 6.6 %collective-permute-start.1 = (bf16[32,640]{1,0:T(8,128)(2,1)}, bf16[32,640]{1,0:T(8,128)(2,1)S(1)}, u32[]{:S(2)}, u32[]{:S(2)}) collective-permute-start(bf16[32,640]{1,0:T(8,128)(2,1)} %bitcast.49), channel_id=1, source_target_pairs={{0,4},{2,6},{4,0},{6,2},{8,12},{10,14},{12,8},{14,10},{1,5},{3,7},... | collective-permute-start | bytes 122888 | tf_op jit(solution)/shard_map/ppermute | solution.py:29
  5.6 11.3 %collective-permute-start = (bf16[32,640]{1,0:T(8,128)(2,1)}, bf16[32,640]{1,0:T(8,128)(2,1)S(1)}, u32[]{:S(2)}, u32[]{:S(2)}) collective-permute-start(bf16[32,640]{1,0:T(8,128)(2,1)} %bitcast.50), channel_id=1, source_target_pairs={{0,2},{2,0},{4,6},{6,4},{8,10},{10,8},{12,14},{14,12},{1,3},{3,1},... | collective-permute-start | bytes 122888 | tf_op jit(solution)/shard_map/ppermute | solution.py:29
  7.4 9.6 %collective-permute-start.6 = (bf16[32,640]{1,0:T(8,128)(2,1)S(1)}, bf16[32,640]{1,0:T(8,128)(2,1)S(1)}, u32[]{:S(2)}, u32[]{:S(2)}) collective-permute-start(bf16[32,640]{1,0:T(8,128)(2,1)S(1)} %collective-permute-done.5.refs_7_), channel_id=1, source_target_pairs={{0,2},{2,0},{4,6},{6,4},{8,10},{10,8},{12,14},{14,12},{1,3},{3,1},... | collective-permute-start | bytes 122888 | tf_op jit(solution)/shard_map/ppermute | solution.py:29
  10.2 6.8 %collective-permute-start.4 = (bf16[32,640]{1,0:T(8,128)(2,1)S(1)}, bf16[32,640]{1,0:T(8,128)(2,1)S(1)}, u32[]{:S(2)}, u32[]{:S(2)}) collective-permute-start(bf16[32,640]{1,0:T(8,128)(2,1)S(1)} %collective-permute-done.3.refs_5_), channel_id=1, source_target_pairs={{0,2},{2,0},{4,6},{6,4},{8,10},{10,8},{12,14},{14,12},{1,3},{3,1},... | collective-permute-start | bytes 122888 | tf_op jit(solution)/shard_map/ppermute | solution.py:29
  11.7 5.3 %collective-permute-start.2 = (bf16[32,640]{1,0:T(8,128)(2,1)S(1)}, bf16[32,640]{1,0:T(8,128)(2,1)S(1)}, u32[]{:S(2)}, u32[]{:S(2)}) collective-permute-start(bf16[32,640]{1,0:T(8,128)(2,1)S(1)} %collective-permute-done.1.refs_3_), channel_id=1, source_target_pairs={{0,2},{2,0},{4,6},{6,4},{8,10},{10,8},{12,14},{14,12},{1,3},{3,1},... | collective-permute-start | bytes 122888 | tf_op jit(solution)/shard_map/ppermute | solution.py:29
  12.2 1.0 %copy-start = (bf16[10,40,512]{2,1,0:T(8,128)(2,1)S(1)}, bf16[10,40,512]{2,1,0:T(8,128)(2,1)}, u32[]{:S(2)}) copy-start(bf16[10,40,512]{2,1,0:T(8,128)(2,1)} %refs_2_.1) | copy-start | bytes 1228804
  13.2 3.8 %copy-start.1 = (bf16[640,32]{0,1:T(8,128)(2,1)S(1)}, bf16[640,32]{0,1:T(8,128)(2,1)}, u32[]{:S(2)}) copy-start(bf16[640,32]{0,1:T(8,128)(2,1)} %param.7) | copy-start | bytes 122884
  17.1 1.7 %collective-permute-start.7 = (bf16[8,32,640]{2,1,0:T(8,128)(2,1)S(1)}, bf16[8,32,640]{2,1,0:T(8,128)(2,1)S(1)}, u32[]{:S(2)}, u32[]{:S(2)}) collective-permute-start(bf16[8,32,640]{2,1,0:T(8,128)(2,1)S(1)} %stack.1.refs_0_), channel_id=1, source_target_pairs={{0,1},{1,0},{2,3},{3,2},{4,5},{5,4},{6,7},{7,6},{8,9},{9,8},{10,11... | collective-permute-start | bytes 983048 | tf_op jit(solution)/shard_map/ppermute | solution.py:29
  21.2 8.3 %collective-permute-start.8 = (bf16[5,32,512]{2,1,0:T(8,128)(2,1)S(1)}, bf16[5,32,512]{2,1,0:T(8,128)(2,1)S(1)}, u32[]{:S(2)}, u32[]{:S(2)}) collective-permute-start(bf16[5,32,512]{2,1,0:T(8,128)(2,1)S(1)} %get-tuple-element.15), channel_id=1, source_target_pairs={{0,16},{16,0},{1,17},{17,1},{2,18},{18,2},{3,19},{19,3},{4,20},{20... | collective-permute-start | bytes 491528 | tf_op jit(solution)/shard_map/ppermute | solution.py:29
  23.6 5.9 %copy-start.2 = (f32[10,512]{1,0:T(8,128)S(1)}, f32[10,512]{1,0:T(8,128)}, u32[]{:S(2)}) copy-start(f32[10,512]{1,0:T(8,128)} %refs_4_.1) | copy-start | bytes 61444
  23.6 5.9 %copy-start.3 = (s32[10]{0:T(128)S(1)}, s32[10]{0:T(128)}, u32[]{:S(2)}) copy-start(s32[10]{0:T(128)} %refs_0_.3) | copy-start | bytes 124
  24.5 4.0 %collective-permute-start.9 = (f32[32,256]{1,0:T(8,128)S(1)}, f32[32,256]{1,0:T(8,128)S(1)}, u32[]{:S(2)}, u32[]{:S(2)}) collective-permute-start(f32[32,256]{1,0:T(8,128)S(1)} %fac1.1.refs_0_), channel_id=1, source_target_pairs={{0,16},{16,0},{1,17},{17,1},{2,18},{18,2},{3,19},{19,3},{4,20},{20... | collective-permute-start | bytes 98312 | tf_op jit(solution)/shard_map/ppermute | solution.py:29
  29.4 19.2 %copy-start.4 = (f32[640]{0:T(1024)S(1)}, f32[640]{0:T(1024)}, u32[]{:S(2)}) copy-start(f32[640]{0:T(1024)} %param.8) | copy-start | bytes 7684
  32.1 1.7 %collective-permute-start.10 = (bf16[8,32,640]{2,1,0:T(8,128)(2,1)S(1)}, bf16[8,32,640]{2,1,0:T(8,128)(2,1)S(1)}, u32[]{:S(2)}, u32[]{:S(2)}) collective-permute-start(bf16[8,32,640]{2,1,0:T(8,128)(2,1)S(1)} %get-tuple-element.18), channel_id=1, source_target_pairs={{0,1},{1,0},{2,3},{3,2},{4,5},{5,4},{6,7},{7,6},{8,9},{9,8},{10,11... | collective-permute-start | bytes 983048 | tf_op jit(solution)/shard_map/ppermute | solution.py:29
  33.9 6.3 %collective-permute-start.11 = (bf16[4,32,640]{2,1,0:T(8,128)(2,1)S(1)}, bf16[4,32,640]{2,1,0:T(8,128)(2,1)S(1)}, u32[]{:S(2)}, u32[]{:S(2)}) collective-permute-start(bf16[4,32,640]{2,1,0:T(8,128)(2,1)S(1)} %fusion.2), channel_id=1, source_target_pairs={{0,2},{2,0},{4,6},{6,4},{8,10},{10,8},{12,14},{14,12},{1,3},{3,1},... | collective-permute-start | bytes 491528 | tf_op jit(solution)/shard_map/ppermute | solution.py:29
  40.3 4.5 %collective-permute-start.12 = (bf16[1,32,640]{2,1,0:T(8,128)(2,1)S(1)}, bf16[1,32,640]{2,1,0:T(8,128)(2,1)S(1)}, u32[]{:S(2)}, u32[]{:S(2)}) collective-permute-start(bf16[1,32,640]{2,1,0:T(8,128)(2,1)S(1)} %get-tuple-element.21), channel_id=1, source_target_pairs={{0,4},{2,6},{4,0},{6,2},{8,12},{10,14},{12,8},{14,10},{1,5},{3,7},... | collective-permute-start | bytes 122888 | tf_op jit(solution)/shard_map/ppermute | solution.py:29
  40.4 6.3 %collective-permute-start.14 = (bf16[1,32,640]{2,1,0:T(8,128)(2,1)S(1)}, bf16[1,32,640]{2,1,0:T(8,128)(2,1)S(1)}, u32[]{:S(2)}, u32[]{:S(2)}) collective-permute-start(bf16[1,32,640]{2,1,0:T(8,128)(2,1)S(1)} %get-tuple-element.22), channel_id=1, source_target_pairs={{0,12},{2,14},{4,8},{6,10},{8,4},{10,6},{12,0},{14,2},{1,13},{3,15... | collective-permute-start | bytes 122888 | tf_op jit(solution)/shard_map/ppermute | solution.py:29
  43.3 5.3 %collective-permute-start.13 = (bf16[1,32,640]{2,1,0:T(8,128)(2,1)S(1)}, bf16[1,32,640]{2,1,0:T(8,128)(2,1)S(1)}, u32[]{:S(2)}, u32[]{:S(2)}) collective-permute-start(bf16[1,32,640]{2,1,0:T(8,128)(2,1)S(1)} %get-tuple-element.23), channel_id=1, source_target_pairs={{0,8},{2,10},{4,12},{6,14},{8,0},{10,2},{12,4},{14,6},{1,9},{3,11}... | collective-permute-start | bytes 122888 | tf_op jit(solution)/shard_map/ppermute | solution.py:29

commit v3 on v2

v3 whole, which is shorter than its diff:
```python
import jax
import jax.numpy as jnp
from jax import lax
from jax.experimental import pallas as pl
from jax.experimental.pallas import tpu as pltpu
from jax.sharding import PartitionSpec as P

LANES = 128
HEAD = 10**10
NT = (((1,), (1,)), ((), ()))
NN = (((1,), (0,)), ((), ()))
VMEM = pl.BlockSpec(memory_space=pltpu.VMEM)
SMEM = pl.BlockSpec(memory_space=pltpu.SMEM)
HBM = pl.BlockSpec(memory_space=pltpu.HBM)


def digits_of(count):
    digits, stride = [], 1
    bits = count.bit_length() - 1
    if bits % 2:
        digits.append((1, 2))
        stride = 2
    while stride < count:
        digits.append((stride, 4))
        stride *= 4
    return digits


def swap(x, axis, count, mask):
    return lax.ppermute(x, axis, [(i, i ^ mask) for i in range(count)])


def call(body, out_shape, in_specs, flops=0, scratch=(), limit=24, name=None):
    return pl.pallas_call(
        body,
        out_shape=out_shape,
        in_specs=in_specs,
        out_specs=jax.tree.map(lambda _: VMEM, out_shape),
        scratch_shapes=list(scratch),
        compiler_params=pltpu.CompilerParams(vmem_limit_bytes=limit * 2**20),
        name=name,
        cost_estimate=pl.CostEstimate(flops=flops, bytes_accessed=0, transcendentals=0),
    )


def shape(dims, dtype):
    return jax.ShapeDtypeStruct(dims, dtype)


class Plan:
    def __init__(self, sizes, trial, coulomb_factors, occ_values, vir_values):
        self.groups, self.blks, self.vecs = sizes
        self.rows, self.k = trial.shape
        self.aux = coulomb_factors.shape[0] // self.vecs
        self.pairs = coulomb_factors.shape[1] // self.groups
        self.batches = occ_values.shape[0] // self.vecs
        self.occ_all, self.points = occ_values.shape[1:]
        self.occs = self.occ_all // self.groups
        self.virs = vir_values.shape[2]
        self.aligned = self.rows % LANES == 0
        self.count = self.blks if self.aligned else 1
        self.length = self.rows if self.aligned else self.pairs // self.vecs
        self.per = self.length // LANES

    def owner(self, m):
        return lax.axis_index("blk") ^ m if self.aligned else 0

    def part(self, h):
        return lax.axis_index("vec") ^ h if self.aligned else h

    def block(self, h, m, j):
        return (self.owner(m) * self.vecs + self.part(h)) * self.per + j

    def place(self, h, m, j):
        at = self.block(h, m, j)
        tiles = self.virs // LANES
        return (
            pl.ds(pl.multiple_of((at // tiles) * self.k, self.k), self.k),
            pl.ds(pl.multiple_of((at % tiles) * LANES, LANES), LANES),
        )


def head_kernel(plan, given, out):
    out[...] = given[...]


def flat_of(ref, count):
    return jnp.concatenate([ref[m] for m in range(count)], axis=1)


def stack_kernel(plan, *refs):
    for m, piece in enumerate(refs[:-1]):
        refs[-1][m] = piece[...]


def occ_rows(plan, occ, b, occ32):
    occ32[...] = occ[lax.axis_index("vec") * plan.batches + b].astype(jnp.float32)
    base = lax.axis_index("grp") * plan.occs
    return lambda i: occ32[pl.ds(base + i, 1), :]


def dens_kernel(plan, mine, other, vir, occ, fac_hbm, dens, sent, fac, rows, occ32, fsem):
    k = plan.k
    grp, vec = lax.axis_index("grp"), lax.axis_index("vec")
    top = pl.multiple_of(vec * plan.aux, 8)
    copies = []
    for h in range(plan.vecs):
        for m in range(plan.count):
            at = pl.multiple_of(grp * plan.pairs + plan.block(h, m, 0) * LANES, LANES)
            copies.append(
                pltpu.make_async_copy(
                    fac_hbm.at[pl.ds(top, plan.aux), pl.ds(at, plan.length)],
                    fac.at[h, :, pl.ds(m * plan.length, plan.length)],
                    fsem.at[h, m],
                )
            )
    for copy in copies:
        copy.start()
    for h, half in enumerate((mine, other)):
        for m in range(plan.count):
            for j in range(plan.per):
                rows[plan.place(h, m, j)] = half[m, :, j * LANES : (j + 1) * LANES]
    for b in range(plan.batches):
        row = occ_rows(plan, occ, b, occ32.at[b])
        trans = lax.dot_general(
            rows[...], vir[vec * plan.batches + b], NT, preferred_element_type=jnp.float32
        )
        total = row(0) * trans[:k, :]
        for i in range(1, plan.occs):
            total = total + row(i) * trans[i * k : (i + 1) * k, :]
        dens[b] = total
        sent[b] = total.astype(sent.dtype)
    for copy in copies:
        copy.wait()


def fac_kernel(plan, mine, other, fac, out):
    value = 0.0
    for h, half in enumerate((mine, other)):
        value += lax.dot_general(
            flat_of(half, plan.count), fac[h], NT, preferred_element_type=jnp.float32
        )
    out[...] = value


def grid_kernel(plan, live, dens_a, dens_b, occ, weight, vir, acc, scaled, occ32):
    k = plan.k
    base = lax.axis_index("vec") * plan.batches
    slots = lax.broadcasted_iota(jnp.int32, (1, plan.points), 1)
    for b in range(plan.batches):
        row = occ_rows(plan, occ, b, occ32.at[b])
        density = dens_a[b] + dens_b[b].astype(jnp.float32)
        used = jnp.where(slots < live[base + b], weight[pl.ds(base + b, 1), :], 0.0)
        weighted = density * used
        for i in range(plan.occs):
            scaled[i * k : (i + 1) * k, :] = (row(i) * weighted).astype(jnp.bfloat16)
        value = lax.dot_general(
            scaled[...], vir[base + b], NN, preferred_element_type=jnp.float32
        )
        if b == 0:
            acc[...] = value
        else:
            acc[...] += value


def back_kernel(plan, part_a, part_b, fac, acc, stay, sent):
    both = (part_a[...] + part_b[...]).astype(jnp.bfloat16)
    for h, out in enumerate((stay, sent)):
        value = 2.0 * lax.dot_general(both, fac[h], NN, preferred_element_type=jnp.float32)
        for m in range(plan.count):
            for j in range(plan.per):
                at = m * plan.length + j * LANES
                total = value[:, at : at + LANES] + acc[plan.place(h, m, j)]
                out[m, :, j * LANES : (j + 1) * LANES] = total.astype(out.dtype)


def local(trial, energy_gap, coulomb_factors, occ_values, vir_values, kernel, live_points, sizes):
    plan = Plan(sizes, trial, coulomb_factors, occ_values, vir_values)
    groups, blks, vecs, k = plan.groups, plan.blks, plan.vecs, plan.k
    batches, points, virs, occs = plan.batches, plan.points, plan.virs, plan.occs
    digits = digits_of(blks)
    half = (plan.count, k, plan.length)
    bf16, f32 = jnp.bfloat16, jnp.float32

    def bind(body, *first):
        return lambda *refs: body(plan, *first, *refs)

    trial_cols = trial.T
    start = call(
        bind(head_kernel), shape(trial_cols.shape, bf16), [VMEM], flops=HEAD, name="head"
    )(trial_cols)
    pieces, masks = [start], [0]
    for stride, radix in reversed(digits):
        known = len(masks)
        for d in range(1, radix):
            for n in range(known):
                pieces.append(swap(pieces[n], "blk", blks, d * stride))
                masks.append(masks[n] ^ (d * stride))
    pieces = [p for _, p in sorted(zip(masks, pieces), key=lambda pair: pair[0])]

    if plan.aligned:
        mine = call(bind(stack_kernel), shape(half, bf16), [VMEM] * len(pieces), name="stack")(
            *pieces
        )
        other = swap(mine, "vec", vecs, 1)
    else:
        me, vec = lax.axis_index("blk"), lax.axis_index("vec")
        mine = jnp.take(jnp.stack(pieces), me ^ jnp.arange(blks), axis=0)
        both = jnp.stack([mine, swap(mine, "vec", vecs, 1)])
        both = jnp.take(both, vec ^ jnp.arange(vecs), axis=0)
        both = both.transpose(2, 1, 0, 3).reshape(k, vecs, plan.length)
        mine, other = both[None, :, 0], both[None, :, 1]

    flops = 2 * k * plan.aux * plan.pairs
    grid_flops = 2 * batches * points * virs * occs * k
    occ_scratch = pltpu.VMEM((batches, plan.occ_all, points), f32)
    dens, sent, fac = call(
        bind(dens_kernel),
        (
            shape((batches, k, points), f32),
            shape((batches, k, points), bf16),
            shape((vecs, plan.aux, plan.count * plan.length), bf16),
        ),
        [VMEM] * 4 + [HBM],
        grid_flops,
        [
            pltpu.VMEM((occs * k, virs), bf16),
            occ_scratch,
            pltpu.SemaphoreType.DMA((vecs, plan.count)),
        ],
        name="dens",
    )(mine, other, vir_values, occ_values, coulomb_factors)
    other_dens = swap(sent, "grp", groups, 1)

    part = call(bind(fac_kernel), shape((k, plan.aux), f32), [VMEM] * 3, flops, name="fac")(
        mine, other, fac
    )
    other_part = swap(part, "grp", groups, 1)

    acc = call(
        bind(grid_kernel),
        shape((occs * k, virs), f32),
        [SMEM] + [VMEM] * 5,
        grid_flops,
        [pltpu.VMEM((occs * k, points), bf16), occ_scratch],
        name="grid",
    )(live_points, dens, other_dens, occ_values, kernel, vir_values)
    stay, sent = call(
        bind(back_kernel), (shape(half, f32), shape(half, bf16)), [VMEM] * 4, flops, name="back"
    )(part, other_part, fac, acc)

    if plan.aligned:
        total = stay + swap(sent, "vec", vecs, 1).astype(f32)
    else:
        full = jnp.concatenate([stay[0], sent[0].astype(f32)], axis=1)
        full = full.reshape(k, blks, vecs, plan.rows).transpose(2, 1, 0, 3)
        full = jnp.take(full, me ^ jnp.arange(blks), axis=1)
        full = jnp.take(full, vec ^ jnp.arange(vecs), axis=0)
        total = full[0] + swap(full[1].astype(bf16), "vec", vecs, 1).astype(f32)

    for stride, radix in digits:
        total = total.reshape((-1, radix) + total.shape[1:])
        came = [
            swap(total[:, d].astype(bf16), "blk", blks, d * stride).astype(f32)
            for d in range(1, radix)
        ]
        total = sum(came, total[:, 0])
    result = energy_gap[None, :] * start.astype(f32) + total[0]
    return result.astype(bf16).T


def solution(mesh):
    sizes = tuple(mesh.shape[a] for a in ("grp", "blk", "vec"))
    in_specs = (
        P(("grp", "blk", "vec"), None),
        P(("grp", "blk", "vec")),
        P("blk", None),
        P("blk", None, None),
        P("blk", None, None),
        P("blk", None),
        P("blk"),
    )
    out_specs = P(("grp", "blk", "vec"), None)

    def program(*args):
        return local(*args, sizes=sizes)

    return jax.shard_map(program, mesh=mesh, in_specs=in_specs, out_specs=out_specs, check_vma=False)
```

time: 49.5 us -> 49.7 us (level)
  waiting for transfers between devices: 17.2 us -> 20.3 us
  Pallas kernels: 11.5 us -> 10.1 us
  starting transfers between devices: 18.6 us -> 17.5 us
    pallas_call x6 -> x5, Pallas kernels: 9.04 us -> 5.08 us  [the longest x1 2.4 us: local(): call(bind(grid_kernel), shape((occs * k, virs), f32), [SMEM] + [VMEM] * 5...]
    ppermute x15, waiting for transfers between devices: 17.2 us -> 20.3 us  [swap(): return lax.ppermute(x, axis, [(i, i ^ mask) for i in range(count)])]
    pallas_call x1, Pallas kernels: 2.44 us -> 5 us  [local(): call(bind(dens_kernel), (shape((batches, k, points), f32), shape((batches...]
    ppermute x15, starting transfers between devices: 18.6 us -> 17.5 us  [swap(): return lax.ppermute(x, axis, [(i, i ^ mask) for i in range(count)])]
    unnamed x10 -> x12, local copies, waits for them, and re-layouts: 1.02 us -> 0.8 us
  transfers between devices with their start and end apart: 15 -> 15, of which waited for: 8 -> 10; matrix products, arithmetic and copies ran while one was open for 0% -> 0% of each run, Pallas kernels for 13% -> 8%
where the time goes in v3:
time: 49.7 us; the launch traced here: 49.6 us
  waiting for transfers between devices  20.3 us (41%)
  starting transfers between devices  17.5 us (35%)
  Pallas kernels  10.1 us (20%)
  local copies, waits for them, and re-layouts  0.84 us (2%)
  other arithmetic  0.77 us (2%)
    ppermute x15, waiting for transfers between devices, swap(): return lax.ppermute(x, axis, [(i, i ^ mask) for i in range(count)])  20.3 us
    ppermute x15, starting transfers between devices, swap(): return lax.ppermute(x, axis, [(i, i ^ mask) for i in range(count)])  17.5 us
    pallas_call x1, Pallas kernels, local(): call(bind(dens_kernel), (shape((batches, k, points), f32), shape((batches...  5 us
    pallas_call x1, Pallas kernels, local(): call(bind(grid_kernel), shape((occs * k, virs), f32), [SMEM] + [VMEM] * 5...  2.4 us
    pallas_call x1, Pallas kernels, local(): call(bind(fac_kernel), shape((k, plan.aux), f32), [VMEM] * 3, flops, name...  1.62 us
    pallas_call x1, Pallas kernels, local(): call(bind(back_kernel), (shape(half, f32), shape(half, bf16)), [VMEM] * 4...  1.04 us
  transfers between devices with their start and end apart: 15, of which 10 were waited for; matrix products, arithmetic and copies ran while one was open for 0% of the time, Pallas kernels for 8%

profile of v3, /device:TPU:0, one launch (start us, length us, event | category | flops | bytes accessed | tf_op | source)
XLA Modules:
  0.0 49.6 jit_solution(302875222809386408)
XLA Ops:
  0.0 0.0 copy-start.4
  0.0 0.8 %copy-done.4 = bf16[640,32]{0,1:T(8,128)(2,1)S(1)} copy-done((bf16[640,32]{0,1:T(8,128)(2,1)S(1)}, bf16[640,32]{0,1:T(8,128)(2,1)}, u32[]{:S(2)}) %copy-start.4) | copy-done | bytes 40984
  0.8 0.0 copy-start
  0.8 0.0 copy-start.1
  0.8 5.1 %collective-permute-start.5 = (bf16[32,640]{1,0:T(8,128)(2,1)S(1)}, bf16[32,640]{1,0:T(8,128)(2,1)S(1)}, u32[]{:S(2)}, u32[]{:S(2)}) collective-permute-start(bf16[32,640]{1,0:T(8,128)(2,1)S(1)} %head.1.refs_0_), channel_id=1, source_target_pairs={{0,12},{2,14},{4,8},{6,10},{8,4},{10,6},{12,0},{14,2},{1,13},{3,15... | collective-permute-start | bytes 122888 | tf_op jit(solution)/shard_map/ppermute | solution.py:30
  5.9 0.0 collective-permute-start.3
  5.9 0.6 %collective-permute-start.1 = (bf16[32,640]{1,0:T(8,128)(2,1)S(1)}, bf16[32,640]{1,0:T(8,128)(2,1)S(1)}, u32[]{:S(2)}, u32[]{:S(2)}) collective-permute-start(bf16[32,640]{1,0:T(8,128)(2,1)S(1)} %head.1.refs_0_), channel_id=1, source_target_pairs={{0,4},{2,6},{4,0},{6,2},{8,12},{10,14},{12,8},{14,10},{1,5},{3,7},... | collective-permute-start | bytes 122888 | tf_op jit(solution)/shard_map/ppermute | solution.py:30
  6.6 1.7 %collective-permute-start = (bf16[32,640]{1,0:T(8,128)(2,1)S(1)}, bf16[32,640]{1,0:T(8,128)(2,1)S(1)}, u32[]{:S(2)}, u32[]{:S(2)}) collective-permute-start(bf16[32,640]{1,0:T(8,128)(2,1)S(1)} %head.1.refs_0_), channel_id=1, source_target_pairs={{0,2},{2,0},{4,6},{6,4},{8,10},{10,8},{12,14},{14,12},{1,3},{3,1},... | collective-permute-start | bytes 122888 | tf_op jit(solution)/shard_map/ppermute | solution.py:30
  8.2 0.0 collective-permute-done.5.refs_6_
  8.2 1.6 %collective-permute-start.6 = (bf16[32,640]{1,0:T(8,128)(2,1)S(1)}, bf16[32,640]{1,0:T(8,128)(2,1)S(1)}, u32[]{:S(2)}, u32[]{:S(2)}) collective-permute-start(bf16[32,640]{1,0:T(8,128)(2,1)S(1)} %collective-permute-done.5.refs_6_), channel_id=1, source_target_pairs={{0,2},{2,0},{4,6},{6,4},{8,10},{10,8},{12,14},{14,12},{1,3},{3,1},... | collective-permute-start | bytes 122888 | tf_op jit(solution)/shard_map/ppermute | solution.py:30
  9.8 1.0 %collective-permute-done.3.refs_4_ = bf16[32,640]{1,0:T(8,128)(2,1)S(1)} collective-permute-done((bf16[32,640]{1,0:T(8,128)(2,1)S(1)}, bf16[32,640]{1,0:T(8,128)(2,1)S(1)}, u32[]{:S(2)}, u32[]{:S(2)}) %collective-permute-start.3) | collective-permute-done | bytes 40992 | tf_op jit(solution)/shard_map/ppermute | solution.py:30
  10.8 1.5 %collective-permute-start.4 = (bf16[32,640]{1,0:T(8,128)(2,1)S(1)}, bf16[32,640]{1,0:T(8,128)(2,1)S(1)}, u32[]{:S(2)}, u32[]{:S(2)}) collective-permute-start(bf16[32,640]{1,0:T(8,128)(2,1)S(1)} %collective-permute-done.3.refs_4_), channel_id=1, source_target_pairs={{0,2},{2,0},{4,6},{6,4},{8,10},{10,8},{12,14},{14,12},{1,3},{3,1},... | collective-permute-start | bytes 122888 | tf_op jit(solution)/shard_map/ppermute | solution.py:30
  12.4 0.0 collective-permute-done.1.refs_2_
  12.4 0.5 %collective-permute-start.2 = (bf16[32,640]{1,0:T(8,128)(2,1)S(1)}, bf16[32,640]{1,0:T(8,128)(2,1)S(1)}, u32[]{:S(2)}, u32[]{:S(2)}) collective-permute-start(bf16[32,640]{1,0:T(8,128)(2,1)S(1)} %collective-permute-done.1.refs_2_), channel_id=1, source_target_pairs={{0,2},{2,0},{4,6},{6,4},{8,10},{10,8},{12,14},{14,12},{1,3},{3,1},... | collective-permute-start | bytes 122888 | tf_op jit(solution)/shard_map/ppermute | solution.py:30
  12.9 0.0 collective-permute-done.refs_1_
  12.9 0.0 collective-permute-done.6.refs_7_
  12.9 2.0 %collective-permute-done.4.refs_5_ = bf16[32,640]{1,0:T(8,128)(2,1)S(1)} collective-permute-done((bf16[32,640]{1,0:T(8,128)(2,1)S(1)}, bf16[32,640]{1,0:T(8,128)(2,1)S(1)}, u32[]{:S(2)}, u32[]{:S(2)}) %collective-permute-start.4) | collective-permute-done | bytes 40992 | tf_op jit(solution)/shard_map/ppermute | solution.py:30
  14.8 1.5 %collective-permute-done.2.refs_3_ = bf16[32,640]{1,0:T(8,128)(2,1)S(1)} collective-permute-done((bf16[32,640]{1,0:T(8,128)(2,1)S(1)}, bf16[32,640]{1,0:T(8,128)(2,1)S(1)}, u32[]{:S(2)}, u32[]{:S(2)}) %collective-permute-start.2) | collective-permute-done | bytes 40992 | tf_op jit(solution)/shard_map/ppermute | solution.py:30
  16.4 0.1 collective-permute-start.7
  16.5 1.6 %collective-permute-done.7.refs_1_ = bf16[8,32,640]{2,1,0:T(8,128)(2,1)S(1)} collective-permute-done((bf16[8,32,640]{2,1,0:T(8,128)(2,1)S(1)}, bf16[8,32,640]{2,1,0:T(8,128)(2,1)S(1)}, u32[]{:S(2)}, u32[]{:S(2)}) %collective-permute-start.7) | collective-permute-done | bytes 327712 | tf_op jit(solution)/shard_map/ppermute | solution.py:30
  18.1 0.0 copy-done
  18.1 0.0 copy-done.1
  18.1 5.0 %dens.1 = (f32[5,32,512]{2,1,0:T(8,128)S(1)}, bf16[5,32,512]{2,1,0:T(8,128)(2,1)S(1)}, bf16[2,256,5120]{2,1,0:T(8,128)(2,1)S(1)}) custom-call(bf16[8,32,640]{2,1,0:T(8,128)(2,1)S(1)} %stack.1.refs_0_, bf16[8,32,640]{2,1,0:T(8,128)(2,1)S(1)} %collective-permute-done.7.refs_1_, bf16[10,512,512]{2,1,0:T(8,128)(2,1)S(1)} %copy-done, ...), custom_call_target="tpu_custom_call" | custom-call | flops 1677721600 | tf_op jit(solution)/shard_map/dens/pallas_call | solution.py:217
  23.1 0.0 copy-start.2
  23.1 0.0 copy-start.3
  23.1 1.6 %collective-permute-start.9 = (bf16[5,32,512]{2,1,0:T(8,128)(2,1)S(1)}, bf16[5,32,512]{2,1,0:T(8,128)(2,1)S(1)}, u32[]{:S(2)}, u32[]{:S(2)}) collective-permute-start(bf16[5,32,512]{2,1,0:T(8,128)(2,1)S(1)} %get-tuple-element.12), channel_id=1, source_target_pairs={{0,16},{16,0},{1,17},{17,1},{2,18},{18,2},{3,19},{19,3},{4,20},{20... | collective-permute-start | bytes 491528 | tf_op jit(solution)/shard_map/ppermute | solution.py:30
  24.7 1.6 %fac.1.refs_0_ = f32[32,256]{1,0:T(8,128)S(1)} custom-call(bf16[8,32,640]{2,1,0:T(8,128)(2,1)S(1)} %stack.1.refs_0_, bf16[8,32,640]{2,1,0:T(8,128)(2,1)S(1)} %collective-permute-done.7.refs_1_, bf16[2,256,5120]{2,1,0:T(8,128)(2,1)S(1)} %get-tuple-element.10.refs_2_), custom_call_target="tpu_custom_call" | custom-call | flops 167772160 | tf_op jit(solution)/shard_map/fac/pallas_call | solution.py:235
  26.3 0.6 %collective-permute-start.8 = (f32[32,256]{1,0:T(8,128)S(1)}, f32[32,256]{1,0:T(8,128)S(1)}, u32[]{:S(2)}, u32[]{:S(2)}) collective-permute-start(f32[32,256]{1,0:T(8,128)S(1)} %fac.1.refs_0_), channel_id=1, source_target_pairs={{0,16},{16,0},{1,17},{17,1},{2,18},{18,2},{3,19},{19,3},{4,20},{20... | collective-permute-start | bytes 98312 | tf_op jit(solution)/shard_map/ppermute | solution.py:30
  26.9 2.9 %collective-permute-done.9.refs_2_ = bf16[5,32,512]{2,1,0:T(8,128)(2,1)S(1)} collective-permute-done((bf16[5,32,512]{2,1,0:T(8,128)(2,1)S(1)}, bf16[5,32,512]{2,1,0:T(8,128)(2,1)S(1)}, u32[]{:S(2)}, u32[]{:S(2)}) %collective-permute-start.9) | collective-permute-done | bytes 163872 | tf_op jit(solution)/shard_map/ppermute | solution.py:30
  29.8 0.0 copy-done.2
  29.8 0.0 copy-done.3
  29.8 2.4 %grid.1.refs_3_ = f32[640,512]{1,0:T(8,128)S(1)} custom-call(s32[10]{0:T(128)S(1)} %copy-done.3, f32[5,32,512]{2,1,0:T(8,128)S(1)} %get-tuple-element.11.refs_1_, bf16[5,32,512]{2,1,0:T(8,128)(2,1)S(1)} %collective-permute-done.9.refs_2_, bf16[10,40,512]{2,1,0:T(8,128)(2,1)S(1)} %copy-done.1, f32[10,512]{1,0:T(8,128)S(1)} %copy-done.2, ...), custom_call_target="tpu_custom_call" | custom-call | flops 1677721600 | tf_op jit(solution)/shard_map/grid/pallas_call | solution.py:240
  32.2 0.0 copy-start.5
  32.2 0.0 collective-permute-done.8.refs_1_
  32.2 1.0 %back.1 = (f32[8,32,640]{2,1,0:T(8,128)S(1)}, bf16[8,32,640]{2,1,0:T(8,128)(2,1)S(1)}) custom-call(f32[32,256]{1,0:T(8,128)S(1)} %fac.1.refs_0_, f32[32,256]{1,0:T(8,128)S(1)} %collective-permute-done.8.refs_1_, bf16[2,256,5120]{2,1,0:T(8,128)(2,1)S(1)} %get-tuple-element.10.refs_2_, f32[640,512]{1,0:T(8,128)S(1)} %grid.1.refs_3_), custom_call_target="tpu_custom_call" | custom-call | flops 167772160 | tf_op jit(solution)/shard_map/back/pallas_call | solution.py:248
  33.2 0.1 collective-permute-start.10
  33.3 1.6 %collective-permute-done.10 = bf16[8,32,640]{2,1,0:T(8,128)(2,1)S(1)} collective-permute-done((bf16[8,32,640]{2,1,0:T(8,128)(2,1)S(1)}, bf16[8,32,640]{2,1,0:T(8,128)(2,1)S(1)}, u32[]{:S(2)}, u32[]{:S(2)}) %collective-permute-start.10) | collective-permute-done | bytes 327712 | tf_op jit(solution)/shard_map/ppermute | solution.py:30
  34.9 0.1 convert_add_fusion
  35.1 0.6 %collective-permute-start.11 = (bf16[4,32,640]{2,1,0:T(8,128)(2,1)S(1)}, bf16[4,32,640]{2,1,0:T(8,128)(2,1)S(1)}, u32[]{:S(2)}, u32[]{:S(2)}) collective-permute-start(bf16[4,32,640]{2,1,0:T(8,128)(2,1)S(1)} %fusion.2), channel_id=1, source_target_pairs={{0,2},{2,0},{4,6},{6,4},{8,10},{10,8},{12,14},{14,12},{1,3},{3,1},... | collective-permute-start | bytes 491528 | tf_op jit(solution)/shard_map/ppermute | solution.py:30
  35.6 5.7 %collective-permute-done.11 = bf16[4,32,640]{2,1,0:T(8,128)(2,1)S(1)} collective-permute-done((bf16[4,32,640]{2,1,0:T(8,128)(2,1)S(1)}, bf16[4,32,640]{2,1,0:T(8,128)(2,1)S(1)}, u32[]{:S(2)}, u32[]{:S(2)}) %collective-permute-start.11) | collective-permute-done | bytes 163872 | tf_op jit(solution)/shard_map/ppermute | solution.py:30
  41.4 0.1 collective-permute-start.12
  41.5 2.1 %collective-permute-start.14 = (bf16[1,32,640]{2,1,0:T(8,128)(2,1)S(1)}, bf16[1,32,640]{2,1,0:T(8,128)(2,1)S(1)}, u32[]{:S(2)}, u32[]{:S(2)}) collective-permute-start(bf16[1,32,640]{2,1,0:T(8,128)(2,1)S(1)} %get-tuple-element.18), channel_id=1, source_target_pairs={{0,12},{2,14},{4,8},{6,10},{8,4},{10,6},{12,0},{14,2},{1,13},{3,15... | collective-permute-start | bytes 122888 | tf_op jit(solution)/shard_map/ppermute | solution.py:30
  43.6 1.4 %collective-permute-start.13 = (bf16[1,32,640]{2,1,0:T(8,128)(2,1)S(1)}, bf16[1,32,640]{2,1,0:T(8,128)(2,1)S(1)}, u32[]{:S(2)}, u32[]{:S(2)}) collective-permute-start(bf16[1,32,640]{2,1,0:T(8,128)(2,1)S(1)} %get-tuple-element.19), channel_id=1, source_target_pairs={{0,8},{2,10},{4,12},{6,14},{8,0},{10,2},{12,4},{14,6},{1,9},{3,11}... | collective-permute-start | bytes 122888 | tf_op jit(solution)/shard_map/ppermute | solution.py:30
  45.0 0.8 %collective-permute-done.12 = bf16[1,32,640]{2,1,0:T(8,128)(2,1)S(1)} collective-permute-done((bf16[1,32,640]{2,1,0:T(8,128)(2,1)S(1)}, bf16[1,32,640]{2,1,0:T(8,128)(2,1)S(1)}, u32[]{:S(2)}, u32[]{:S(2)}) %collective-permute-start.12) | collective-permute-done | bytes 40992 | tf_op jit(solution)/shard_map/ppermute | solution.py:30
  45.7 1.6 %collective-permute-done.14 = bf16[1,32,640]{2,1,0:T(8,128)(2,1)S(1)} collective-permute-done((bf16[1,32,640]{2,1,0:T(8,128)(2,1)S(1)}, bf16[1,32,640]{2,1,0:T(8,128)(2,1)S(1)}, u32[]{:S(2)}, u32[]{:S(2)}) %collective-permute-start.14) | collective-permute-done | bytes 40992 | tf_op jit(solution)/shard_map/ppermute | solution.py:30
  47.4 1.5 %collective-permute-done.13 = bf16[1,32,640]{2,1,0:T(8,128)(2,1)S(1)} collective-permute-done((bf16[1,32,640]{2,1,0:T(8,128)(2,1)S(1)}, bf16[1,32,640]{2,1,0:T(8,128)(2,1)S(1)}, u32[]{:S(2)}, u32[]{:S(2)}) %collective-permute-start.13) | collective-permute-done | bytes 40992 | tf_op jit(solution)/shard_map/ppermute | solution.py:30
  48.9 0.0 copy-done.5
  48.9 0.7 %fusion.9 = bf16[640,32]{0,1:T(8,128)(2,1)} fusion(bf16[1,32,640]{2,1,0:T(8,128)(2,1)S(1)} %collective-permute-done.14, bf16[1,32,640]{2,1,0:T(8,128)(2,1)S(1)} %collective-permute-done.13, bf16[1,32,640]{2,1,0:T(8,128)(2,1)S(1)} %collective-permute-done.12, f32[1,4,32,640]{3,2,1,0:T(8,128)S(1)} %get-tuple-element.16, bf16[32,640]{1,0:T(8,128)(2,1)S(1)} %head.1.refs_0_, ...), kind=kLoop, calls=%fused_computation.13 | loop fusion | flops 204800 | bytes 289280 | tf_op jit(solution)/shard_map/transpose | solution.py:269
  (5 shorter events, 0.1 us)
Async XLA Ops:
  0.0 0.8 %copy-start.4 = (bf16[640,32]{0,1:T(8,128)(2,1)S(1)}, bf16[640,32]{0,1:T(8,128)(2,1)}, u32[]{:S(2)}) copy-start(bf16[640,32]{0,1:T(8,128)(2,1)} %param.7) | copy-start | bytes 122884
  0.8 17.3 %copy-start = (bf16[10,512,512]{2,1,0:T(8,128)(2,1)S(1)}, bf16[10,512,512]{2,1,0:T(8,128)(2,1)}, u32[]{:S(2)}) copy-start(bf16[10,512,512]{2,1,0:T(8,128)(2,1)} %refs_5_.1) | copy-start | bytes 15728644
  0.8 17.3 %copy-start.1 = (bf16[10,40,512]{2,1,0:T(8,128)(2,1)S(1)}, bf16[10,40,512]{2,1,0:T(8,128)(2,1)}, u32[]{:S(2)}) copy-start(bf16[10,40,512]{2,1,0:T(8,128)(2,1)} %refs_3_.3) | copy-start | bytes 1228804
  0.8 7.5 %collective-permute-start.5 = (bf16[32,640]{1,0:T(8,128)(2,1)S(1)}, bf16[32,640]{1,0:T(8,128)(2,1)S(1)}, u32[]{:S(2)}, u32[]{:S(2)}) collective-permute-start(bf16[32,640]{1,0:T(8,128)(2,1)S(1)} %head.1.refs_0_), channel_id=1, source_target_pairs={{0,12},{2,14},{4,8},{6,10},{8,4},{10,6},{12,0},{14,2},{1,13},{3,15... | collective-permute-start | bytes 122888 | tf_op jit(solution)/shard_map/ppermute | solution.py:30
  5.9 4.9 %collective-permute-start.3 = (bf16[32,640]{1,0:T(8,128)(2,1)S(1)}, bf16[32,640]{1,0:T(8,128)(2,1)S(1)}, u32[]{:S(2)}, u32[]{:S(2)}) collective-permute-start(bf16[32,640]{1,0:T(8,128)(2,1)S(1)} %head.1.refs_0_), channel_id=1, source_target_pairs={{0,8},{2,10},{4,12},{6,14},{8,0},{10,2},{12,4},{14,6},{1,9},{3,11}... | collective-permute-start | bytes 122888 | tf_op jit(solution)/shard_map/ppermute | solution.py:30
  5.9 6.4 %collective-permute-start.1 = (bf16[32,640]{1,0:T(8,128)(2,1)S(1)}, bf16[32,640]{1,0:T(8,128)(2,1)S(1)}, u32[]{:S(2)}, u32[]{:S(2)}) collective-permute-start(bf16[32,640]{1,0:T(8,128)(2,1)S(1)} %head.1.refs_0_), channel_id=1, source_target_pairs={{0,4},{2,6},{4,0},{6,2},{8,12},{10,14},{12,8},{14,10},{1,5},{3,7},... | collective-permute-start | bytes 122888 | tf_op jit(solution)/shard_map/ppermute | solution.py:30
  6.6 6.3 %collective-permute-start = (bf16[32,640]{1,0:T(8,128)(2,1)S(1)}, bf16[32,640]{1,0:T(8,128)(2,1)S(1)}, u32[]{:S(2)}, u32[]{:S(2)}) collective-permute-start(bf16[32,640]{1,0:T(8,128)(2,1)S(1)} %head.1.refs_0_), channel_id=1, source_target_pairs={{0,2},{2,0},{4,6},{6,4},{8,10},{10,8},{12,14},{14,12},{1,3},{3,1},... | collective-permute-start | bytes 122888 | tf_op jit(solution)/shard_map/ppermute | solution.py:30
  8.2 4.6 %collective-permute-start.6 = (bf16[32,640]{1,0:T(8,128)(2,1)S(1)}, bf16[32,640]{1,0:T(8,128)(2,1)S(1)}, u32[]{:S(2)}, u32[]{:S(2)}) collective-permute-start(bf16[32,640]{1,0:T(8,128)(2,1)S(1)} %collective-permute-done.5.refs_6_), channel_id=1, source_target_pairs={{0,2},{2,0},{4,6},{6,4},{8,10},{10,8},{12,14},{14,12},{1,3},{3,1},... | collective-permute-start | bytes 122888 | tf_op jit(solution)/shard_map/ppermute | solution.py:30
  10.8 4.0 %collective-permute-start.4 = (bf16[32,640]{1,0:T(8,128)(2,1)S(1)}, bf16[32,640]{1,0:T(8,128)(2,1)S(1)}, u32[]{:S(2)}, u32[]{:S(2)}) collective-permute-start(bf16[32,640]{1,0:T(8,128)(2,1)S(1)} %collective-permute-done.3.refs_4_), channel_id=1, source_target_pairs={{0,2},{2,0},{4,6},{6,4},{8,10},{10,8},{12,14},{14,12},{1,3},{3,1},... | collective-permute-start | bytes 122888 | tf_op jit(solution)/shard_map/ppermute | solution.py:30
  12.4 4.0 %collective-permute-start.2 = (bf16[32,640]{1,0:T(8,128)(2,1)S(1)}, bf16[32,640]{1,0:T(8,128)(2,1)S(1)}, u32[]{:S(2)}, u32[]{:S(2)}) collective-permute-start(bf16[32,640]{1,0:T(8,128)(2,1)S(1)} %collective-permute-done.1.refs_2_), channel_id=1, source_target_pairs={{0,2},{2,0},{4,6},{6,4},{8,10},{10,8},{12,14},{14,12},{1,3},{3,1},... | collective-permute-start | bytes 122888 | tf_op jit(solution)/shard_map/ppermute | solution.py:30
  16.4 1.7 %collective-permute-start.7 = (bf16[8,32,640]{2,1,0:T(8,128)(2,1)S(1)}, bf16[8,32,640]{2,1,0:T(8,128)(2,1)S(1)}, u32[]{:S(2)}, u32[]{:S(2)}) collective-permute-start(bf16[8,32,640]{2,1,0:T(8,128)(2,1)S(1)} %stack.1.refs_0_), channel_id=1, source_target_pairs={{0,1},{1,0},{2,3},{3,2},{4,5},{5,4},{6,7},{7,6},{8,9},{9,8},{10,11... | collective-permute-start | bytes 983048 | tf_op jit(solution)/shard_map/ppermute | solution.py:30
  23.1 6.7 %copy-start.2 = (f32[10,512]{1,0:T(8,128)S(1)}, f32[10,512]{1,0:T(8,128)}, u32[]{:S(2)}) copy-start(f32[10,512]{1,0:T(8,128)} %refs_4_.3) | copy-start | bytes 61444
  23.1 6.7 %copy-start.3 = (s32[10]{0:T(128)S(1)}, s32[10]{0:T(128)}, u32[]{:S(2)}) copy-start(s32[10]{0:T(128)} %refs_0_.1) | copy-start | bytes 124
  23.1 6.7 %collective-permute-start.9 = (bf16[5,32,512]{2,1,0:T(8,128)(2,1)S(1)}, bf16[5,32,512]{2,1,0:T(8,128)(2,1)S(1)}, u32[]{:S(2)}, u32[]{:S(2)}) collective-permute-start(bf16[5,32,512]{2,1,0:T(8,128)(2,1)S(1)} %get-tuple-element.12), channel_id=1, source_target_pairs={{0,16},{16,0},{1,17},{17,1},{2,18},{18,2},{3,19},{19,3},{4,20},{20... | collective-permute-start | bytes 491528 | tf_op jit(solution)/shard_map/ppermute | solution.py:30
  26.3 5.9 %collective-permute-start.8 = (f32[32,256]{1,0:T(8,128)S(1)}, f32[32,256]{1,0:T(8,128)S(1)}, u32[]{:S(2)}, u32[]{:S(2)}) collective-permute-start(f32[32,256]{1,0:T(8,128)S(1)} %fac.1.refs_0_), channel_id=1, source_target_pairs={{0,16},{16,0},{1,17},{17,1},{2,18},{18,2},{3,19},{19,3},{4,20},{20... | collective-permute-start | bytes 98312 | tf_op jit(solution)/shard_map/ppermute | solution.py:30
  32.2 16.7 %copy-start.5 = (f32[640]{0:T(1024)S(1)}, f32[640]{0:T(1024)}, u32[]{:S(2)}) copy-start(f32[640]{0:T(1024)} %param.8) | copy-start | bytes 7684
  33.2 1.7 %collective-permute-start.10 = (bf16[8,32,640]{2,1,0:T(8,128)(2,1)S(1)}, bf16[8,32,640]{2,1,0:T(8,128)(2,1)S(1)}, u32[]{:S(2)}, u32[]{:S(2)}) collective-permute-start(bf16[8,32,640]{2,1,0:T(8,128)(2,1)S(1)} %get-tuple-element.14), channel_id=1, source_target_pairs={{0,1},{1,0},{2,3},{3,2},{4,5},{5,4},{6,7},{7,6},{8,9},{9,8},{10,11... | collective-permute-start | bytes 983048 | tf_op jit(solution)/shard_map/ppermute | solution.py:30
  35.1 6.3 %collective-permute-start.11 = (bf16[4,32,640]{2,1,0:T(8,128)(2,1)S(1)}, bf16[4,32,640]{2,1,0:T(8,128)(2,1)S(1)}, u32[]{:S(2)}, u32[]{:S(2)}) collective-permute-start(bf16[4,32,640]{2,1,0:T(8,128)(2,1)S(1)} %fusion.2), channel_id=1, source_target_pairs={{0,2},{2,0},{4,6},{6,4},{8,10},{10,8},{12,14},{14,12},{1,3},{3,1},... | collective-permute-start | bytes 491528 | tf_op jit(solution)/shard_map/ppermute | solution.py:30
  41.4 4.3 %collective-permute-start.12 = (bf16[1,32,640]{2,1,0:T(8,128)(2,1)S(1)}, bf16[1,32,640]{2,1,0:T(8,128)(2,1)S(1)}, u32[]{:S(2)}, u32[]{:S(2)}) collective-permute-start(bf16[1,32,640]{2,1,0:T(8,128)(2,1)S(1)} %get-tuple-element.17), channel_id=1, source_target_pairs={{0,4},{2,6},{4,0},{6,2},{8,12},{10,14},{12,8},{14,10},{1,5},{3,7},... | collective-permute-start | bytes 122888 | tf_op jit(solution)/shard_map/ppermute | solution.py:30
  41.5 5.9 %collective-permute-start.14 = (bf16[1,32,640]{2,1,0:T(8,128)(2,1)S(1)}, bf16[1,32,640]{2,1,0:T(8,128)(2,1)S(1)}, u32[]{:S(2)}, u32[]{:S(2)}) collective-permute-start(bf16[1,32,640]{2,1,0:T(8,128)(2,1)S(1)} %get-tuple-element.18), channel_id=1, source_target_pairs={{0,12},{2,14},{4,8},{6,10},{8,4},{10,6},{12,0},{14,2},{1,13},{3,15... | collective-permute-start | bytes 122888 | tf_op jit(solution)/shard_map/ppermute | solution.py:30
  43.6 5.3 %collective-permute-start.13 = (bf16[1,32,640]{2,1,0:T(8,128)(2,1)S(1)}, bf16[1,32,640]{2,1,0:T(8,128)(2,1)S(1)}, u32[]{:S(2)}, u32[]{:S(2)}) collective-permute-start(bf16[1,32,640]{2,1,0:T(8,128)(2,1)S(1)} %get-tuple-element.19), channel_id=1, source_target_pairs={{0,8},{2,10},{4,12},{6,14},{8,0},{10,2},{12,4},{14,6},{1,9},{3,11}... | collective-permute-start | bytes 122888 | tf_op jit(solution)/shard_map/ppermute | solution.py:30

commit v4 on v3

--- a/solution.py
+++ b/solution.py
@@ -30,7 +30,7 @@
     return lax.ppermute(x, axis, [(i, i ^ mask) for i in range(count)])
 
 
-def call(body, out_shape, in_specs, flops=0, scratch=(), limit=24, name=None):
+def call(body, out_shape, in_specs, flops=0, scratch=(), limit=14, name=None):
     return pl.pallas_call(
         body,
         out_shape=out_shape,
@@ -84,10 +84,6 @@
     out[...] = given[...]
 
 
-def flat_of(ref, count):
-    return jnp.concatenate([ref[m] for m in range(count)], axis=1)
-
-
 def stack_kernel(plan, *refs):
     for m, piece in enumerate(refs[:-1]):
         refs[-1][m] = piece[...]
@@ -99,23 +95,15 @@
     return lambda i: occ32[pl.ds(base + i, 1), :]
 
 
-def dens_kernel(plan, mine, other, vir, occ, fac_hbm, dens, sent, fac, rows, occ32, fsem):
+def factor_block(plan, fac, m, width):
+    top = pl.multiple_of(lax.axis_index("vec") * plan.aux, plan.aux)
+    at = lax.axis_index("grp") * plan.pairs + plan.owner(m) * width
+    return fac[pl.ds(top, plan.aux), pl.ds(pl.multiple_of(at, LANES), width)]
+
+
+def dens_kernel(plan, mine, other, vir, occ, dens, sent, rows, occ32):
     k = plan.k
-    grp, vec = lax.axis_index("grp"), lax.axis_index("vec")
-    top = pl.multiple_of(vec * plan.aux, 8)
-    copies = []
-    for h in range(plan.vecs):
-        for m in range(plan.count):
-            at = pl.multiple_of(grp * plan.pairs + plan.block(h, m, 0) * LANES, LANES)
-            copies.append(
-                pltpu.make_async_copy(
-                    fac_hbm.at[pl.ds(top, plan.aux), pl.ds(at, plan.length)],
-                    fac.at[h, :, pl.ds(m * plan.length, plan.length)],
-                    fsem.at[h, m],
-                )
-            )
-    for copy in copies:
-        copy.start()
+    vec = lax.axis_index("vec")
     for h, half in enumerate((mine, other)):
         for m in range(plan.count):
             for j in range(plan.per):
@@ -130,15 +118,21 @@
             total = total + row(i) * trans[i * k : (i + 1) * k, :]
         dens[b] = total
         sent[b] = total.astype(sent.dtype)
-    for copy in copies:
-        copy.wait()
-
-
-def fac_kernel(plan, mine, other, fac, out):
+
+
+def fac_kernel(plan, mine, other, fac, out, flat):
+    width = plan.vecs * plan.length
+    for h, half in enumerate((mine, other)):
+        for m in range(plan.count):
+            at = m * width + plan.part(h) * plan.length
+            flat[:, pl.ds(pl.multiple_of(at, LANES), plan.length)] = half[m]
     value = 0.0
-    for h, half in enumerate((mine, other)):
+    for m in range(plan.count):
         value += lax.dot_general(
-            flat_of(half, plan.count), fac[h], NT, preferred_element_type=jnp.float32
+            flat[:, m * width : (m + 1) * width],
+            factor_block(plan, fac, m, width),
+            NT,
+            preferred_element_type=jnp.float32,
         )
     out[...] = value
 
@@ -165,13 +159,20 @@
 
 def back_kernel(plan, part_a, part_b, fac, acc, stay, sent):
     both = (part_a[...] + part_b[...]).astype(jnp.bfloat16)
-    for h, out in enumerate((stay, sent)):
-        value = 2.0 * lax.dot_general(both, fac[h], NN, preferred_element_type=jnp.float32)
-        for m in range(plan.count):
+    width = plan.vecs * plan.length
+    for m in range(plan.count):
+        value = 2.0 * lax.dot_general(
+            both, factor_block(plan, fac, m, width), NN, preferred_element_type=jnp.float32
+        )
+        for h, out in enumerate((stay, sent)):
+            chosen = value[:, : plan.length]
+            for p in range(1, plan.vecs):
+                part = value[:, p * plan.length : (p + 1) * plan.length]
+                chosen = jnp.where(plan.part(h) == p, part, chosen)
             for j in range(plan.per):
-                at = m * plan.length + j * LANES
-                total = value[:, at : at + LANES] + acc[plan.place(h, m, j)]
-                out[m, :, j * LANES : (j + 1) * LANES] = total.astype(out.dtype)
+                lanes = slice(j * LANES, (j + 1) * LANES)
+                total = chosen[:, lanes] + acc[plan.place(h, m, j)]
+                out[m, :, lanes] = total.astype(out.dtype)
 
 
 def local(trial, energy_gap, coulomb_factors, occ_values, vir_values, kernel, live_points, sizes):
@@ -189,13 +190,14 @@
     start = call(
         bind(head_kernel), shape(trial_cols.shape, bf16), [VMEM], flops=HEAD, name="head"
     )(trial_cols)
-    pieces, masks = [start], [0]
+    pieces, masks = [trial_cols], [0]
     for stride, radix in reversed(digits):
         known = len(masks)
         for d in range(1, radix):
             for n in range(known):
                 pieces.append(swap(pieces[n], "blk", blks, d * stride))
                 masks.append(masks[n] ^ (d * stride))
+    pieces[0] = start
     pieces = [p for _, p in sorted(zip(masks, pieces), key=lambda pair: pair[0])]
 
     if plan.aligned:
@@ -214,27 +216,30 @@
     flops = 2 * k * plan.aux * plan.pairs
     grid_flops = 2 * batches * points * virs * occs * k
     occ_scratch = pltpu.VMEM((batches, plan.occ_all, points), f32)
-    dens, sent, fac = call(
+    dens, sent = call(
         bind(dens_kernel),
         (
             shape((batches, k, points), f32),
             shape((batches, k, points), bf16),
-            shape((vecs, plan.aux, plan.count * plan.length), bf16),
         ),
-        [VMEM] * 4 + [HBM],
+        [VMEM] * 4,
         grid_flops,
         [
             pltpu.VMEM((occs * k, virs), bf16),
             occ_scratch,
-            pltpu.SemaphoreType.DMA((vecs, plan.count)),
         ],
         name="dens",
-    )(mine, other, vir_values, occ_values, coulomb_factors)
+    )(mine, other, vir_values, occ_values)
     other_dens = swap(sent, "grp", groups, 1)
 
-    part = call(bind(fac_kernel), shape((k, plan.aux), f32), [VMEM] * 3, flops, name="fac")(
-        mine, other, fac
-    )
+    part = call(
+        bind(fac_kernel),
+        shape((k, plan.aux), f32),
+        [VMEM] * 3,
+        flops,
+        [pltpu.VMEM((k, plan.pairs), bf16)],
+        name="fac",
+    )(mine, other, coulomb_factors)
     other_part = swap(part, "grp", groups, 1)
 
     acc = call(
@@ -247,7 +252,7 @@
     )(live_points, dens, other_dens, occ_values, kernel, vir_values)
     stay, sent = call(
         bind(back_kernel), (shape(half, f32), shape(half, bf16)), [VMEM] * 4, flops, name="back"
-    )(part, other_part, fac, acc)
+    )(part, other_part, coulomb_factors, acc)
 
     if plan.aligned:
         total = stay + swap(sent, "vec", vecs, 1).astype(f32)

time: 49.7 us -> 46.7 us (0.940)
  Pallas kernels: 10.1 us -> 7.63 us
  waiting for transfers between devices: 20.3 us -> 19.5 us
    pallas_call x1, Pallas kernels: 5 us -> 2.48 us  [local(): call(bind(dens_kernel), (shape((batches, k, points), f32), shape((batches...]
    ppermute x15, waiting for transfers between devices: 20.3 us -> 19.5 us  [swap(): return lax.ppermute(x, axis, [(i, i ^ mask) for i in range(count)])]
  transfers between devices with their start and end apart: 15 -> 15, of which waited for: 10 -> 10; matrix products, arithmetic and copies ran while one was open for 0% -> 0% of each run, Pallas kernels for 8% -> 9%
where the time goes in v4:
time: 46.7 us; the launch traced here: 46.6 us
  waiting for transfers between devices  19.5 us (42%)
  starting transfers between devices  17.7 us (38%)
  Pallas kernels  7.63 us (16%)
  local copies, waits for them, and re-layouts  0.85 us (2%)
  other arithmetic  0.77 us (2%)
    ppermute x15, waiting for transfers between devices, swap(): return lax.ppermute(x, axis, [(i, i ^ mask) for i in range(count)])  19.5 us
    ppermute x15, starting transfers between devices, swap(): return lax.ppermute(x, axis, [(i, i ^ mask) for i in range(count)])  17.7 us
    pallas_call x1, Pallas kernels, local(): call(bind(dens_kernel), (shape((batches, k, points), f32), shape((batches...  2.48 us
    pallas_call x1, Pallas kernels, local(): call(bind(grid_kernel), shape((occs * k, virs), f32), [SMEM] + [VMEM] * 5...  2.4 us
    pallas_call x1, Pallas kernels, local(): call(bind(fac_kernel), shape((k, plan.aux), f32), [VMEM] * 3, flops, [plt...  1.63 us
    pallas_call x1, Pallas kernels, local(): call(bind(back_kernel), (shape(half, f32), shape(half, bf16)), [VMEM] * 4...  1.09 us
  transfers between devices with their start and end apart: 15, of which 10 were waited for; matrix products, arithmetic and copies ran while one was open for 0% of the time, Pallas kernels for 9%

profile of v4, /device:TPU:0, one launch (start us, length us, event | category | flops | bytes accessed | tf_op | source)
XLA Modules:
  0.0 46.6 jit_solution(16876678771531905877)
XLA Ops:
  0.0 0.0 slice-start
  0.0 0.0 slice-start.1
  0.0 0.0 copy-start.1
  0.0 5.1 %collective-permute-start.5 = (bf16[32,640]{1,0:T(8,128)(2,1)}, bf16[32,640]{1,0:T(8,128)(2,1)S(1)}, u32[]{:S(2)}, u32[]{:S(2)}) collective-permute-start(bf16[32,640]{1,0:T(8,128)(2,1)} %bitcast.48), channel_id=1, source_target_pairs={{0,12},{2,14},{4,8},{6,10},{8,4},{10,6},{12,0},{14,2},{1,13},{3,15... | collective-permute-start | bytes 122888 | tf_op jit(solution)/shard_map/ppermute | solution.py:30
  5.2 0.0 collective-permute-start.3
  5.2 0.6 %collective-permute-start.1 = (bf16[32,640]{1,0:T(8,128)(2,1)}, bf16[32,640]{1,0:T(8,128)(2,1)S(1)}, u32[]{:S(2)}, u32[]{:S(2)}) collective-permute-start(bf16[32,640]{1,0:T(8,128)(2,1)} %bitcast.50), channel_id=1, source_target_pairs={{0,4},{2,6},{4,0},{6,2},{8,12},{10,14},{12,8},{14,10},{1,5},{3,7},... | collective-permute-start | bytes 122888 | tf_op jit(solution)/shard_map/ppermute | solution.py:30
  5.8 1.7 %collective-permute-start = (bf16[32,640]{1,0:T(8,128)(2,1)}, bf16[32,640]{1,0:T(8,128)(2,1)S(1)}, u32[]{:S(2)}, u32[]{:S(2)}) collective-permute-start(bf16[32,640]{1,0:T(8,128)(2,1)} %bitcast.51), channel_id=1, source_target_pairs={{0,2},{2,0},{4,6},{6,4},{8,10},{10,8},{12,14},{14,12},{1,3},{3,1},... | collective-permute-start | bytes 122888 | tf_op jit(solution)/shard_map/ppermute | solution.py:30
  7.5 0.0 collective-permute-done.5.refs_6_
  7.5 1.8 %collective-permute-start.6 = (bf16[32,640]{1,0:T(8,128)(2,1)S(1)}, bf16[32,640]{1,0:T(8,128)(2,1)S(1)}, u32[]{:S(2)}, u32[]{:S(2)}) collective-permute-start(bf16[32,640]{1,0:T(8,128)(2,1)S(1)} %collective-permute-done.5.refs_6_), channel_id=1, source_target_pairs={{0,2},{2,0},{4,6},{6,4},{8,10},{10,8},{12,14},{14,12},{1,3},{3,1},... | collective-permute-start | bytes 122888 | tf_op jit(solution)/shard_map/ppermute | solution.py:30
  9.2 1.0 %collective-permute-done.3.refs_4_ = bf16[32,640]{1,0:T(8,128)(2,1)S(1)} collective-permute-done((bf16[32,640]{1,0:T(8,128)(2,1)}, bf16[32,640]{1,0:T(8,128)(2,1)S(1)}, u32[]{:S(2)}, u32[]{:S(2)}) %collective-permute-start.3) | collective-permute-done | bytes 40992 | tf_op jit(solution)/shard_map/ppermute | solution.py:30
  10.3 1.5 %collective-permute-start.4 = (bf16[32,640]{1,0:T(8,128)(2,1)S(1)}, bf16[32,640]{1,0:T(8,128)(2,1)S(1)}, u32[]{:S(2)}, u32[]{:S(2)}) collective-permute-start(bf16[32,640]{1,0:T(8,128)(2,1)S(1)} %collective-permute-done.3.refs_4_), channel_id=1, source_target_pairs={{0,2},{2,0},{4,6},{6,4},{8,10},{10,8},{12,14},{14,12},{1,3},{3,1},... | collective-permute-start | bytes 122888 | tf_op jit(solution)/shard_map/ppermute | solution.py:30
  11.8 0.0 collective-permute-done.1.refs_2_
  11.8 0.5 %collective-permute-start.2 = (bf16[32,640]{1,0:T(8,128)(2,1)S(1)}, bf16[32,640]{1,0:T(8,128)(2,1)S(1)}, u32[]{:S(2)}, u32[]{:S(2)}) collective-permute-start(bf16[32,640]{1,0:T(8,128)(2,1)S(1)} %collective-permute-done.1.refs_2_), channel_id=1, source_target_pairs={{0,2},{2,0},{4,6},{6,4},{8,10},{10,8},{12,14},{14,12},{1,3},{3,1},... | collective-permute-start | bytes 122888 | tf_op jit(solution)/shard_map/ppermute | solution.py:30
  12.3 0.0 copy-start.4
  12.3 0.8 %copy-done.4 = bf16[640,32]{0,1:T(8,128)(2,1)S(1)} copy-done((bf16[640,32]{0,1:T(8,128)(2,1)S(1)}, bf16[640,32]{0,1:T(8,128)(2,1)}, u32[]{:S(2)}) %copy-start.4) | copy-done | bytes 40984
  13.1 0.0 copy-start
  13.1 0.0 collective-permute-done.refs_1_
  13.1 0.0 collective-permute-done.6.refs_7_
  13.1 1.2 %collective-permute-done.4.refs_5_ = bf16[32,640]{1,0:T(8,128)(2,1)S(1)} collective-permute-done((bf16[32,640]{1,0:T(8,128)(2,1)S(1)}, bf16[32,640]{1,0:T(8,128)(2,1)S(1)}, u32[]{:S(2)}, u32[]{:S(2)}) %collective-permute-start.4) | collective-permute-done | bytes 40992 | tf_op jit(solution)/shard_map/ppermute | solution.py:30
  14.3 1.5 %collective-permute-done.2.refs_3_ = bf16[32,640]{1,0:T(8,128)(2,1)S(1)} collective-permute-done((bf16[32,640]{1,0:T(8,128)(2,1)S(1)}, bf16[32,640]{1,0:T(8,128)(2,1)S(1)}, u32[]{:S(2)}, u32[]{:S(2)}) %collective-permute-start.2) | collective-permute-done | bytes 40992 | tf_op jit(solution)/shard_map/ppermute | solution.py:30
  15.8 0.1 collective-permute-start.7
  15.9 1.6 %collective-permute-done.7.refs_1_ = bf16[8,32,640]{2,1,0:T(8,128)(2,1)S(1)} collective-permute-done((bf16[8,32,640]{2,1,0:T(8,128)(2,1)S(1)}, bf16[8,32,640]{2,1,0:T(8,128)(2,1)S(1)}, u32[]{:S(2)}, u32[]{:S(2)}) %collective-permute-start.7) | collective-permute-done | bytes 327712 | tf_op jit(solution)/shard_map/ppermute | solution.py:30
  17.5 0.0 slice-done
  17.5 0.0 slice-done.1
  17.5 0.0 copy-done.1
  17.5 2.5 %dens.1 = (f32[5,32,512]{2,1,0:T(8,128)S(1)}, bf16[5,32,512]{2,1,0:T(8,128)(2,1)S(1)}) custom-call(bf16[8,32,640]{2,1,0:T(8,128)(2,1)S(1)} %stack.1.refs_0_, bf16[8,32,640]{2,1,0:T(8,128)(2,1)S(1)} %collective-permute-done.7.refs_1_, bf16[10,512,512]{2,1,0:T(8,128)(2,1)S(1)} %bitcast.47, bf16[10,40,512]{2,1,0:T(8,128)(2,1)S(1)} %copy-done.1), custom_call_target="tpu_custom_call" | custom-call | flops 1677721600 | tf_op jit(solution)/shard_map/dens/pallas_call | solution.py:219
  20.0 0.0 copy-start.2
  20.0 0.0 copy-start.3
  20.0 1.5 %collective-permute-start.9 = (bf16[5,32,512]{2,1,0:T(8,128)(2,1)S(1)}, bf16[5,32,512]{2,1,0:T(8,128)(2,1)S(1)}, u32[]{:S(2)}, u32[]{:S(2)}) collective-permute-start(bf16[5,32,512]{2,1,0:T(8,128)(2,1)S(1)} %get-tuple-element.10), channel_id=1, source_target_pairs={{0,16},{16,0},{1,17},{17,1},{2,18},{18,2},{3,19},{19,3},{4,20},{20... | collective-permute-start | bytes 491528 | tf_op jit(solution)/shard_map/ppermute | solution.py:30
  21.6 0.0 copy-done
  21.6 1.6 %fac.1.refs_0_ = f32[32,256]{1,0:T(8,128)S(1)} custom-call(bf16[8,32,640]{2,1,0:T(8,128)(2,1)S(1)} %stack.1.refs_0_, bf16[8,32,640]{2,1,0:T(8,128)(2,1)S(1)} %collective-permute-done.7.refs_1_, bf16[512,20480]{1,0:T(8,128)(2,1)S(1)} %copy-done), custom_call_target="tpu_custom_call" | custom-call | flops 167772160 | tf_op jit(solution)/shard_map/fac/pallas_call | solution.py:235
  23.2 0.6 %collective-permute-start.8 = (f32[32,256]{1,0:T(8,128)S(1)}, f32[32,256]{1,0:T(8,128)S(1)}, u32[]{:S(2)}, u32[]{:S(2)}) collective-permute-start(f32[32,256]{1,0:T(8,128)S(1)} %fac.1.refs_0_), channel_id=1, source_target_pairs={{0,16},{16,0},{1,17},{17,1},{2,18},{18,2},{3,19},{19,3},{4,20},{20... | collective-permute-start | bytes 98312 | tf_op jit(solution)/shard_map/ppermute | solution.py:30
  23.8 2.8 %collective-permute-done.9.refs_2_ = bf16[5,32,512]{2,1,0:T(8,128)(2,1)S(1)} collective-permute-done((bf16[5,32,512]{2,1,0:T(8,128)(2,1)S(1)}, bf16[5,32,512]{2,1,0:T(8,128)(2,1)S(1)}, u32[]{:S(2)}, u32[]{:S(2)}) %collective-permute-start.9) | collective-permute-done | bytes 163872 | tf_op jit(solution)/shard_map/ppermute | solution.py:30
  26.7 0.0 copy-done.2
  26.7 0.0 copy-done.3
  26.7 2.4 %grid.1.refs_3_ = f32[640,512]{1,0:T(8,128)S(1)} custom-call(s32[10]{0:T(128)S(1)} %copy-done.3, f32[5,32,512]{2,1,0:T(8,128)S(1)} %get-tuple-element.9.refs_1_, bf16[5,32,512]{2,1,0:T(8,128)(2,1)S(1)} %collective-permute-done.9.refs_2_, bf16[10,40,512]{2,1,0:T(8,128)(2,1)S(1)} %copy-done.1, f32[10,512]{1,0:T(8,128)S(1)} %copy-done.2, ...), custom_call_target="tpu_custom_call" | custom-call | flops 1677721600 | tf_op jit(solution)/shard_map/grid/pallas_call | solution.py:245
  29.1 0.0 copy-start.5
  29.1 0.0 collective-permute-done.8.refs_1_
  29.1 1.1 %back.1 = (f32[8,32,640]{2,1,0:T(8,128)S(1)}, bf16[8,32,640]{2,1,0:T(8,128)(2,1)S(1)}) custom-call(f32[32,256]{1,0:T(8,128)S(1)} %fac.1.refs_0_, f32[32,256]{1,0:T(8,128)S(1)} %collective-permute-done.8.refs_1_, bf16[512,20480]{1,0:T(8,128)(2,1)S(1)} %copy-done, f32[640,512]{1,0:T(8,128)S(1)} %grid.1.refs_3_), custom_call_target="tpu_custom_call" | custom-call | flops 167772160 | tf_op jit(solution)/shard_map/back/pallas_call | solution.py:253
  30.2 0.1 collective-permute-start.10
  30.3 1.6 %collective-permute-done.10 = bf16[8,32,640]{2,1,0:T(8,128)(2,1)S(1)} collective-permute-done((bf16[8,32,640]{2,1,0:T(8,128)(2,1)S(1)}, bf16[8,32,640]{2,1,0:T(8,128)(2,1)S(1)}, u32[]{:S(2)}, u32[]{:S(2)}) %collective-permute-start.10) | collective-permute-done | bytes 327712 | tf_op jit(solution)/shard_map/ppermute | solution.py:30
  31.9 0.1 convert_add_fusion
  32.0 0.6 %collective-permute-start.11 = (bf16[4,32,640]{2,1,0:T(8,128)(2,1)S(1)}, bf16[4,32,640]{2,1,0:T(8,128)(2,1)S(1)}, u32[]{:S(2)}, u32[]{:S(2)}) collective-permute-start(bf16[4,32,640]{2,1,0:T(8,128)(2,1)S(1)} %fusion.2), channel_id=1, source_target_pairs={{0,2},{2,0},{4,6},{6,4},{8,10},{10,8},{12,14},{14,12},{1,3},{3,1},... | collective-permute-start | bytes 491528 | tf_op jit(solution)/shard_map/ppermute | solution.py:30
  32.6 5.7 %collective-permute-done.11 = bf16[4,32,640]{2,1,0:T(8,128)(2,1)S(1)} collective-permute-done((bf16[4,32,640]{2,1,0:T(8,128)(2,1)S(1)}, bf16[4,32,640]{2,1,0:T(8,128)(2,1)S(1)}, u32[]{:S(2)}, u32[]{:S(2)}) %collective-permute-start.11) | collective-permute-done | bytes 163872 | tf_op jit(solution)/shard_map/ppermute | solution.py:30
  38.4 0.1 collective-permute-start.12
  38.5 2.1 %collective-permute-start.14 = (bf16[1,32,640]{2,1,0:T(8,128)(2,1)S(1)}, bf16[1,32,640]{2,1,0:T(8,128)(2,1)S(1)}, u32[]{:S(2)}, u32[]{:S(2)}) collective-permute-start(bf16[1,32,640]{2,1,0:T(8,128)(2,1)S(1)} %get-tuple-element.16), channel_id=1, source_target_pairs={{0,12},{2,14},{4,8},{6,10},{8,4},{10,6},{12,0},{14,2},{1,13},{3,15... | collective-permute-start | bytes 122888 | tf_op jit(solution)/shard_map/ppermute | solution.py:30
  40.6 1.4 %collective-permute-start.13 = (bf16[1,32,640]{2,1,0:T(8,128)(2,1)S(1)}, bf16[1,32,640]{2,1,0:T(8,128)(2,1)S(1)}, u32[]{:S(2)}, u32[]{:S(2)}) collective-permute-start(bf16[1,32,640]{2,1,0:T(8,128)(2,1)S(1)} %get-tuple-element.17), channel_id=1, source_target_pairs={{0,8},{2,10},{4,12},{6,14},{8,0},{10,2},{12,4},{14,6},{1,9},{3,11}... | collective-permute-start | bytes 122888 | tf_op jit(solution)/shard_map/ppermute | solution.py:30
  42.0 0.8 %collective-permute-done.12 = bf16[1,32,640]{2,1,0:T(8,128)(2,1)S(1)} collective-permute-done((bf16[1,32,640]{2,1,0:T(8,128)(2,1)S(1)}, bf16[1,32,640]{2,1,0:T(8,128)(2,1)S(1)}, u32[]{:S(2)}, u32[]{:S(2)}) %collective-permute-start.12) | collective-permute-done | bytes 40992 | tf_op jit(solution)/shard_map/ppermute | solution.py:30
  42.7 1.6 %collective-permute-done.14 = bf16[1,32,640]{2,1,0:T(8,128)(2,1)S(1)} collective-permute-done((bf16[1,32,640]{2,1,0:T(8,128)(2,1)S(1)}, bf16[1,32,640]{2,1,0:T(8,128)(2,1)S(1)}, u32[]{:S(2)}, u32[]{:S(2)}) %collective-permute-start.14) | collective-permute-done | bytes 40992 | tf_op jit(solution)/shard_map/ppermute | solution.py:30
  44.4 1.5 %collective-permute-done.13 = bf16[1,32,640]{2,1,0:T(8,128)(2,1)S(1)} collective-permute-done((bf16[1,32,640]{2,1,0:T(8,128)(2,1)S(1)}, bf16[1,32,640]{2,1,0:T(8,128)(2,1)S(1)}, u32[]{:S(2)}, u32[]{:S(2)}) %collective-permute-start.13) | collective-permute-done | bytes 40992 | tf_op jit(solution)/shard_map/ppermute | solution.py:30
  45.9 0.0 copy-done.5
  45.9 0.7 %fusion.9 = bf16[640,32]{0,1:T(8,128)(2,1)} fusion(bf16[1,32,640]{2,1,0:T(8,128)(2,1)S(1)} %collective-permute-done.14, bf16[1,32,640]{2,1,0:T(8,128)(2,1)S(1)} %collective-permute-done.13, bf16[1,32,640]{2,1,0:T(8,128)(2,1)S(1)} %collective-permute-done.12, f32[1,4,32,640]{3,2,1,0:T(8,128)S(1)} %get-tuple-element.14, bf16[32,640]{1,0:T(8,128)(2,1)S(1)} %head.1.refs_0_, ...), kind=kLoop, calls=%fused_computation.13 | loop fusion | flops 204800 | bytes 289280 | tf_op jit(solution)/shard_map/transpose | solution.py:274
  (6 shorter events, 0.1 us)
Async XLA Ops:
  0.0 17.5 %slice-start = ((s8[5242880]{0:T(1024)(128)(4,1)}), s8[4194304]{0:T(1024)(128)(4,1)S(1)}, s32[]{:S(2)}) async-start(s8[5242880]{0:T(1024)(128)(4,1)} %bitcast.46), calls=%async_computation | async-start | bytes 8388608
  0.0 17.5 %slice-start.1 = ((s8[5242880]{0:T(1024)(128)(4,1)}), s8[1048576]{0:T(1024)(128)(4,1)S(1)}, s32[]{:S(2)}) async-start(s8[5242880]{0:T(1024)(128)(4,1)} %bitcast.46), calls=%async_computation.1 | async-start | bytes 2097152
  0.0 17.5 %copy-start.1 = (bf16[10,40,512]{2,1,0:T(8,128)(2,1)S(1)}, bf16[10,40,512]{2,1,0:T(8,128)(2,1)}, u32[]{:S(2)}) copy-start(bf16[10,40,512]{2,1,0:T(8,128)(2,1)} %refs_3_.3) | copy-start | bytes 1228804
  0.0 7.5 %collective-permute-start.5 = (bf16[32,640]{1,0:T(8,128)(2,1)}, bf16[32,640]{1,0:T(8,128)(2,1)S(1)}, u32[]{:S(2)}, u32[]{:S(2)}) collective-permute-start(bf16[32,640]{1,0:T(8,128)(2,1)} %bitcast.48), channel_id=1, source_target_pairs={{0,12},{2,14},{4,8},{6,10},{8,4},{10,6},{12,0},{14,2},{1,13},{3,15... | collective-permute-start | bytes 122888 | tf_op jit(solution)/shard_map/ppermute | solution.py:30
  5.2 5.1 %collective-permute-start.3 = (bf16[32,640]{1,0:T(8,128)(2,1)}, bf16[32,640]{1,0:T(8,128)(2,1)S(1)}, u32[]{:S(2)}, u32[]{:S(2)}) collective-permute-start(bf16[32,640]{1,0:T(8,128)(2,1)} %bitcast.49), channel_id=1, source_target_pairs={{0,8},{2,10},{4,12},{6,14},{8,0},{10,2},{12,4},{14,6},{1,9},{3,11}... | collective-permute-start | bytes 122888 | tf_op jit(solution)/shard_map/ppermute | solution.py:30
  5.2 6.6 %collective-permute-start.1 = (bf16[32,640]{1,0:T(8,128)(2,1)}, bf16[32,640]{1,0:T(8,128)(2,1)S(1)}, u32[]{:S(2)}, u32[]{:S(2)}) collective-permute-start(bf16[32,640]{1,0:T(8,128)(2,1)} %bitcast.50), channel_id=1, source_target_pairs={{0,4},{2,6},{4,0},{6,2},{8,12},{10,14},{12,8},{14,10},{1,5},{3,7},... | collective-permute-start | bytes 122888 | tf_op jit(solution)/shard_map/ppermute | solution.py:30
  5.8 7.3 %collective-permute-start = (bf16[32,640]{1,0:T(8,128)(2,1)}, bf16[32,640]{1,0:T(8,128)(2,1)S(1)}, u32[]{:S(2)}, u32[]{:S(2)}) collective-permute-start(bf16[32,640]{1,0:T(8,128)(2,1)} %bitcast.51), channel_id=1, source_target_pairs={{0,2},{2,0},{4,6},{6,4},{8,10},{10,8},{12,14},{14,12},{1,3},{3,1},... | collective-permute-start | bytes 122888 | tf_op jit(solution)/shard_map/ppermute | solution.py:30
  7.5 5.6 %collective-permute-start.6 = (bf16[32,640]{1,0:T(8,128)(2,1)S(1)}, bf16[32,640]{1,0:T(8,128)(2,1)S(1)}, u32[]{:S(2)}, u32[]{:S(2)}) collective-permute-start(bf16[32,640]{1,0:T(8,128)(2,1)S(1)} %collective-permute-done.5.refs_6_), channel_id=1, source_target_pairs={{0,2},{2,0},{4,6},{6,4},{8,10},{10,8},{12,14},{14,12},{1,3},{3,1},... | collective-permute-start | bytes 122888 | tf_op jit(solution)/shard_map/ppermute | solution.py:30
  10.3 4.0 %collective-permute-start.4 = (bf16[32,640]{1,0:T(8,128)(2,1)S(1)}, bf16[32,640]{1,0:T(8,128)(2,1)S(1)}, u32[]{:S(2)}, u32[]{:S(2)}) collective-permute-start(bf16[32,640]{1,0:T(8,128)(2,1)S(1)} %collective-permute-done.3.refs_4_), channel_id=1, source_target_pairs={{0,2},{2,0},{4,6},{6,4},{8,10},{10,8},{12,14},{14,12},{1,3},{3,1},... | collective-permute-start | bytes 122888 | tf_op jit(solution)/shard_map/ppermute | solution.py:30
  11.8 4.0 %collective-permute-start.2 = (bf16[32,640]{1,0:T(8,128)(2,1)S(1)}, bf16[32,640]{1,0:T(8,128)(2,1)S(1)}, u32[]{:S(2)}, u32[]{:S(2)}) collective-permute-start(bf16[32,640]{1,0:T(8,128)(2,1)S(1)} %collective-permute-done.1.refs_2_), channel_id=1, source_target_pairs={{0,2},{2,0},{4,6},{6,4},{8,10},{10,8},{12,14},{14,12},{1,3},{3,1},... | collective-permute-start | bytes 122888 | tf_op jit(solution)/shard_map/ppermute | solution.py:30
  12.3 0.8 %copy-start.4 = (bf16[640,32]{0,1:T(8,128)(2,1)S(1)}, bf16[640,32]{0,1:T(8,128)(2,1)}, u32[]{:S(2)}) copy-start(bf16[640,32]{0,1:T(8,128)(2,1)} %param.7) | copy-start | bytes 122884
  13.1 8.5 %copy-start = (bf16[512,20480]{1,0:T(8,128)(2,1)S(1)}, bf16[512,20480]{1,0:T(8,128)(2,1)}, u32[]{:S(2)}) copy-start(bf16[512,20480]{1,0:T(8,128)(2,1)} %refs_2_.5) | copy-start | bytes 62914564
  15.8 1.7 %collective-permute-start.7 = (bf16[8,32,640]{2,1,0:T(8,128)(2,1)S(1)}, bf16[8,32,640]{2,1,0:T(8,128)(2,1)S(1)}, u32[]{:S(2)}, u32[]{:S(2)}) collective-permute-start(bf16[8,32,640]{2,1,0:T(8,128)(2,1)S(1)} %stack.1.refs_0_), channel_id=1, source_target_pairs={{0,1},{1,0},{2,3},{3,2},{4,5},{5,4},{6,7},{7,6},{8,9},{9,8},{10,11... | collective-permute-start | bytes 983048 | tf_op jit(solution)/shard_map/ppermute | solution.py:30
  20.0 6.7 %copy-start.2 = (f32[10,512]{1,0:T(8,128)S(1)}, f32[10,512]{1,0:T(8,128)}, u32[]{:S(2)}) copy-start(f32[10,512]{1,0:T(8,128)} %refs_4_.1) | copy-start | bytes 61444
  20.0 6.7 %copy-start.3 = (s32[10]{0:T(128)S(1)}, s32[10]{0:T(128)}, u32[]{:S(2)}) copy-start(s32[10]{0:T(128)} %refs_0_.1) | copy-start | bytes 124
  20.0 6.6 %collective-permute-start.9 = (bf16[5,32,512]{2,1,0:T(8,128)(2,1)S(1)}, bf16[5,32,512]{2,1,0:T(8,128)(2,1)S(1)}, u32[]{:S(2)}, u32[]{:S(2)}) collective-permute-start(bf16[5,32,512]{2,1,0:T(8,128)(2,1)S(1)} %get-tuple-element.10), channel_id=1, source_target_pairs={{0,16},{16,0},{1,17},{17,1},{2,18},{18,2},{3,19},{19,3},{4,20},{20... | collective-permute-start | bytes 491528 | tf_op jit(solution)/shard_map/ppermute | solution.py:30
  23.2 5.9 %collective-permute-start.8 = (f32[32,256]{1,0:T(8,128)S(1)}, f32[32,256]{1,0:T(8,128)S(1)}, u32[]{:S(2)}, u32[]{:S(2)}) collective-permute-start(f32[32,256]{1,0:T(8,128)S(1)} %fac.1.refs_0_), channel_id=1, source_target_pairs={{0,16},{16,0},{1,17},{17,1},{2,18},{18,2},{3,19},{19,3},{4,20},{20... | collective-permute-start | bytes 98312 | tf_op jit(solution)/shard_map/ppermute | solution.py:30
  29.1 16.8 %copy-start.5 = (f32[640]{0:T(1024)S(1)}, f32[640]{0:T(1024)}, u32[]{:S(2)}) copy-start(f32[640]{0:T(1024)} %param.8) | copy-start | bytes 7684
  30.2 1.7 %collective-permute-start.10 = (bf16[8,32,640]{2,1,0:T(8,128)(2,1)S(1)}, bf16[8,32,640]{2,1,0:T(8,128)(2,1)S(1)}, u32[]{:S(2)}, u32[]{:S(2)}) collective-permute-start(bf16[8,32,640]{2,1,0:T(8,128)(2,1)S(1)} %get-tuple-element.12), channel_id=1, source_target_pairs={{0,1},{1,0},{2,3},{3,2},{4,5},{5,4},{6,7},{7,6},{8,9},{9,8},{10,11... | collective-permute-start | bytes 983048 | tf_op jit(solution)/shard_map/ppermute | solution.py:30
  32.0 6.3 %collective-permute-start.11 = (bf16[4,32,640]{2,1,0:T(8,128)(2,1)S(1)}, bf16[4,32,640]{2,1,0:T(8,128)(2,1)S(1)}, u32[]{:S(2)}, u32[]{:S(2)}) collective-permute-start(bf16[4,32,640]{2,1,0:T(8,128)(2,1)S(1)} %fusion.2), channel_id=1, source_target_pairs={{0,2},{2,0},{4,6},{6,4},{8,10},{10,8},{12,14},{14,12},{1,3},{3,1},... | collective-permute-start | bytes 491528 | tf_op jit(solution)/shard_map/ppermute | solution.py:30
  38.4 4.3 %collective-permute-start.12 = (bf16[1,32,640]{2,1,0:T(8,128)(2,1)S(1)}, bf16[1,32,640]{2,1,0:T(8,128)(2,1)S(1)}, u32[]{:S(2)}, u32[]{:S(2)}) collective-permute-start(bf16[1,32,640]{2,1,0:T(8,128)(2,1)S(1)} %get-tuple-element.15), channel_id=1, source_target_pairs={{0,4},{2,6},{4,0},{6,2},{8,12},{10,14},{12,8},{14,10},{1,5},{3,7},... | collective-permute-start | bytes 122888 | tf_op jit(solution)/shard_map/ppermute | solution.py:30
  38.5 5.9 %collective-permute-start.14 = (bf16[1,32,640]{2,1,0:T(8,128)(2,1)S(1)}, bf16[1,32,640]{2,1,0:T(8,128)(2,1)S(1)}, u32[]{:S(2)}, u32[]{:S(2)}) collective-permute-start(bf16[1,32,640]{2,1,0:T(8,128)(2,1)S(1)} %get-tuple-element.16), channel_id=1, source_target_pairs={{0,12},{2,14},{4,8},{6,10},{8,4},{10,6},{12,0},{14,2},{1,13},{3,15... | collective-permute-start | bytes 122888 | tf_op jit(solution)/shard_map/ppermute | solution.py:30
  40.6 5.3 %collective-permute-start.13 = (bf16[1,32,640]{2,1,0:T(8,128)(2,1)S(1)}, bf16[1,32,640]{2,1,0:T(8,128)(2,1)S(1)}, u32[]{:S(2)}, u32[]{:S(2)}) collective-permute-start(bf16[1,32,640]{2,1,0:T(8,128)(2,1)S(1)} %get-tuple-element.17), channel_id=1, source_target_pairs={{0,8},{2,10},{4,12},{6,14},{8,0},{10,2},{12,4},{14,6},{1,9},{3,11}... | collective-permute-start | bytes 122888 | tf_op jit(solution)/shard_map/ppermute | solution.py:30

commit v5 on v4

v5 whole, which is shorter than its diff:
```python
import jax
import jax.numpy as jnp
from jax import lax
from jax.experimental import pallas as pl
from jax.experimental.pallas import tpu as pltpu
from jax.sharding import PartitionSpec as P


LANES = 128
HEAD = 10**10
NT = (((1,), (1,)), ((), ()))
NN = (((1,), (0,)), ((), ()))
VMEM = pl.BlockSpec(memory_space=pltpu.VMEM)
SMEM = pl.BlockSpec(memory_space=pltpu.SMEM)
ANY = pl.BlockSpec(memory_space=pl.ANY)


def digits_of(count):
    digits, stride = [], 1
    bits = count.bit_length() - 1
    if bits % 2:
        digits.append((1, 2))
        stride = 2
    while stride < count:
        digits.append((stride, 4))
        stride *= 4
    return digits


def swap(x, axis, count, mask):
    return lax.ppermute(x, axis, [(i, i ^ mask) for i in range(count)])


def call(body, out_shape, in_specs, flops=0, scratch=(), limit=14):
    return pl.pallas_call(
        body,
        out_shape=out_shape,
        in_specs=in_specs,
        out_specs=jax.tree.map(lambda _: VMEM, out_shape),
        scratch_shapes=list(scratch),
        compiler_params=pltpu.CompilerParams(vmem_limit_bytes=limit * 2**20),
        cost_estimate=pl.CostEstimate(flops=flops, bytes_accessed=0, transcendentals=0),
    )


def after(body, count):
    return lambda *refs: body(*refs[:count], *refs[count + 1 :])


def shape(dims, dtype):
    return jax.ShapeDtypeStruct(dims, dtype)


class Plan:
    def __init__(self, sizes, trial, coulomb_factors, occ_values, vir_values):
        self.groups, self.blks, self.vecs = sizes
        self.rows, self.k = trial.shape
        self.aux = coulomb_factors.shape[0] // self.vecs
        self.pairs = coulomb_factors.shape[1] // self.groups
        self.batches = occ_values.shape[0] // self.vecs
        self.occ_all, self.points = occ_values.shape[1:]
        self.occs = self.occ_all // self.groups
        self.virs = vir_values.shape[2]
        self.aligned = self.rows % LANES == 0
        self.count = self.blks if self.aligned else 1
        self.length = self.rows if self.aligned else self.pairs // self.vecs
        self.per = self.length // LANES
        self.digits = digits_of(self.blks)
        stride, radix = self.digits[-1]
        self.top = stride
        if self.aligned and radix == 4 and len(self.digits) == 2 and self.occs % radix == 0:
            self.parts = [(2, 3), (0, 1)]
            self.run = self.occs // radix
        else:
            assert not self.aligned
            self.parts = [(0,)]
            self.run = self.occs

    def masks(self, part):
        if len(self.parts) == 1:
            return list(range(self.count))
        return [d * self.top + low for d in part for low in range(self.top)]

    def first_row(self, d):
        return (lax.axis_index("blk") // self.top ^ d) * self.run if len(self.parts) > 1 else 0

    def owner(self, m):
        return lax.axis_index("blk") ^ m if self.aligned else 0

    def part(self, h):
        return lax.axis_index("vec") ^ h if self.aligned else h

    def block(self, h, m, j):
        return (self.owner(m) * self.vecs + self.part(h)) * self.per + j

    def place(self, h, m, j):
        at = self.block(h, m, j)
        tiles = self.virs // LANES
        return (
            pl.ds(pl.multiple_of((at // tiles) * self.k, self.k), self.k),
            pl.ds(pl.multiple_of((at % tiles) * LANES, LANES), LANES),
        )


def copy_kernel(plan, given, out):
    out[...] = given[...]


def stack_kernel(plan, *refs):
    for m, piece in enumerate(refs[:-1]):
        refs[-1][m] = piece[...]


def occ_rows(plan, occ, b, occ32):
    occ32[...] = occ[lax.axis_index("vec") * plan.batches + b].astype(jnp.float32)
    base = lax.axis_index("grp") * plan.occs
    return lambda i: occ32[pl.ds(base + i, 1), :]


def factor_block(plan, fac, m, p):
    top = pl.multiple_of(lax.axis_index("vec") * plan.aux, plan.aux)
    at = lax.axis_index("grp") * plan.pairs + (plan.owner(m) * plan.vecs + p) * plan.length
    return fac[pl.ds(top, plan.aux), pl.ds(pl.multiple_of(at, LANES), plan.length)]


def rows_kernel(plan, mine, other, rows):
    for h, half in enumerate((mine, other)):
        for m in range(plan.count):
            for j in range(plan.per):
                rows[plan.place(h, m, j)] = half[m, :, j * LANES : (j + 1) * LANES]


def dens_kernel(plan, span, rows, vir, occ, dens, sent, occ32):
    k = plan.k
    vec = lax.axis_index("vec")
    for n, b in enumerate(span):
        row = occ_rows(plan, occ, b, occ32.at[n])
        trans = lax.dot_general(
            rows[...], vir[vec * plan.batches + b], NT, preferred_element_type=jnp.float32
        )
        total = row(0) * trans[:k, :]
        for i in range(1, plan.occs):
            total = total + row(i) * trans[i * k : (i + 1) * k, :]
        dens[n] = total
        sent[n] = total.astype(sent.dtype)


def first_dens_kernel(plan, span, mine, other, vir, occ, dens, sent, rows, occ32):
    rows_kernel(plan, mine, other, rows)
    dens_kernel(plan, span, rows, vir, occ, dens, sent, occ32)


def fac_kernel(plan, h, half, fac, *refs):
    value = refs[0][...] if len(refs) > 1 else 0.0
    for m in range(plan.count):
        value += lax.dot_general(
            half[m], factor_block(plan, fac, m, plan.part(h)), NT, preferred_element_type=jnp.float32
        )
    refs[-1][...] = value


def grid_kernel(plan, part, spans, live, *refs):
    count = len(spans)
    pairs = refs[: 2 * count]
    occ, weight, vir, acc, scaled, occ32 = refs[2 * count :]
    k = plan.k
    base = lax.axis_index("vec") * plan.batches
    slots = lax.broadcasted_iota(jnp.int32, (1, plan.points), 1)
    for c, span in enumerate(spans):
        for n, b in enumerate(span):
            row = occ_rows(plan, occ, b, occ32.at[b])
            density = pairs[2 * c][n] + pairs[2 * c + 1][n].astype(jnp.float32)
            used = jnp.where(slots < live[base + b], weight[pl.ds(base + b, 1), :], 0.0)
            weighted = density * used
            for t, d in enumerate(part):
                first = plan.first_row(d)
                for r in range(plan.run):
                    at = (t * plan.run + r) * k
                    scaled[at : at + k, :] = (row(first + r) * weighted).astype(jnp.bfloat16)
            value = lax.dot_general(
                scaled[...], vir[base + b], NN, preferred_element_type=jnp.float32
            )
            if b == 0:
                acc[...] = value
            else:
                acc[...] += value


def back_kernel(plan, part, part_a, part_b, fac, acc, stay, sent):
    both = (part_a[...] + part_b[...]).astype(jnp.bfloat16)
    k, tiles = plan.k, plan.virs // LANES
    masks = plan.masks(part)
    for n, m in enumerate(masks):
        t = n * len(part) // len(masks)
        first = plan.first_row(part[t])
        for h, out in enumerate((stay, sent)):
            value = 2.0 * lax.dot_general(
                both,
                factor_block(plan, fac, m, plan.part(h)),
                NN,
                preferred_element_type=jnp.float32,
            )
            for j in range(plan.per):
                at = plan.block(h, m, j)
                row = (at // tiles - first + t * plan.run) * k
                found = acc[
                    pl.ds(pl.multiple_of(row, k), k),
                    pl.ds(pl.multiple_of((at % tiles) * LANES, LANES), LANES),
                ]
                lanes = slice(j * LANES, (j + 1) * LANES)
                out[n, :, lanes] = (value[:, lanes] + found).astype(out.dtype)


def sum_kernel(plan, radix, stay, came, *outs):
    for n in range(stay.shape[0]):
        out = outs[n % radix]
        out[n // radix] = (stay[n] + came[n].astype(jnp.float32)).astype(out.dtype)


def split_kernel(plan, own, *refs):
    outs = refs[-own.shape[0] :]
    for n, out in enumerate(outs):
        total = own[n]
        for came in refs[: -len(outs)]:
            total = total + came[n].astype(jnp.float32)
        out[...] = total.astype(out.dtype)


def local(trial, energy_gap, coulomb_factors, occ_values, vir_values, kernel, live_points, sizes):
    plan = Plan(sizes, trial, coulomb_factors, occ_values, vir_values)
    groups, blks, vecs, k = plan.groups, plan.blks, plan.vecs, plan.k
    batches, points, virs, occs = plan.batches, plan.points, plan.virs, plan.occs
    digits = plan.digits
    half = (plan.count, k, plan.length)
    bf16, f32 = jnp.bfloat16, jnp.float32

    def bind(body, *first):
        return lambda *refs: body(plan, *first, *refs)

    trial_cols = trial.T
    pieces, masks = [trial_cols], [0]
    for stride, radix in reversed(digits):
        known = len(masks)
        for d in range(1, radix):
            for n in range(known):
                pieces.append(swap(pieces[n], "blk", blks, d * stride))
                masks.append(masks[n] ^ (d * stride))
        if known == 1:
            pieces[-1] = call(
                bind(copy_kernel), shape(trial_cols.shape, bf16), [VMEM], flops=HEAD
            )(pieces[-1])
    pieces = [p for _, p in sorted(zip(masks, pieces), key=lambda pair: pair[0])]

    if plan.aligned:
        mine = call(bind(stack_kernel), shape(half, bf16), [VMEM] * len(pieces))(*pieces)
        other = swap(mine, "vec", vecs, 1)
    else:
        me, vec = lax.axis_index("blk"), lax.axis_index("vec")
        mine = jnp.take(jnp.stack(pieces), me ^ jnp.arange(blks), axis=0)
        both = jnp.stack([mine, swap(mine, "vec", vecs, 1)])
        both = jnp.take(both, vec ^ jnp.arange(vecs), axis=0)
        both = both.transpose(2, 1, 0, 3).reshape(k, vecs, plan.length)
        mine, other = both[None, :, 0], both[None, :, 1]

    flops = k * plan.aux * plan.pairs
    part = call(bind(fac_kernel, 0), shape((k, plan.aux), f32), [VMEM] * 2, flops)(
        mine, coulomb_factors
    )

    cut = (batches + 1) // 2
    spans = [tuple(range(cut)), tuple(range(cut, batches))]
    grid_flops = 2 * points * virs * occs * k
    occ_scratch = pltpu.VMEM((batches, plan.occ_all, points), f32)
    rows = None
    density = []
    for span in spans:
        chunk = (len(span), k, points)
        out = (shape(chunk, f32), shape(chunk, bf16))
        if rows is None:
            dens, sent, rows = call(
                after(bind(first_dens_kernel, span), 4),
                out + (shape((occs * k, virs), bf16),),
                [VMEM] * 4 + [ANY],
                grid_flops * len(span),
                [occ_scratch],
            )(mine, other, vir_values, occ_values, part)
        else:
            dens, sent = call(
                bind(dens_kernel, span), out, [VMEM] * 3, grid_flops * len(span), [occ_scratch]
            )(rows, vir_values, occ_values)
        density += [dens, swap(sent, "grp", groups, 1)]

    part = call(bind(fac_kernel, 1), shape((k, plan.aux), f32), [VMEM] * 3, flops)(
        other, coulomb_factors, part
    )
    other_part = swap(part, "grp", groups, 1)

    def grid(number, *order):
        chosen = plan.parts[number]
        used = plan.run * len(chosen)
        body = bind(grid_kernel, chosen, spans)
        return call(
            after(body, len(density) + 4) if order else body,
            shape((used * k, virs), f32),
            [SMEM] + [VMEM] * (len(density) + 3) + [ANY] * len(order),
            grid_flops * batches * used // occs,
            [pltpu.VMEM((used * k, points), bf16), occ_scratch],
        )(live_points, *density, occ_values, kernel, vir_values, *order)

    def back(number, acc, *order):
        chosen = plan.parts[number]
        share = (len(plan.masks(chosen)),) + half[1:]
        body = bind(back_kernel, chosen)
        return call(
            after(body, 4) if order else body,
            (shape(share, f32), shape(share, bf16)),
            [VMEM] * 4 + [ANY] * len(order),
            2 * flops // len(plan.parts),
        )(part, other_part, coulomb_factors, acc, *order)

    if len(plan.parts) == 2:
        (stride, radix), (top, _) = digits
        count = plan.count // 2

        def first_sum(stay, sent, *order):
            body = bind(sum_kernel, radix)
            return call(
                after(body, 2) if order else body,
                (shape((count // radix,) + half[1:], f32),)
                + (shape((count // radix,) + half[1:], bf16),) * (radix - 1),
                [VMEM] * 2 + [ANY] * len(order),
            )(stay, swap(sent, "vec", vecs, 1), *order)

        def next_sum(number, own, sends):
            came = [swap(x, "blk", blks, (d + 1) * stride) for d, x in enumerate(sends)]
            out = [shape(half[1:], bf16 if d else f32) for d in plan.parts[number]]
            outs = call(bind(split_kernel), out, [VMEM] * (1 + len(came)))(own, *came)
            return [
                swap(x, "blk", blks, d * top) if d else x
                for d, x in zip(plan.parts[number], outs)
            ]

        acc = grid(0)
        stay, sent = back(0, acc)
        acc = grid(1, stay)
        far = first_sum(stay, sent, acc)
        stay, sent = back(1, acc, far[0])
        near = first_sum(stay, sent)
        came = next_sum(0, far[0], far[1:]) + next_sum(1, near[0], near[1:])
    else:
        stay, sent = back(0, grid(0))
        full = jnp.concatenate([stay[0], sent[0].astype(f32)], axis=1)
        full = full.reshape(k, blks, vecs, plan.rows).transpose(2, 1, 0, 3)
        full = jnp.take(full, me ^ jnp.arange(blks), axis=1)
        full = jnp.take(full, vec ^ jnp.arange(vecs), axis=0)
        total = full[0] + swap(full[1].astype(bf16), "vec", vecs, 1).astype(f32)
        for stride, radix in digits:
            total = total.reshape((-1, radix) + total.shape[1:])
            total = sum(
                (
                    swap(total[:, d].astype(bf16), "blk", blks, d * stride).astype(f32)
                    for d in range(1, radix)
                ),
                total[:, 0],
            )
        came = [total[0]]
    total = sum((x.astype(f32) for x in came[1:]), came[0].astype(f32))
    result = energy_gap[None, :] * trial_cols.astype(f32) + total
    return result.astype(bf16).T


def solution(mesh):
    sizes = tuple(mesh.shape[a] for a in ("grp", "blk", "vec"))
    in_specs = (
        P(("grp", "blk", "vec"), None),
        P(("grp", "blk", "vec")),
        P("blk", None),
        P("blk", None, None),
        P("blk", None, None),
        P("blk", None),
        P("blk"),
    )
    out_specs = P(("grp", "blk", "vec"), None)

    def program(*args):
        return local(*args, sizes=sizes)

    return jax.shard_map(
        program, mesh=mesh, in_specs=in_specs, out_specs=out_specs, check_vma=False
    )
```

time: 46.7 us -> 43.6 us (0.934)
  waiting for transfers between devices: 19.5 us -> 13 us
  starting transfers between devices: 17.7 us -> 20.9 us
  Pallas kernels: 7.63 us -> 8.69 us
  local copies, waits for them, and re-layouts: 0.85 us -> 0.05 us
    ppermute x15 -> x18, waiting for transfers between devices: 19.5 us -> 13 us  [swap(): return lax.ppermute(x, axis, [(i, i ^ mask) for i in range(count)])]
    ppermute x15 -> x18, starting transfers between devices: 17.7 us -> 20.9 us  [swap(): return lax.ppermute(x, axis, [(i, i ^ mask) for i in range(count)])]
    pallas_call x6 -> x14, Pallas kernels: 7.63 us -> 8.69 us  [the longest x2 3.1 us: grid(): call(after(body, len(density) + 4) if order else body, shape((used * k, v...]
    unnamed x16, local copies, waits for them, and re-layouts: 0.81 us -> 0.05 us
  transfers between devices with their start and end apart: 15 -> 18, of which waited for: 10 -> 9; matrix products, arithmetic and copies ran while one was open for 0% -> 0% of each run, Pallas kernels for 9% -> 13%
where the time goes in v5:
time: 43.6 us; the launch traced here: 43.4 us
  starting transfers between devices  20.9 us (48%)
  waiting for transfers between devices  13 us (30%)
  Pallas kernels  8.69 us (20%)
  other arithmetic  0.65 us (1%)
    ppermute x18, starting transfers between devices, swap(): return lax.ppermute(x, axis, [(i, i ^ mask) for i in range(count)])  20.9 us
    ppermute x18, waiting for transfers between devices, swap(): return lax.ppermute(x, axis, [(i, i ^ mask) for i in range(count)])  13 us
    pallas_call x2, Pallas kernels, grid(): call(after(body, len(density) + 4) if order else body, shape((used * k, v...  3.1 us
    pallas_call x1, Pallas kernels, local(): call(after(bind(first_dens_kernel, span), 4), out + (shape((occs * k, vir...  1.78 us
    pallas_call x2, Pallas kernels, back(): call(after(body, 4) if order else body, (shape(share, f32), shape(share,...  1.07 us
    pallas_call x1, Pallas kernels, local(): call(bind(dens_kernel, span), out, [VMEM] * 3, grid_flops * len(span), [o...  0.88 us
  transfers between devices with their start and end apart: 18, of which 9 were waited for; matrix products, arithmetic and copies ran while one was open for 0% of the time, Pallas kernels for 13%

profile of v5, /device:TPU:0, one launch (start us, length us, event | category | flops | bytes accessed | tf_op | source)
XLA Modules:
  0.0 43.4 jit_solution(616935900453409845)
XLA Ops:
  0.0 0.0 copy-start.2
  0.0 0.0 copy-start
  0.0 0.0 slice-start
  0.0 0.0 slice-start.1
  0.0 0.0 copy-start.1
  0.0 5.2 %collective-permute-start.5 = (bf16[32,640]{1,0:T(8,128)(2,1)}, bf16[32,640]{1,0:T(8,128)(2,1)S(1)}, u32[]{:S(2)}, u32[]{:S(2)}) collective-permute-start(bf16[32,640]{1,0:T(8,128)(2,1)} %bitcast.6), channel_id=1, source_target_pairs={{0,12},{2,14},{4,8},{6,10},{8,4},{10,6},{12,0},{14,2},{1,13},{3,15... | collective-permute-start | bytes 122888 | tf_op jit(solution)/shard_map/ppermute | solution.py:31
  5.2 0.0 collective-permute-start.3
  5.2 0.6 %collective-permute-start.1 = (bf16[32,640]{1,0:T(8,128)(2,1)}, bf16[32,640]{1,0:T(8,128)(2,1)S(1)}, u32[]{:S(2)}, u32[]{:S(2)}) collective-permute-start(bf16[32,640]{1,0:T(8,128)(2,1)} %bitcast.8), channel_id=1, source_target_pairs={{0,4},{2,6},{4,0},{6,2},{8,12},{10,14},{12,8},{14,10},{1,5},{3,7},... | collective-permute-start | bytes 122888 | tf_op jit(solution)/shard_map/ppermute | solution.py:31
  5.8 1.7 %collective-permute-start = (bf16[32,640]{1,0:T(8,128)(2,1)}, bf16[32,640]{1,0:T(8,128)(2,1)S(1)}, u32[]{:S(2)}, u32[]{:S(2)}) collective-permute-start(bf16[32,640]{1,0:T(8,128)(2,1)} %bitcast.9), channel_id=1, source_target_pairs={{0,2},{2,0},{4,6},{6,4},{8,10},{10,8},{12,14},{14,12},{1,3},{3,1},... | collective-permute-start | bytes 122888 | tf_op jit(solution)/shard_map/ppermute | solution.py:31
  7.5 0.0 collective-permute-done.5.refs_0_
  7.5 1.8 %collective-permute-start.6 = (bf16[32,640]{1,0:T(8,128)(2,1)S(1)}, bf16[32,640]{1,0:T(8,128)(2,1)S(1)}, u32[]{:S(2)}, u32[]{:S(2)}) collective-permute-start(bf16[32,640]{1,0:T(8,128)(2,1)S(1)} %shard_map.73.refs_6_), channel_id=1, source_target_pairs={{0,2},{2,0},{4,6},{6,4},{8,10},{10,8},{12,14},{14,12},{1,3},{3,1},... | collective-permute-start | bytes 122888 | tf_op jit(solution)/shard_map/ppermute | solution.py:31
  9.3 1.0 %collective-permute-done.3.refs_4_ = bf16[32,640]{1,0:T(8,128)(2,1)S(1)} collective-permute-done((bf16[32,640]{1,0:T(8,128)(2,1)}, bf16[32,640]{1,0:T(8,128)(2,1)S(1)}, u32[]{:S(2)}, u32[]{:S(2)}) %collective-permute-start.3) | collective-permute-done | bytes 40992 | tf_op jit(solution)/shard_map/ppermute | solution.py:31
  10.3 1.5 %collective-permute-start.4 = (bf16[32,640]{1,0:T(8,128)(2,1)S(1)}, bf16[32,640]{1,0:T(8,128)(2,1)S(1)}, u32[]{:S(2)}, u32[]{:S(2)}) collective-permute-start(bf16[32,640]{1,0:T(8,128)(2,1)S(1)} %collective-permute-done.3.refs_4_), channel_id=1, source_target_pairs={{0,2},{2,0},{4,6},{6,4},{8,10},{10,8},{12,14},{14,12},{1,3},{3,1},... | collective-permute-start | bytes 122888 | tf_op jit(solution)/shard_map/ppermute | solution.py:31
  11.8 0.0 collective-permute-done.1.refs_2_
  11.8 0.5 %collective-permute-start.2 = (bf16[32,640]{1,0:T(8,128)(2,1)S(1)}, bf16[32,640]{1,0:T(8,128)(2,1)S(1)}, u32[]{:S(2)}, u32[]{:S(2)}) collective-permute-start(bf16[32,640]{1,0:T(8,128)(2,1)S(1)} %collective-permute-done.1.refs_2_), channel_id=1, source_target_pairs={{0,2},{2,0},{4,6},{6,4},{8,10},{10,8},{12,14},{14,12},{1,3},{3,1},... | collective-permute-start | bytes 122888 | tf_op jit(solution)/shard_map/ppermute | solution.py:31
  12.3 0.0 collective-permute-done.refs_1_
  12.3 0.0 collective-permute-done.6.refs_7_
  12.3 2.0 %collective-permute-done.4.refs_5_ = bf16[32,640]{1,0:T(8,128)(2,1)S(1)} collective-permute-done((bf16[32,640]{1,0:T(8,128)(2,1)S(1)}, bf16[32,640]{1,0:T(8,128)(2,1)S(1)}, u32[]{:S(2)}, u32[]{:S(2)}) %collective-permute-start.4) | collective-permute-done | bytes 40992 | tf_op jit(solution)/shard_map/ppermute | solution.py:31
  14.3 1.5 %collective-permute-done.2.refs_3_ = bf16[32,640]{1,0:T(8,128)(2,1)S(1)} collective-permute-done((bf16[32,640]{1,0:T(8,128)(2,1)S(1)}, bf16[32,640]{1,0:T(8,128)(2,1)S(1)}, u32[]{:S(2)}, u32[]{:S(2)}) %collective-permute-start.2) | collective-permute-done | bytes 40992 | tf_op jit(solution)/shard_map/ppermute | solution.py:31
  15.8 0.0 copy-done.2
  15.8 0.1 collective-permute-start.7
  15.9 0.0 copy-done
  15.9 0.9 %shard_map.75.refs_2_.refs_4_ = f32[32,256]{1,0:T(8,128)S(1)} custom-call(bf16[8,32,640]{2,1,0:T(8,128)(2,1)S(1)} %shard_map.74.refs_0_, bf16[512,20480]{1,0:T(8,128)(2,1)S(1)} %copy-done), custom_call_target="tpu_custom_call" | custom-call | flops 83886080 | tf_op jit(solution)/shard_map/pallas_call | solution.py:266
  16.8 0.0 copy-start.3
  16.8 0.0 copy-start.4
  16.8 0.7 %collective-permute-done.7.refs_0_.refs_1_ = bf16[8,32,640]{2,1,0:T(8,128)(2,1)S(1)} collective-permute-done((bf16[8,32,640]{2,1,0:T(8,128)(2,1)S(1)}, bf16[8,32,640]{2,1,0:T(8,128)(2,1)S(1)}, u32[]{:S(2)}, u32[]{:S(2)}) %collective-permute-start.7) | collective-permute-done | bytes 327712 | tf_op jit(solution)/shard_map/ppermute | solution.py:31
  17.5 0.0 slice-done
  17.5 0.0 slice-done.1
  17.5 0.0 copy-done.1
  17.6 1.8 %shard_map.77 = (f32[3,32,512]{2,1,0:T(8,128)S(1)}, bf16[3,32,512]{2,1,0:T(8,128)(2,1)S(1)}, bf16[640,512]{1,0:T(8,128)(2,1)S(1)}) custom-call(bf16[8,32,640]{2,1,0:T(8,128)(2,1)S(1)} %shard_map.74.refs_0_, bf16[8,32,640]{2,1,0:T(8,128)(2,1)S(1)} %collective-permute-done.7.refs_0_.refs_1_, bf16[10,512,512]{2,1,0:T(8,128)(2,1)S(1)} %bitcast.5, ...), custom_call_target="tpu_custom_call" | custom-call | flops 1006632960 | tf_op jit(solution)/shard_map/pallas_call | solution.py:280
  19.3 1.6 %collective-permute-start.9 = (bf16[3,32,512]{2,1,0:T(8,128)(2,1)S(1)}, bf16[3,32,512]{2,1,0:T(8,128)(2,1)S(1)}, u32[]{:S(2)}, u32[]{:S(2)}) collective-permute-start(bf16[3,32,512]{2,1,0:T(8,128)(2,1)S(1)} %get-tuple-element.23), channel_id=1, source_target_pairs={{0,16},{16,0},{1,17},{17,1},{2,18},{18,2},{3,19},{19,3},{4,20},{20... | collective-permute-start | bytes 294920 | tf_op jit(solution)/shard_map/ppermute | solution.py:31
  20.9 0.9 %shard_map.78 = (f32[2,32,512]{2,1,0:T(8,128)S(1)}, bf16[2,32,512]{2,1,0:T(8,128)(2,1)S(1)}) custom-call(bf16[640,512]{1,0:T(8,128)(2,1)S(1)} %get-tuple-element.24.refs_0_, bf16[10,512,512]{2,1,0:T(8,128)(2,1)S(1)} %bitcast.5, bf16[10,40,512]{2,1,0:T(8,128)(2,1)S(1)} %copy-done.1), custom_call_target="tpu_custom_call" | custom-call | flops 671088640 | tf_op jit(solution)/shard_map/pallas_call | solution.py:288
  21.8 0.6 %collective-permute-start.10 = (bf16[2,32,512]{2,1,0:T(8,128)(2,1)S(1)}, bf16[2,32,512]{2,1,0:T(8,128)(2,1)S(1)}, u32[]{:S(2)}, u32[]{:S(2)}) collective-permute-start(bf16[2,32,512]{2,1,0:T(8,128)(2,1)S(1)} %get-tuple-element.26), channel_id=1, source_target_pairs={{0,16},{16,0},{1,17},{17,1},{2,18},{18,2},{3,19},{19,3},{4,20},{20... | collective-permute-start | bytes 196616 | tf_op jit(solution)/shard_map/ppermute | solution.py:31
  22.4 0.8 %shard_map.76.refs_0_ = f32[32,256]{1,0:T(8,128)S(1)} custom-call(bf16[8,32,640]{2,1,0:T(8,128)(2,1)S(1)} %collective-permute-done.7.refs_0_.refs_1_, bf16[512,20480]{1,0:T(8,128)(2,1)S(1)} %copy-done, f32[32,256]{1,0:T(8,128)S(1)} %shard_map.75.refs_2_.refs_4_), custom_call_target="tpu_custom_call" | custom-call | flops 83886080 | tf_op jit(solution)/shard_map/pallas_call | solution.py:293
  23.2 1.5 %collective-permute-start.8 = (f32[32,256]{1,0:T(8,128)S(1)}, f32[32,256]{1,0:T(8,128)S(1)}, u32[]{:S(2)}, u32[]{:S(2)}) collective-permute-start(f32[32,256]{1,0:T(8,128)S(1)} %shard_map.76.refs_0_), channel_id=1, source_target_pairs={{0,16},{16,0},{1,17},{17,1},{2,18},{18,2},{3,19},{19,3},{4,20},{20... | collective-permute-start | bytes 98312 | tf_op jit(solution)/shard_map/ppermute | solution.py:31
  24.8 1.7 %collective-permute-done.10.refs_4_ = bf16[2,32,512]{2,1,0:T(8,128)(2,1)S(1)} collective-permute-done((bf16[2,32,512]{2,1,0:T(8,128)(2,1)S(1)}, bf16[2,32,512]{2,1,0:T(8,128)(2,1)S(1)}, u32[]{:S(2)}, u32[]{:S(2)}) %collective-permute-start.10) | collective-permute-done | bytes 65568 | tf_op jit(solution)/shard_map/ppermute | solution.py:31
  26.5 0.0 collective-permute-done.9.refs_2_
  26.5 0.0 copy-done.3
  26.5 0.0 copy-done.4
  26.5 1.6 %shard_map.79.refs_3_ = f32[320,512]{1,0:T(8,128)S(1)} custom-call(s32[10]{0:T(128)S(1)} %copy-done.4, f32[3,32,512]{2,1,0:T(8,128)S(1)} %get-tuple-element.22.refs_1_, bf16[3,32,512]{2,1,0:T(8,128)(2,1)S(1)} %collective-permute-done.9.refs_2_, f32[2,32,512]{2,1,0:T(8,128)S(1)} %get-tuple-element.25.refs_3_, ...), custom_call_target="tpu_custom_call" | custom-call | flops 838860800 | tf_op jit(solution)/shard_map/pallas_call | solution.py:302
  28.0 0.0 collective-permute-done.8.refs_1_
  28.1 0.5 %shard_map.80 = (f32[4,32,640]{2,1,0:T(8,128)S(1)}, bf16[4,32,640]{2,1,0:T(8,128)(2,1)S(1)}) custom-call(f32[32,256]{1,0:T(8,128)S(1)} %shard_map.76.refs_0_, f32[32,256]{1,0:T(8,128)S(1)} %collective-permute-done.8.refs_1_, bf16[512,20480]{1,0:T(8,128)(2,1)S(1)} %copy-done, f32[320,512]{1,0:T(8,128)S(1)} %shard_map.79.refs_3_), custom_call_target="tpu_custom_call" | custom-call | flops 83886080 | tf_op jit(solution)/shard_map/pallas_call | solution.py:314
  28.6 0.0 copy-start.5
  28.6 0.1 collective-permute-start.11
  28.7 1.6 %shard_map.81.refs_2_.refs_3_ = f32[320,512]{1,0:T(8,128)S(1)} custom-call(s32[10]{0:T(128)S(1)} %copy-done.4, f32[3,32,512]{2,1,0:T(8,128)S(1)} %get-tuple-element.22.refs_1_, bf16[3,32,512]{2,1,0:T(8,128)(2,1)S(1)} %collective-permute-done.9.refs_2_, f32[2,32,512]{2,1,0:T(8,128)S(1)} %get-tuple-element.25.refs_3_, ...), custom_call_target="tpu_custom_call" | custom-call | flops 838860800 | tf_op jit(solution)/shard_map/pallas_call | solution.py:302
  30.2 0.0 collective-permute-done.11.refs_1_
  30.3 0.5 %shard_map.84 = (f32[4,32,640]{2,1,0:T(8,128)S(1)}, bf16[4,32,640]{2,1,0:T(8,128)(2,1)S(1)}) custom-call(f32[32,256]{1,0:T(8,128)S(1)} %shard_map.76.refs_0_, f32[32,256]{1,0:T(8,128)S(1)} %collective-permute-done.8.refs_1_, bf16[512,20480]{1,0:T(8,128)(2,1)S(1)} %copy-done, f32[320,512]{1,0:T(8,128)S(1)} %shard_map.81.refs_2_.refs_3_, ...), custom_call_target="tpu_custom_call" | custom-call | flops 83886080 | tf_op jit(solution)/shard_map/pallas_call | solution.py:314
  30.8 0.6 %collective-permute-start.15 = (bf16[4,32,640]{2,1,0:T(8,128)(2,1)S(1)}, bf16[4,32,640]{2,1,0:T(8,128)(2,1)S(1)}, u32[]{:S(2)}, u32[]{:S(2)}) collective-permute-start(bf16[4,32,640]{2,1,0:T(8,128)(2,1)S(1)} %get-tuple-element.34), channel_id=1, source_target_pairs={{0,1},{1,0},{2,3},{3,2},{4,5},{5,4},{6,7},{7,6},{8,9},{9,8},{10,11... | collective-permute-start | bytes 491528 | tf_op jit(solution)/shard_map/ppermute | solution.py:31
  31.4 0.5 %collective-permute-start.12 = (bf16[2,32,640]{2,1,0:T(8,128)(2,1)S(1)}, bf16[2,32,640]{2,1,0:T(8,128)(2,1)S(1)}, u32[]{:S(2)}, u32[]{:S(2)}) collective-permute-start(bf16[2,32,640]{2,1,0:T(8,128)(2,1)S(1)} %get-tuple-element.30), channel_id=1, source_target_pairs={{0,2},{2,0},{4,6},{6,4},{8,10},{10,8},{12,14},{14,12},{1,3},{3,1},... | collective-permute-start | bytes 245768 | tf_op jit(solution)/shard_map/ppermute | solution.py:31
  31.9 0.5 %collective-permute-done.15.refs_1_ = bf16[4,32,640]{2,1,0:T(8,128)(2,1)S(1)} collective-permute-done((bf16[4,32,640]{2,1,0:T(8,128)(2,1)S(1)}, bf16[4,32,640]{2,1,0:T(8,128)(2,1)S(1)}, u32[]{:S(2)}, u32[]{:S(2)}) %collective-permute-start.15) | collective-permute-done | bytes 163872 | tf_op jit(solution)/shard_map/ppermute | solution.py:31
  32.5 1.1 %collective-permute-start.16 = (bf16[2,32,640]{2,1,0:T(8,128)(2,1)S(1)}, bf16[2,32,640]{2,1,0:T(8,128)(2,1)S(1)}, u32[]{:S(2)}, u32[]{:S(2)}) collective-permute-start(bf16[2,32,640]{2,1,0:T(8,128)(2,1)S(1)} %get-tuple-element.36), channel_id=1, source_target_pairs={{0,2},{2,0},{4,6},{6,4},{8,10},{10,8},{12,14},{14,12},{1,3},{3,1},... | collective-permute-start | bytes 245768 | tf_op jit(solution)/shard_map/ppermute | solution.py:31
  33.6 2.7 %collective-permute-done.12.refs_1_ = bf16[2,32,640]{2,1,0:T(8,128)(2,1)S(1)} collective-permute-done((bf16[2,32,640]{2,1,0:T(8,128)(2,1)S(1)}, bf16[2,32,640]{2,1,0:T(8,128)(2,1)S(1)}, u32[]{:S(2)}, u32[]{:S(2)}) %collective-permute-start.12) | collective-permute-done | bytes 81952 | tf_op jit(solution)/shard_map/ppermute | solution.py:31
  36.2 0.7 %collective-permute-start.13 = (bf16[32,640]{1,0:T(8,128)(2,1)S(1)}, bf16[32,640]{1,0:T(8,128)(2,1)S(1)}, u32[]{:S(2)}, u32[]{:S(2)}) collective-permute-start(bf16[32,640]{1,0:T(8,128)(2,1)S(1)} %get-tuple-element.31), channel_id=1, source_target_pairs={{0,8},{2,10},{4,12},{6,14},{8,0},{10,2},{12,4},{14,6},{1,9},{3,11}... | collective-permute-start | bytes 122888 | tf_op jit(solution)/shard_map/ppermute | solution.py:31
  36.9 1.3 %collective-permute-start.14 = (bf16[32,640]{1,0:T(8,128)(2,1)S(1)}, bf16[32,640]{1,0:T(8,128)(2,1)S(1)}, u32[]{:S(2)}, u32[]{:S(2)}) collective-permute-start(bf16[32,640]{1,0:T(8,128)(2,1)S(1)} %get-tuple-element.32), channel_id=1, source_target_pairs={{0,12},{2,14},{4,8},{6,10},{8,4},{10,6},{12,0},{14,2},{1,13},{3,15... | collective-permute-start | bytes 122888 | tf_op jit(solution)/shard_map/ppermute | solution.py:31
  38.2 0.0 collective-permute-done.16.refs_1_
  38.3 1.6 %collective-permute-start.17 = (bf16[32,640]{1,0:T(8,128)(2,1)S(1)}, bf16[32,640]{1,0:T(8,128)(2,1)S(1)}, u32[]{:S(2)}, u32[]{:S(2)}) collective-permute-start(bf16[32,640]{1,0:T(8,128)(2,1)S(1)} %get-tuple-element.38), channel_id=1, source_target_pairs={{0,4},{2,6},{4,0},{6,2},{8,12},{10,14},{12,8},{14,10},{1,5},{3,7},... | collective-permute-start | bytes 122888 | tf_op jit(solution)/shard_map/ppermute | solution.py:31
  39.9 1.3 %collective-permute-done.13 = bf16[32,640]{1,0:T(8,128)(2,1)S(1)} collective-permute-done((bf16[32,640]{1,0:T(8,128)(2,1)S(1)}, bf16[32,640]{1,0:T(8,128)(2,1)S(1)}, u32[]{:S(2)}, u32[]{:S(2)}) %collective-permute-start.13) | collective-permute-done | bytes 40992 | tf_op jit(solution)/shard_map/ppermute | solution.py:31
  41.2 1.6 %collective-permute-done.14 = bf16[32,640]{1,0:T(8,128)(2,1)S(1)} collective-permute-done((bf16[32,640]{1,0:T(8,128)(2,1)S(1)}, bf16[32,640]{1,0:T(8,128)(2,1)S(1)}, u32[]{:S(2)}, u32[]{:S(2)}) %collective-permute-start.14) | collective-permute-done | bytes 40992 | tf_op jit(solution)/shard_map/ppermute | solution.py:31
  42.8 0.0 collective-permute-done.17
  42.8 0.0 copy-done.5
  42.8 0.7 %fusion = bf16[640,32]{0,1:T(8,128)(2,1)} fusion(bf16[32,640]{1,0:T(8,128)(2,1)S(1)} %collective-permute-done.17, f32[32,640]{1,0:T(8,128)S(1)} %get-tuple-element.37, bf16[32,640]{1,0:T(8,128)(2,1)S(1)} %collective-permute-done.14, bf16[32,640]{1,0:T(8,128)(2,1)S(1)} %collective-permute-done.13, f32[640]{0:T(1024)S(1)} %copy-done.5, ...), kind=kLoop, calls=%fused_computation.1 | loop fusion | flops 204800 | bytes 289280 | tf_op jit(solution)/shard_map/transpose | solution.py:369
  (7 shorter events, 0.1 us)
Async XLA Ops:
  0.0 15.8 %copy-start.2 = (bf16[640,32]{0,1:T(8,128)(2,1)S(1)}, bf16[640,32]{0,1:T(8,128)(2,1)}, u32[]{:S(2)}) copy-start(bf16[640,32]{0,1:T(8,128)(2,1)} %param.7) | copy-start | bytes 122884
  0.0 15.9 %copy-start = (bf16[512,20480]{1,0:T(8,128)(2,1)S(1)}, bf16[512,20480]{1,0:T(8,128)(2,1)}, u32[]{:S(2)}) copy-start(bf16[512,20480]{1,0:T(8,128)(2,1)} %refs_2_.7) | copy-start | bytes 62914564
  0.0 17.5 %slice-start = ((s8[5242880]{0:T(1024)(128)(4,1)}), s8[4194304]{0:T(1024)(128)(4,1)S(1)}, s32[]{:S(2)}) async-start(s8[5242880]{0:T(1024)(128)(4,1)} %bitcast.4), calls=%async_computation | async-start | bytes 8388608
  0.0 17.5 %slice-start.1 = ((s8[5242880]{0:T(1024)(128)(4,1)}), s8[1048576]{0:T(1024)(128)(4,1)S(1)}, s32[]{:S(2)}) async-start(s8[5242880]{0:T(1024)(128)(4,1)} %bitcast.4), calls=%async_computation.1 | async-start | bytes 2097152
  0.0 17.5 %copy-start.1 = (bf16[10,40,512]{2,1,0:T(8,128)(2,1)S(1)}, bf16[10,40,512]{2,1,0:T(8,128)(2,1)}, u32[]{:S(2)}) copy-start(bf16[10,40,512]{2,1,0:T(8,128)(2,1)} %refs_5_.3) | copy-start | bytes 1228804
  0.0 7.5 %collective-permute-start.5 = (bf16[32,640]{1,0:T(8,128)(2,1)}, bf16[32,640]{1,0:T(8,128)(2,1)S(1)}, u32[]{:S(2)}, u32[]{:S(2)}) collective-permute-start(bf16[32,640]{1,0:T(8,128)(2,1)} %bitcast.6), channel_id=1, source_target_pairs={{0,12},{2,14},{4,8},{6,10},{8,4},{10,6},{12,0},{14,2},{1,13},{3,15... | collective-permute-start | bytes 122888 | tf_op jit(solution)/shard_map/ppermute | solution.py:31
  5.2 5.1 %collective-permute-start.3 = (bf16[32,640]{1,0:T(8,128)(2,1)}, bf16[32,640]{1,0:T(8,128)(2,1)S(1)}, u32[]{:S(2)}, u32[]{:S(2)}) collective-permute-start(bf16[32,640]{1,0:T(8,128)(2,1)} %bitcast.7), channel_id=1, source_target_pairs={{0,8},{2,10},{4,12},{6,14},{8,0},{10,2},{12,4},{14,6},{1,9},{3,11}... | collective-permute-start | bytes 122888 | tf_op jit(solution)/shard_map/ppermute | solution.py:31
  5.2 6.6 %collective-permute-start.1 = (bf16[32,640]{1,0:T(8,128)(2,1)}, bf16[32,640]{1,0:T(8,128)(2,1)S(1)}, u32[]{:S(2)}, u32[]{:S(2)}) collective-permute-start(bf16[32,640]{1,0:T(8,128)(2,1)} %bitcast.8), channel_id=1, source_target_pairs={{0,4},{2,6},{4,0},{6,2},{8,12},{10,14},{12,8},{14,10},{1,5},{3,7},... | collective-permute-start | bytes 122888 | tf_op jit(solution)/shard_map/ppermute | solution.py:31
  5.8 6.5 %collective-permute-start = (bf16[32,640]{1,0:T(8,128)(2,1)}, bf16[32,640]{1,0:T(8,128)(2,1)S(1)}, u32[]{:S(2)}, u32[]{:S(2)}) collective-permute-start(bf16[32,640]{1,0:T(8,128)(2,1)} %bitcast.9), channel_id=1, source_target_pairs={{0,2},{2,0},{4,6},{6,4},{8,10},{10,8},{12,14},{14,12},{1,3},{3,1},... | collective-permute-start | bytes 122888 | tf_op jit(solution)/shard_map/ppermute | solution.py:31
  7.5 4.8 %collective-permute-start.6 = (bf16[32,640]{1,0:T(8,128)(2,1)S(1)}, bf16[32,640]{1,0:T(8,128)(2,1)S(1)}, u32[]{:S(2)}, u32[]{:S(2)}) collective-permute-start(bf16[32,640]{1,0:T(8,128)(2,1)S(1)} %shard_map.73.refs_6_), channel_id=1, source_target_pairs={{0,2},{2,0},{4,6},{6,4},{8,10},{10,8},{12,14},{14,12},{1,3},{3,1},... | collective-permute-start | bytes 122888 | tf_op jit(solution)/shard_map/ppermute | solution.py:31
  10.3 4.0 %collective-permute-start.4 = (bf16[32,640]{1,0:T(8,128)(2,1)S(1)}, bf16[32,640]{1,0:T(8,128)(2,1)S(1)}, u32[]{:S(2)}, u32[]{:S(2)}) collective-permute-start(bf16[32,640]{1,0:T(8,128)(2,1)S(1)} %collective-permute-done.3.refs_4_), channel_id=1, source_target_pairs={{0,2},{2,0},{4,6},{6,4},{8,10},{10,8},{12,14},{14,12},{1,3},{3,1},... | collective-permute-start | bytes 122888 | tf_op jit(solution)/shard_map/ppermute | solution.py:31
  11.8 4.0 %collective-permute-start.2 = (bf16[32,640]{1,0:T(8,128)(2,1)S(1)}, bf16[32,640]{1,0:T(8,128)(2,1)S(1)}, u32[]{:S(2)}, u32[]{:S(2)}) collective-permute-start(bf16[32,640]{1,0:T(8,128)(2,1)S(1)} %collective-permute-done.1.refs_2_), channel_id=1, source_target_pairs={{0,2},{2,0},{4,6},{6,4},{8,10},{10,8},{12,14},{14,12},{1,3},{3,1},... | collective-permute-start | bytes 122888 | tf_op jit(solution)/shard_map/ppermute | solution.py:31
  15.8 1.7 %collective-permute-start.7 = (bf16[8,32,640]{2,1,0:T(8,128)(2,1)S(1)}, bf16[8,32,640]{2,1,0:T(8,128)(2,1)S(1)}, u32[]{:S(2)}, u32[]{:S(2)}) collective-permute-start(bf16[8,32,640]{2,1,0:T(8,128)(2,1)S(1)} %shard_map.74.refs_0_), channel_id=1, source_target_pairs={{0,1},{1,0},{2,3},{3,2},{4,5},{5,4},{6,7},{7,6},{8,9},{9,8},{10,11... | collective-permute-start | bytes 983048 | tf_op jit(solution)/shard_map/ppermute | solution.py:31
  16.8 9.7 %copy-start.3 = (f32[10,512]{1,0:T(8,128)S(1)}, f32[10,512]{1,0:T(8,128)}, u32[]{:S(2)}) copy-start(f32[10,512]{1,0:T(8,128)} %refs_6_.3) | copy-start | bytes 61444
  16.8 9.7 %copy-start.4 = (s32[10]{0:T(128)S(1)}, s32[10]{0:T(128)}, u32[]{:S(2)}) copy-start(s32[10]{0:T(128)} %refs_0_.3) | copy-start | bytes 124
  19.3 7.1 %collective-permute-start.9 = (bf16[3,32,512]{2,1,0:T(8,128)(2,1)S(1)}, bf16[3,32,512]{2,1,0:T(8,128)(2,1)S(1)}, u32[]{:S(2)}, u32[]{:S(2)}) collective-permute-start(bf16[3,32,512]{2,1,0:T(8,128)(2,1)S(1)} %get-tuple-element.23), channel_id=1, source_target_pairs={{0,16},{16,0},{1,17},{17,1},{2,18},{18,2},{3,19},{19,3},{4,20},{20... | collective-permute-start | bytes 294920 | tf_op jit(solution)/shard_map/ppermute | solution.py:31
  21.8 4.7 %collective-permute-start.10 = (bf16[2,32,512]{2,1,0:T(8,128)(2,1)S(1)}, bf16[2,32,512]{2,1,0:T(8,128)(2,1)S(1)}, u32[]{:S(2)}, u32[]{:S(2)}) collective-permute-start(bf16[2,32,512]{2,1,0:T(8,128)(2,1)S(1)} %get-tuple-element.26), channel_id=1, source_target_pairs={{0,16},{16,0},{1,17},{17,1},{2,18},{18,2},{3,19},{19,3},{4,20},{20... | collective-permute-start | bytes 196616 | tf_op jit(solution)/shard_map/ppermute | solution.py:31
  23.2 4.8 %collective-permute-start.8 = (f32[32,256]{1,0:T(8,128)S(1)}, f32[32,256]{1,0:T(8,128)S(1)}, u32[]{:S(2)}, u32[]{:S(2)}) collective-permute-start(f32[32,256]{1,0:T(8,128)S(1)} %shard_map.76.refs_0_), channel_id=1, source_target_pairs={{0,16},{16,0},{1,17},{17,1},{2,18},{18,2},{3,19},{19,3},{4,20},{20... | collective-permute-start | bytes 98312 | tf_op jit(solution)/shard_map/ppermute | solution.py:31
  28.6 14.2 %copy-start.5 = (f32[640]{0:T(1024)S(1)}, f32[640]{0:T(1024)}, u32[]{:S(2)}) copy-start(f32[640]{0:T(1024)} %param.8) | copy-start | bytes 7684
  28.6 1.6 %collective-permute-start.11 = (bf16[4,32,640]{2,1,0:T(8,128)(2,1)S(1)}, bf16[4,32,640]{2,1,0:T(8,128)(2,1)S(1)}, u32[]{:S(2)}, u32[]{:S(2)}) collective-permute-start(bf16[4,32,640]{2,1,0:T(8,128)(2,1)S(1)} %get-tuple-element.28), channel_id=1, source_target_pairs={{0,1},{1,0},{2,3},{3,2},{4,5},{5,4},{6,7},{7,6},{8,9},{9,8},{10,11... | collective-permute-start | bytes 491528 | tf_op jit(solution)/shard_map/ppermute | solution.py:31
  30.8 1.6 %collective-permute-start.15 = (bf16[4,32,640]{2,1,0:T(8,128)(2,1)S(1)}, bf16[4,32,640]{2,1,0:T(8,128)(2,1)S(1)}, u32[]{:S(2)}, u32[]{:S(2)}) collective-permute-start(bf16[4,32,640]{2,1,0:T(8,128)(2,1)S(1)} %get-tuple-element.34), channel_id=1, source_target_pairs={{0,1},{1,0},{2,3},{3,2},{4,5},{5,4},{6,7},{7,6},{8,9},{9,8},{10,11... | collective-permute-start | bytes 491528 | tf_op jit(solution)/shard_map/ppermute | solution.py:31
  31.4 4.8 %collective-permute-start.12 = (bf16[2,32,640]{2,1,0:T(8,128)(2,1)S(1)}, bf16[2,32,640]{2,1,0:T(8,128)(2,1)S(1)}, u32[]{:S(2)}, u32[]{:S(2)}) collective-permute-start(bf16[2,32,640]{2,1,0:T(8,128)(2,1)S(1)} %get-tuple-element.30), channel_id=1, source_target_pairs={{0,2},{2,0},{4,6},{6,4},{8,10},{10,8},{12,14},{14,12},{1,3},{3,1},... | collective-permute-start | bytes 245768 | tf_op jit(solution)/shard_map/ppermute | solution.py:31
  32.5 5.8 %collective-permute-start.16 = (bf16[2,32,640]{2,1,0:T(8,128)(2,1)S(1)}, bf16[2,32,640]{2,1,0:T(8,128)(2,1)S(1)}, u32[]{:S(2)}, u32[]{:S(2)}) collective-permute-start(bf16[2,32,640]{2,1,0:T(8,128)(2,1)S(1)} %get-tuple-element.36), channel_id=1, source_target_pairs={{0,2},{2,0},{4,6},{6,4},{8,10},{10,8},{12,14},{14,12},{1,3},{3,1},... | collective-permute-start | bytes 245768 | tf_op jit(solution)/shard_map/ppermute | solution.py:31
  36.2 5.0 %collective-permute-start.13 = (bf16[32,640]{1,0:T(8,128)(2,1)S(1)}, bf16[32,640]{1,0:T(8,128)(2,1)S(1)}, u32[]{:S(2)}, u32[]{:S(2)}) collective-permute-start(bf16[32,640]{1,0:T(8,128)(2,1)S(1)} %get-tuple-element.31), channel_id=1, source_target_pairs={{0,8},{2,10},{4,12},{6,14},{8,0},{10,2},{12,4},{14,6},{1,9},{3,11}... | collective-permute-start | bytes 122888 | tf_op jit(solution)/shard_map/ppermute | solution.py:31
  36.9 5.9 %collective-permute-start.14 = (bf16[32,640]{1,0:T(8,128)(2,1)S(1)}, bf16[32,640]{1,0:T(8,128)(2,1)S(1)}, u32[]{:S(2)}, u32[]{:S(2)}) collective-permute-start(bf16[32,640]{1,0:T(8,128)(2,1)S(1)} %get-tuple-element.32), channel_id=1, source_target_pairs={{0,12},{2,14},{4,8},{6,10},{8,4},{10,6},{12,0},{14,2},{1,13},{3,15... | collective-permute-start | bytes 122888 | tf_op jit(solution)/shard_map/ppermute | solution.py:31
  38.3 4.5 %collective-permute-start.17 = (bf16[32,640]{1,0:T(8,128)(2,1)S(1)}, bf16[32,640]{1,0:T(8,128)(2,1)S(1)}, u32[]{:S(2)}, u32[]{:S(2)}) collective-permute-start(bf16[32,640]{1,0:T(8,128)(2,1)S(1)} %get-tuple-element.38), channel_id=1, source_target_pairs={{0,4},{2,6},{4,0},{6,2},{8,12},{10,14},{12,8},{14,10},{1,5},{3,7},... | collective-permute-start | bytes 122888 | tf_op jit(solution)/shard_map/ppermute | solution.py:31
